TPU v7x, 32 devices: a whole 2x2x4 slice. The times are simulated.
32 devices in a mesh: height: 8 (over y, x, core), dp: 4 (over z).
Axes of the slice: x: 2, y: 2, z: 4, core: 2. Of those that a mesh axis runs over, the one named last changes fastest.
Arguments:
- x_next: bfloat16 [4, 16, 320, 128], P('dp', 'height'), may hold values from -12 to 12
- x_cur: bfloat16 [4, 16, 320, 128], P('dp', 'height'), may hold values from -12 to 12
- grad_out: bfloat16 [4, 16, 320, 128], P('dp', 'height'), may hold values from -6 to 6
- kernel: bfloat16 [3, 3, 320, 320], replicated, may hold values from -0.109375 to 0.109375
- gamma: float32 [320], replicated, may hold values from 0.25 to 1.75
- beta: float32 [320], replicated, may hold values from -2.5 to 2.5
Outputs:
- y_next: bfloat16 [4, 16, 320, 128], P('dp', 'height')
- grad_x: bfloat16 [4, 16, 320, 128], P('dp', 'height')
- grad_kernel: float32 [921600], P(('height', 'dp'))
All inputs are finite; a program needn't handle non-finite values.
Results may differ from a plain program's by a relative error of at most 0.0049.
Values may be sent and summed in bfloat16 or wider, within the bound.
No kernel may reach another device: no remote copies, remote signals or barrier semaphores. Data moves between devices by JAX's collectives and lax.ppermute only.
A program may use at most 64 MiB of HBM per device.

v0:
```python
import functools
import math

import jax
import jax.numpy as jnp
from jax import lax
from jax.experimental import pallas as pl
from jax.experimental.pallas import tpu as pltpu
from jax.sharding import PartitionSpec as P

GROUPS = 32

eps = 1e-05


LANES = 128
F32 = jnp.float32
BF16 = jnp.bfloat16


def extended(cells, sides, width):
    for axis, dim in sides:
        count = lax.axis_size(axis)
        ends = count - 1
        head = lax.slice_in_dim(cells, 0, width, axis=dim)
        tail = lax.slice_in_dim(cells, cells.shape[dim] - width, cells.shape[dim], axis=dim)
        cells = jnp.concatenate(
            [
                lax.ppermute(tail, axis, [(i, (i + 1) % count) for i in range(ends)]),
                cells,
                lax.ppermute(head, axis, [((i + 1) % count, i) for i in range(ends)]),
            ],
            axis=dim,
        )
    return cells


def conv_rows(padded, kernel, count):
    width = padded.shape[-1]
    wide = jnp.pad(padded, ((0, 0), (0, 0), (0, 0), (1, 1)))
    total = None
    for tap_row in range(3):
        for tap_col in range(3):
            window = wide[:, tap_row : tap_row + count, :, tap_col : tap_col + width]
            term = jnp.einsum(
                "oc,bhcw->bhow",
                kernel[tap_row, tap_col],
                window,
                preferred_element_type=jnp.float32,
            )
            total = term if total is None else total + term
    return total


def group_sum(value):
    batch, rows, chans, width = value.shape
    return jnp.sum(value.reshape(batch, rows, GROUPS, chans // GROUPS, width), axis=(1, 3, 4))


def row_sharded(x_next, x_cur, grad_out, kernel, gamma, beta):
    _, rows, chans, width = x_next.shape
    height_count = lax.axis_size("height")
    count = height_count * rows * (chans // GROUPS) * width
    gain = gamma[None, None, :, None]
    shift_b = beta[None, None, :, None]

    def expand(stat):
        return jnp.repeat(stat, chans // GROUPS, axis=1)[:, None, :, None]

    stacked = jnp.stack((x_next, x_cur))
    padded = extended(stacked, (("height", 2),), 1)
    xp_next = padded[0]
    xp_cur = padded[1]
    z_next = conv_rows(xp_next, kernel, rows)
    z_cur = conv_rows(xp_cur, kernel, rows)
    sum_next, sum_cur, sq_next, sq_cur = lax.psum(
        (group_sum(z_next), group_sum(z_cur), group_sum(z_next * z_next), group_sum(z_cur * z_cur)),
        "height",
    )
    mean_next = sum_next / count
    mean_cur = sum_cur / count
    var_next = sq_next / count - mean_next * mean_next
    var_cur = sq_cur / count - mean_cur * mean_cur
    rstd_next = lax.rsqrt(var_next + eps)
    rstd_cur = lax.rsqrt(var_cur + eps)
    affine_next = (z_next - expand(mean_next)) * expand(rstd_next) * gain + shift_b
    y_next = (affine_next * jax.nn.sigmoid(affine_next)).astype(jnp.bfloat16)
    normed = (z_cur - expand(mean_cur)) * expand(rstd_cur)
    affine = normed * gain + shift_b
    sig = jax.nn.sigmoid(affine)
    grad_n = grad_out.astype(jnp.float32) * (sig * (1.0 + affine * (1.0 - sig))) * gain
    first_sum, second_sum = lax.psum((group_sum(grad_n), group_sum(grad_n * normed)), "height")
    grad_z = (
        expand(rstd_cur)
        * (grad_n - expand(first_sum / count) - normed * expand(second_sum / count))
    ).astype(jnp.bfloat16)
    grad_pad = extended(grad_z, (("height", 1),), 1)
    grad_own = grad_pad[:, 1:-1]
    grad_wide = jnp.pad(grad_pad, ((0, 0), (0, 0), (0, 0), (1, 1)))
    x_wide = jnp.pad(xp_cur, ((0, 0), (0, 0), (0, 0), (1, 1)))
    grad_input = None
    taps = []
    for tap_row in range(3):
        tap_list = []
        for tap_col in range(3):
            window = grad_wide[
                :, 2 - tap_row : 2 - tap_row + rows, :, 2 - tap_col : 2 - tap_col + width
            ]
            term = jnp.einsum(
                "oc,bhow->bhcw",
                kernel[tap_row, tap_col],
                window,
                preferred_element_type=jnp.float32,
            )
            grad_input = term if grad_input is None else grad_input + term
            source = x_wide[:, tap_row : tap_row + rows, :, tap_col : tap_col + width]
            tap_list.append(
                jnp.einsum("bhow,bhcw->oc", grad_own, source, preferred_element_type=jnp.float32)
            )
        taps.append(jnp.stack(tap_list))
    grad_local = jnp.stack(taps)
    grad_x = grad_input.astype(jnp.bfloat16)
    group_count = lax.axis_size("dp")
    piece = grad_local.size // (height_count * group_count)
    blocks = grad_local.reshape(height_count, group_count, piece)
    shares = lax.psum_scatter(blocks, "dp", scatter_dimension=1, tiled=True)
    grad_kernel = lax.psum_scatter(shares, "height", scatter_dimension=0, tiled=True).reshape(piece)
    return (y_next, grad_x, grad_kernel)


def params(limit=None):
    return pltpu.CompilerParams(vmem_limit_bytes=limit or 40 * 1024 * 1024)


def moved(value, by):
    width = value.shape[-1]
    lane = lax.broadcasted_iota(jnp.int32, value.shape, value.ndim - 1)
    rolled = pltpu.roll(value, by % width, value.ndim - 1)
    keep = lane >= by if by > 0 else lane < width + by
    return jnp.where(keep, rolled, jnp.zeros_like(rolled))


def moved_bf16(value, by):
    return moved(value.astype(F32), by).astype(BF16)


def same_group(rows, chans):
    size = chans // GROUPS
    row = lax.broadcasted_iota(jnp.int32, (rows, rows), 0).astype(F32)
    col = lax.broadcasted_iota(jnp.int32, (rows, rows), 1).astype(F32)
    left = jnp.floor((row + 0.5) * (1.0 / size))
    right = jnp.floor((col + 0.5) * (1.0 / size))
    return jnp.where(left == right, 1.0, 0.0).astype(BF16)


def split3(value):
    high = value.astype(BF16)
    rest = value - high.astype(F32)
    mid = rest.astype(BF16)
    low = (rest - mid.astype(F32)).astype(BF16)
    return high, mid, low


def dot(left, right, dims=((1,), (0,))):
    return lax.dot_general(left, right, (dims, ((), ())), preferred_element_type=F32)


def group_total(same, value):
    column = jnp.sum(value, axis=1, keepdims=True)
    wide = jnp.broadcast_to(column, value.shape)
    high, mid, low = split3(wide)
    return dot(same, high) + (dot(same, mid) + dot(same, low))


def lane_tiles(size):
    return [(at, min(LANES, size - at)) for at in range(0, size, LANES)]


def sigmoid(value):
    return 1.0 / (1.0 + jnp.exp(-value))


def weights_kernel(w_ref, flat_ref):
    chans = flat_ref.shape[1]
    for a in range(3):
        for b in range(3):
            flat_ref[a, :, b * chans : (b + 1) * chans] = w_ref[a, b]


def halves_kernel(g_ref, own_ref, other_ref):
    half = own_ref.shape[1]
    core = lax.axis_index("height") & 1
    for r in range(own_ref.shape[0]):
        own_ref[r] = g_ref[r, pl.ds(pl.multiple_of(core * half, 16), half)]
        other_ref[r] = g_ref[r, pl.ds(pl.multiple_of((1 - core) * half, 16), half)]


def next_conv_kernel(top_ref, x_ref, bottom_ref, w_ref, z_ref, stat_ref, *, rows):
    cells = [top_ref[...]] + [x_ref[r] for r in range(rows)] + [bottom_ref[...]]
    chans, width = cells[0].shape
    sides = [[moved_bf16(cell, 1) for cell in cells], cells, [moved_bf16(cell, -1) for cell in cells]]
    stacks = [jnp.concatenate([side[r] for side in sides], axis=0) for r in range(rows + 2)]
    total = None
    for a in range(3):
        term = dot(w_ref[a], jnp.concatenate(stacks[a : a + rows], axis=1))
        total = term if total is None else total + term
    parts = [total[:, r * width : (r + 1) * width] for r in range(rows)]
    for r in range(rows):
        z_ref[r] = parts[r]
    line = functools.reduce(jnp.add, parts)
    mean = jnp.sum(line, axis=1, keepdims=True) * (1.0 / (rows * width))
    off = functools.reduce(jnp.add, [(part - mean) * (part - mean) for part in parts])
    ones = jnp.ones((8, width), BF16)
    row = lax.broadcasted_iota(jnp.int32, stat_ref.shape, 0)
    packed = jnp.zeros(stat_ref.shape, F32)
    at = 0
    for value in (line, off):
        lane_sum = sum(dot(ones, part, ((1,), (1,))) for part in split3(value))
        for start, size in lane_tiles(chans):
            piece = lane_sum[:1, start : start + size]
            if size < LANES:
                piece = jnp.concatenate([piece, jnp.zeros((1, LANES - size), F32)], axis=1)
            packed = jnp.where(row == at, jnp.broadcast_to(piece, packed.shape), packed)
            at += 1
    stat_ref[...] = packed


def next_out_kernel(*refs, rows, count):
    stat_refs = refs[:-4]
    z_ref, gain_ref, shift_ref, y_ref = refs[-4:]
    chans, width = gain_ref.shape
    same = same_group(chans, chans)
    tiles = lane_tiles(chans)

    def line(value):
        at = value * len(tiles)
        cells = [
            jnp.concatenate([ref[j, at + i : at + i + 1, :size] for i, (_, size) in enumerate(tiles)], axis=1)
            for ref in stat_refs
            for j in range(ref.shape[0])
        ]
        return jnp.concatenate(cells, axis=0)

    sums = line(0)
    offs = line(1)
    each = rows * width
    total = jnp.broadcast_to(jnp.sum(sums, axis=0, keepdims=True), (width, chans))
    mean_line = sum(dot(part, same) for part in split3(total[:8])) * (1.0 / count)
    apart = sums * (1.0 / each) - mean_line[:1]
    spread = jnp.sum(offs + apart * apart * float(each), axis=0, keepdims=True)
    spread = jnp.broadcast_to(spread, (width, chans))
    mean = sum(dot(same, part, ((1,), (1,))) for part in split3(total)) * (1.0 / count)
    var = sum(dot(same, part, ((1,), (1,))) for part in split3(spread)) * (1.0 / count)
    rstd = lax.rsqrt(var + eps)
    for r in range(rows):
        affine = (z_ref[r] - mean) * rstd * gain_ref[...] + shift_ref[...]
        y_ref[r] = (affine * sigmoid(affine)).astype(BF16)


def conv_kernel(*refs, blocks, rows, count, wide):
    x_refs = refs[:blocks]
    w_ref, xs, z, norm, total_ref = refs[blocks:]
    image, half, width = z.shape
    chans = x_refs[0].shape[1]
    home = lax.axis_index("height")
    mine = pl.ds(pl.multiple_of((home & 1) * half, 16), half)
    step = 16

    edge = jnp.zeros((3 * chans, width), BF16)
    xs[0] = edge
    xs[image + 1] = edge
    for k in range(blocks):
        base = (home ^ k) * rows + 1
        for r in range(rows):
            cell = x_refs[k][r]
            xs[base + r, chans : 2 * chans] = cell
            xs[base + r, :chans] = moved_bf16(cell, 1)
            xs[base + r, 2 * chans :] = moved_bf16(cell, -1)

    def conv(p, carry):
        row = p * wide
        total = None
        for a in range(3):
            right = jnp.concatenate([xs[row + a + i] for i in range(wide)], axis=1)
            term = dot(w_ref[a, mine], right)
            total = term if total is None else total + term
        parts = [total[:, i * width : (i + 1) * width] for i in range(wide)]
        for i in range(wide):
            z[row + i] = parts[i]
        return carry

    lax.fori_loop(0, image // wide, conv, 0)
    same = same_group(half, chans)

    def summed(i, carry):
        at = pl.ds(pl.multiple_of(i * step, step), step)
        total_ref[at] = functools.reduce(jnp.add, [z[r, at] for r in range(image)])
        return carry

    lax.fori_loop(0, half // step, summed, 0)
    norm[0] = group_total(same, total_ref[...]) * (1.0 / count)

    def squared(i, carry):
        at = pl.ds(pl.multiple_of(i * step, step), step)
        mean = norm[0, at]
        total = None
        for r in range(image):
            off = z[r, at] - mean
            total = off * off if total is None else total + off * off
        total_ref[at] = total
        return carry

    lax.fori_loop(0, half // step, squared, 0)
    norm[1] = lax.rsqrt(group_total(same, total_ref[...]) * (1.0 / count) + eps)


def pull_kernel(*refs, blocks, rows, count):
    g_refs = refs[: blocks // 2]
    z, norm, gain_ref, shift_ref, gz_ref, gn, ns, coef = refs[blocks // 2 :]
    image, half, _ = z.shape
    chans = gain_ref.shape[0]
    home = lax.axis_index("height")
    core = home & 1
    step = 16

    def pulled(i, carry):
        start = pl.multiple_of(i * step, step)
        at = pl.ds(start, step)
        all_at = pl.ds(pl.multiple_of(core * half + start, step), step)
        mean = norm[0, at]
        rstd = norm[1, at]
        gain = gain_ref[all_at]
        shift = shift_ref[all_at]
        first = None
        second = None
        for k in range(blocks):
            base = (home ^ k) * rows
            for r in range(rows):
                n = (z[base + r, at] - mean) * rstd
                affine = n * gain + shift
                sig = sigmoid(affine)
                slope = sig * (1.0 + affine * (1.0 - sig))
                value = g_refs[k // 2][k % 2, r, at].astype(F32) * slope * gain
                gn[base + r, at] = value
                ns[base + r, at] = n
                first = value if first is None else first + value
                second = value * n if second is None else second + value * n
        coef[0, at] = first
        coef[1, at] = second
        return carry

    lax.fori_loop(0, half // step, pulled, 0)
    same = same_group(half, chans)
    coef[0] = group_total(same, coef[0]) * (1.0 / count)
    coef[1] = group_total(same, coef[1]) * (1.0 / count)

    def rounded(i, carry):
        at = pl.ds(pl.multiple_of(i * step, step), step)
        mean1 = coef[0, at]
        mean2 = coef[1, at]
        rstd = norm[1, at]
        for r in range(image):
            gz_ref[r, at] = (rstd * (gn[r, at] - mean1 - ns[r, at] * mean2)).astype(BF16)
        return carry

    lax.fori_loop(0, half // step, rounded, 0)


def filter_kernel(own_ref, other_ref, xs, *refs, blocks, rows, groups_dp, span):
    outs = refs[:groups_dp]
    gz_out, gz, taps, flat = refs[groups_dp:]
    image, half, width = own_ref.shape
    chans = 2 * half
    home = lax.axis_index("height")
    part = lax.axis_index("dp")
    core = home & 1
    step = 16

    edge = jnp.zeros((chans, width), BF16)
    gz[0] = edge
    gz[image + 1] = edge
    for r in range(image):
        gz[r + 1, pl.ds(pl.multiple_of(core * half, step), half)] = own_ref[r]
        gz[r + 1, pl.ds(pl.multiple_of((1 - core) * half, step), half)] = other_ref[r]
    for r in range(rows + 2):
        gz_out[r] = gz[home * rows + r]

    block = 9 * chans // blocks
    tap0 = (home * block) // chans
    left = jnp.concatenate([gz[r + 1] for r in range(image)], axis=1)
    for j in range(span):
        tap = jnp.minimum(tap0 + j, 8)
        a = tap // 3
        side = pl.ds(pl.multiple_of((tap - a * 3) * chans, step), chans)
        right = jnp.concatenate([xs[r + a, side] for r in range(image)], axis=1)
        rows_of = dot(left, right, ((1,), (1,)))
        for i, (start, size) in enumerate(lane_tiles(chans)):
            taps[i, j * chans : (j + 1) * chans, :size] = rows_of[:, start : start + size]

    off = pl.multiple_of(home * block - tap0 * chans, 8)
    shared = math.gcd(chans, LANES)
    few, many = LANES // shared, chans // shared
    for i in range(taps.shape[0]):
        taps[i, :block] = taps[i, pl.ds(off, block)]
    lines = jnp.concatenate(
        [
            taps[i, pl.ds(line, block // few, stride=few)][:, :size]
            for line in range(few)
            for i, (_, size) in enumerate(lane_tiles(chans))
        ],
        axis=1,
    )
    for i in range(many):
        flat[pl.ds(i, block // few, stride=many)] = lines[:, i * LANES : (i + 1) * LANES]
    piece = flat.shape[0] // groups_dp
    for s in range(groups_dp):
        dest = part ^ s
        value = flat[pl.ds(dest * piece, piece)]
        outs[s][...] = value.astype(outs[s].dtype)


def grad_x_kernel(gz_ref, w_ref, out_ref, *, rows):
    chans, width = gz_ref.shape[1:]
    total = None
    for a in range(3):
        right = jnp.concatenate([gz_ref[2 - a + r] for r in range(rows)], axis=1)
        term = dot(w_ref[a], right, ((0,), (0,)))
        total = term if total is None else total + term
    for r in range(rows):
        part = total[:, r * width : (r + 1) * width]
        value = part[chans : 2 * chans]
        value = value + moved(part[:chans], -1) + moved(part[2 * chans :], 1)
        out_ref[r] = value.astype(BF16)


def vmem(count):
    return [pl.BlockSpec(memory_space=pltpu.VMEM)] * count


def pairs(size, offset):
    return [(i, i ^ offset) for i in range(size)]


def call(kernel, out_shape, args, scratch=(), flops=0, **static):
    single = not isinstance(out_shape, tuple)
    return pl.pallas_call(
        functools.partial(kernel, **static),
        out_shape=out_shape,
        in_specs=vmem(len(args)),
        out_specs=vmem(1)[0] if single else tuple(vmem(len(out_shape))),
        scratch_shapes=list(scratch),
        compiler_params=params(),
        cost_estimate=pl.CostEstimate(flops=flops, bytes_accessed=0, transcendentals=0),
    )(*args)


def gathered(x_next, x_cur, grad_out, kernel, gamma, beta):
    rows, chans, width = x_next.shape[1:]
    blocks = lax.axis_size("height")
    groups_dp = lax.axis_size("dp")
    image = blocks * rows
    half = chans // 2
    count = image * (chans // GROUPS) * width
    block = 9 * chans // blocks
    span = max((h * block % chans + block - 1) // chans + 1 for h in range(blocks))
    piece = block * chans // (groups_dp * LANES)
    flops = 18 * chans * chans * width
    x_next, grad_out = x_next[0], grad_out[0]
    shape = jax.ShapeDtypeStruct

    def far(own):
        held = {0: own}
        for k in sorted(range(2, blocks, 2), key=lambda k: -bin(k).count("1")):
            held[k] = lax.ppermute(own, "height", pairs(blocks, k))
        return held

    def near(own):
        return lax.ppermute(own, "height", pairs(blocks, 1))

    x_far = far(x_cur[0])
    ends = blocks - 1
    top = lax.ppermute(x_next[rows - 1], "height", [(i, i + 1) for i in range(ends)])
    bottom = lax.ppermute(x_next[0], "height", [(i + 1, i) for i in range(ends)])
    own_half, other_half = call(halves_kernel, (shape((rows, half, width), BF16),) * 2, (grad_out,))
    g_pair = jnp.stack((own_half, near(other_half)))
    g_far = far(g_pair)
    gain = jnp.broadcast_to(gamma[:, None], (chans, width))
    shift = jnp.broadcast_to(beta[:, None], (chans, width))
    w_flat = call(weights_kernel, shape((3, chans, 3 * chans), BF16), (kernel,))

    x_far, top, w_flat, _ = lax.optimization_barrier((x_far, top, w_flat, g_pair))
    x_all = []
    for k in range(0, blocks, 2):
        x_all += [x_far[k], near(x_far[k])]
    z_next, stat = call(
        next_conv_kernel,
        (shape((rows, chans, width), F32), shape((8 * -(-2 * len(lane_tiles(chans)) // 8), LANES), F32)),
        (top, x_next, bottom, w_flat),
        flops=rows * flops,
        rows=rows,
    )
    xs, z_cur, norm = call(
        conv_kernel,
        (
            shape((image + 2, 3 * chans, width), BF16),
            shape((image, half, width), F32),
            shape((2, half, width), F32),
        ),
        (*x_all, w_flat),
        scratch=(pltpu.VMEM((half, width), F32),),
        flops=image * flops // 2,
        blocks=blocks,
        rows=rows,
        count=count,
        wide=4 if image % 4 == 0 else 2,
    )
    stat, norm = lax.optimization_barrier((stat, norm))
    stat_pair = jnp.stack((stat, near(stat)))
    gz_own = call(
        pull_kernel,
        shape((image, half, width), BF16),
        (*[g_far[k] for k in range(0, blocks, 2)], z_cur, norm, gain, shift),
        scratch=(
            pltpu.VMEM((image, half, width), F32),
            pltpu.VMEM((image, half, width), F32),
            pltpu.VMEM((2, half, width), F32),
        ),
        flops=image * flops // 8,
        blocks=blocks,
        rows=rows,
        count=count,
    )
    gz_other = near(gz_own)
    stat_pair, gz_own = lax.optimization_barrier((stat_pair, gz_own))
    stat_far = far(stat_pair)
    results = call(
        filter_kernel,
        (shape((piece, LANES), F32),)
        + (shape((piece, LANES), BF16),) * (groups_dp - 1)
        + (shape((rows + 2, chans, width), BF16),),
        (gz_own, gz_other, xs),
        scratch=(
            pltpu.VMEM((image + 2, chans, width), BF16),
            pltpu.VMEM((len(lane_tiles(chans)), span * chans, LANES), F32),
            pltpu.VMEM((groups_dp * piece, LANES), F32),
        ),
        flops=image * flops // 4,
        blocks=blocks,
        rows=rows,
        groups_dp=groups_dp,
        span=span,
    )
    total = results[0]
    for s in range(groups_dp - 1, 0, -1):
        total = total + lax.ppermute(results[s], "dp", pairs(groups_dp, s)).astype(F32)
    grad_x = call(
        grad_x_kernel,
        shape((rows, chans, width), BF16),
        (results[groups_dp], w_flat),
        flops=rows * flops,
        rows=rows,
    )
    y_next = call(
        next_out_kernel,
        shape((rows, chans, width), BF16),
        (*stat_far.values(), z_next, gain, shift),
        flops=rows * flops // 4,
        rows=rows,
        count=count,
    )
    return (y_next[None], grad_x[None], total.reshape(piece * LANES))


def fits(shape, blocks, groups_dp):
    batch, rows, chans, width = shape
    image = blocks * rows
    scratch = image * chans * width * 20 + 9 * chans * chans * 4
    few = LANES // math.gcd(chans, LANES)
    return (
        batch == 1
        and width == LANES
        and chans % 32 == 0
        and chans % GROUPS == 0
        and GROUPS % 2 == 0
        and blocks > 1
        and image % 2 == 0
        and blocks & (blocks - 1) == 0
        and groups_dp & (groups_dp - 1) == 0
        and (9 * chans) % (8 * blocks) == 0
        and (9 * chans // blocks) % few == 0
        and (9 * chans // blocks) * chans % (groups_dp * LANES) == 0
        and scratch < 32 * 1024 * 1024
    )


def solution(mesh):
    blocks, groups_dp = mesh.shape["height"], mesh.shape["dp"]

    def local(x_next, x_cur, grad_out, kernel, gamma, beta):
        if not fits(x_next.shape, blocks, groups_dp):
            return row_sharded(x_next, x_cur, grad_out, kernel, gamma, beta)
        return gathered(x_next, x_cur, grad_out, kernel, gamma, beta)

    placed = (
        P("dp", "height", None, None),
        P("dp", "height", None, None),
        P("dp", "height", None, None),
        P(),
        P(),
        P(),
    )
    return jax.shard_map(
        local,
        mesh=mesh,
        in_specs=placed,
        out_specs=(
            P("dp", "height", None, None),
            P("dp", "height", None, None),
            P(("height", "dp")),
        ),
        check_vma=False,
    )
```

profile of v0, /device:TPU:0, one launch (start us, length us, event | category | flops | bytes accessed | tf_op | source)
XLA Modules:
  0.0 50.6 jit_solution(13361006858962839301)
XLA Ops:
  0.6 3.0 %collective-permute-start = (bf16[2,320,128]{2,1,0:T(8,128)(2,1)}, bf16[2,320,128]{2,1,0:T(8,128)(2,1)S(1)}, u32[]{:S(2)}, u32[]{:S(2)}) collective-permute-start(bf16[2,320,128]{2,1,0:T(8,128)(2,1)} %bitcast.19), channel_id=1, source_target_pairs={{0,8},{4,12},{8,0},{12,4},{16,24},{20,28},{24,16},{28,20},{1,9},{5... | collective-permute-start | bytes 491528 | tf_op jit(solution)/shard_map/ppermute | solution.py:474
  3.7 1.5 %collective-permute-start.1 = (bf16[2,320,128]{2,1,0:T(8,128)(2,1)}, bf16[2,320,128]{2,1,0:T(8,128)(2,1)S(1)}, u32[]{:S(2)}, u32[]{:S(2)}) collective-permute-start(bf16[2,320,128]{2,1,0:T(8,128)(2,1)} %bitcast.20), channel_id=1, source_target_pairs={{0,16},{4,20},{8,24},{12,28},{16,0},{20,4},{24,8},{28,12},{1,17},{... | collective-permute-start | bytes 491528 | tf_op jit(solution)/shard_map/ppermute | solution.py:474
  5.2 0.0 collective-permute-start.2
  5.2 0.0 copy-start.2
  5.2 0.9 %copy-done.2 = bf16[1,2,320,128]{3,2,1,0:T(8,128)(2,1)S(1)} copy-done((bf16[1,2,320,128]{3,2,1,0:T(8,128)(2,1)S(1)}, bf16[1,2,320,128]{3,2,1,0:T(8,128)(2,1)}, u32[]{:S(2)}) %copy-start.2) | copy-done | bytes 163864
  6.1 0.1 collective-permute-start.4
  6.2 0.9 %slice_bitcast_fusion = (bf16[320,128]{1,0:T(8,128)(2,1)S(1)}, bf16[320,128]{1,0:T(8,128)(2,1)S(1)}) fusion(bf16[1,2,320,128]{3,2,1,0:T(8,128)(2,1)} %param.6), kind=kLoop, calls=%fused_computation.2 | loop fusion | bytes 327680 | tf_op jit(solution)/shard_map/squeeze | solution.py:483
  7.2 2.4 %collective-permute-start.3 = (bf16[320,128]{1,0:T(8,128)(2,1)S(1)}, bf16[320,128]{1,0:T(8,128)(2,1)S(1)}, u32[]{:S(2)}, u32[]{:S(2)}) collective-permute-start(bf16[320,128]{1,0:T(8,128)(2,1)S(1)} %get-tuple-element.48), channel_id=1, source_target_pairs={{0,4},{4,8},{8,12},{12,16},{16,20},{20,24},{24,28},{1,5},{5,9},{9,... | collective-permute-start | bytes 245768 | tf_op jit(solution)/shard_map/ppermute | solution.py:482
  9.6 0.0 copy-start
  9.6 1.6 %copy-done = bf16[3,3,320,320]{3,2,1,0:T(8,128)(2,1)S(1)} copy-done((bf16[3,3,320,320]{3,2,1,0:T(8,128)(2,1)S(1)}, bf16[3,3,320,320]{3,2,1,0:T(8,128)(2,1)}, u32[]{:S(2)}) %copy-start) | copy-done | bytes 1843224
  11.2 0.0 copy-start.3
  11.2 0.0 copy-start.1
  11.2 0.4 shard_map.85.w_ref.refs_8_
  11.6 0.0 collective-permute-done.4
  11.6 0.0 collective-permute-done.3.top_ref
  11.6 0.0 collective-permute-done.refs_2_
  11.6 1.4 %collective-permute-done.1.refs_4_ = bf16[2,320,128]{2,1,0:T(8,128)(2,1)S(1)} collective-permute-done((bf16[2,320,128]{2,1,0:T(8,128)(2,1)}, bf16[2,320,128]{2,1,0:T(8,128)(2,1)S(1)}, u32[]{:S(2)}, u32[]{:S(2)}) %collective-permute-start.1) | collective-permute-done | bytes 163872 | tf_op jit(solution)/shard_map/ppermute | solution.py:474
  13.0 0.0 collective-permute-done.2.refs_6_
  13.0 0.0 copy-done.3
  13.0 0.6 %collective-permute-start.6 = (bf16[2,320,128]{2,1,0:T(8,128)(2,1)S(1)}, bf16[2,320,128]{2,1,0:T(8,128)(2,1)S(1)}, u32[]{:S(2)}, u32[]{:S(2)}) collective-permute-start(bf16[2,320,128]{2,1,0:T(8,128)(2,1)S(1)} %bitcast.22), channel_id=1, source_target_pairs={{0,4},{4,0},{8,12},{12,8},{16,20},{20,16},{24,28},{28,24},{1,5},{5... | collective-permute-start | bytes 491528 | tf_op jit(solution)/shard_map/ppermute | solution.py:478
  13.7 0.0 collective-permute-start.7
  13.7 0.5 %collective-permute-start.8 = (bf16[2,320,128]{2,1,0:T(8,128)(2,1)S(1)}, bf16[2,320,128]{2,1,0:T(8,128)(2,1)S(1)}, u32[]{:S(2)}, u32[]{:S(2)}) collective-permute-start(bf16[2,320,128]{2,1,0:T(8,128)(2,1)S(1)} %collective-permute-done.1.refs_4_), channel_id=1, source_target_pairs={{0,4},{4,0},{8,12},{12,8},{16,20},{20,16},{24,28},{28,24},{1,5},{5... | collective-permute-start | bytes 491528 | tf_op jit(solution)/shard_map/ppermute | solution.py:478
  14.2 0.0 collective-permute-start.9
  14.2 1.3 %collective-permute-start.5 = (bf16[320,128]{1,0:T(8,128)(2,1)S(1)}, bf16[320,128]{1,0:T(8,128)(2,1)S(1)}, u32[]{:S(2)}, u32[]{:S(2)}) collective-permute-start(bf16[320,128]{1,0:T(8,128)(2,1)S(1)} %get-tuple-element.47), channel_id=1, source_target_pairs={{4,0},{8,4},{12,8},{16,12},{20,16},{24,20},{28,24},{5,1},{9,5},{13... | collective-permute-start | bytes 245768 | tf_op jit(solution)/shard_map/ppermute | solution.py:483
  15.5 1.9 %collective-permute-done.5.bottom_ref = bf16[320,128]{1,0:T(8,128)(2,1)S(1)} collective-permute-done((bf16[320,128]{1,0:T(8,128)(2,1)S(1)}, bf16[320,128]{1,0:T(8,128)(2,1)S(1)}, u32[]{:S(2)}, u32[]{:S(2)}) %collective-permute-start.5) | collective-permute-done | bytes 81952 | tf_op jit(solution)/shard_map/ppermute | solution.py:483
  17.4 2.9 %collective-permute-start.11 = (bf16[2,2,160,128]{3,2,1,0:T(8,128)(2,1)S(1)}, bf16[2,2,160,128]{3,2,1,0:T(8,128)(2,1)S(1)}, u32[]{:S(2)}, u32[]{:S(2)}) collective-permute-start(bf16[2,2,160,128]{3,2,1,0:T(8,128)(2,1)S(1)} %pad_maximum_fusion.refs_0_), channel_id=1, source_target_pairs={{0,8},{4,12},{8,0},{12,4},{16,24},{20,28},{24,16},{28,20},{1,9},{5... | collective-permute-start | bytes 491528 | tf_op jit(solution)/shard_map/ppermute | solution.py:474
  20.3 0.0 copy-done.1
  20.3 1.2 %shard_map.87 = (f32[2,320,128]{2,1,0:T(8,128)S(1)}, f32[8,128]{1,0:T(8,128)S(1)}) custom-call(bf16[320,128]{1,0:T(8,128)(2,1)S(1)} %collective-permute-done.3.top_ref, bf16[2,320,128]{2,1,0:T(8,128)(2,1)S(1)} %bitcast.15, bf16[320,128]{1,0:T(8,128)(2,1)S(1)} %collective-permute-done.5.bottom_ref, bf16[3,320,960]{2,1,0:T(8,128)(2,1)S(1)} %shard_map.85.w_ref.refs_8_), custom_call_target="tpu_custom_call" | custom-call | flops 471859200 | tf_op jit(solution)/shard_map/pallas_call | solution.py:446
  21.4 0.0 copy-start.5
  21.5 0.0 collective-permute-done.6.refs_1_
  21.5 2.3 %collective-permute-start.12 = (bf16[2,2,160,128]{3,2,1,0:T(8,128)(2,1)S(1)}, bf16[2,2,160,128]{3,2,1,0:T(8,128)(2,1)S(1)}, u32[]{:S(2)}, u32[]{:S(2)}) collective-permute-start(bf16[2,2,160,128]{3,2,1,0:T(8,128)(2,1)S(1)} %pad_maximum_fusion.refs_0_), channel_id=1, source_target_pairs={{0,16},{4,20},{8,24},{12,28},{16,0},{20,4},{24,8},{28,12},{1,17},{... | collective-permute-start | bytes 491528 | tf_op jit(solution)/shard_map/ppermute | solution.py:474
  23.8 0.0 collective-permute-done.7.refs_3_
  23.8 0.2 collective-permute-start.13
  24.0 0.0 collective-permute-done.8.refs_5_
  24.0 0.0 collective-permute-done.9.refs_7_
  24.0 4.8 %shard_map.88 = (bf16[18,960,128]{2,1,0:T(8,128)(2,1)S(1)}, f32[16,160,128]{2,1,0:T(8,128)S(1)}, f32[2,160,128]{2,1,0:T(8,128)S(1)}) custom-call(bf16[2,320,128]{2,1,0:T(8,128)(2,1)S(1)} %bitcast.23, bf16[2,320,128]{2,1,0:T(8,128)(2,1)S(1)} %collective-permute-done.6.refs_1_, bf16[2,320,128]{2,1,0:T(8,128)(2,1)S(1)} %collective-permute-done.refs_2_, ...), custom_call_target="tpu_custom_call" | custom-call | flops 1887436800 | tf_op jit(solution)/shard_map/pallas_call | solution.py:446
  28.8 0.0 collective-permute-done.11.refs_1_
  28.9 2.5 %collective-permute-done.12.refs_2_ = bf16[2,2,160,128]{3,2,1,0:T(8,128)(2,1)S(1)} collective-permute-done((bf16[2,2,160,128]{3,2,1,0:T(8,128)(2,1)S(1)}, bf16[2,2,160,128]{3,2,1,0:T(8,128)(2,1)S(1)}, u32[]{:S(2)}, u32[]{:S(2)}) %collective-permute-start.12) | collective-permute-done | bytes 163872 | tf_op jit(solution)/shard_map/ppermute | solution.py:474
  31.3 0.0 collective-permute-done.13.refs_3_
  31.3 0.0 copy-done.4
  31.3 0.1 broadcast_in_dim.8.refs_6_.refs_5_
  31.4 0.0 copy-done.5
  31.5 0.1 broadcast_in_dim.9.refs_7_.refs_6_
  31.6 1.7 %shard_map.89.own_ref = bf16[16,160,128]{2,1,0:T(8,128)(2,1)S(1)} custom-call(bf16[2,2,160,128]{3,2,1,0:T(8,128)(2,1)S(1)} %pad_maximum_fusion.refs_0_, bf16[2,2,160,128]{3,2,1,0:T(8,128)(2,1)S(1)} %collective-permute-done.11.refs_1_, bf16[2,2,160,128]{3,2,1,0:T(8,128)(2,1)S(1)} %collective-permute-done.12.refs_2_, ...), custom_call_target="tpu_custom_call" | custom-call | flops 471859200 | tf_op jit(solution)/shard_map/pallas_call | solution.py:446
  33.2 0.9 %collective-permute-start.17 = (bf16[16,160,128]{2,1,0:T(8,128)(2,1)S(1)}, bf16[16,160,128]{2,1,0:T(8,128)(2,1)S(1)}, u32[]{:S(2)}, u32[]{:S(2)}) collective-permute-start(bf16[16,160,128]{2,1,0:T(8,128)(2,1)S(1)} %shard_map.89.own_ref), channel_id=1, source_target_pairs={{0,4},{4,0},{8,12},{12,8},{16,20},{20,16},{24,28},{28,24},{1,5},{5... | collective-permute-start | bytes 1966088 | tf_op jit(solution)/shard_map/ppermute | solution.py:478
  34.2 0.1 collective-permute-start.10
  34.3 1.7 %collective-permute-done.10 = f32[8,128]{1,0:T(8,128)S(1)} collective-permute-done((f32[8,128]{1,0:T(8,128)S(1)}, f32[8,128]{1,0:T(8,128)S(1)}, u32[]{:S(2)}, u32[]{:S(2)}) %collective-permute-start.10) | collective-permute-done | bytes 4128 | tf_op jit(solution)/shard_map/ppermute | solution.py:478
  35.9 2.4 %collective-permute-start.14 = (f32[2,8,128]{2,1,0:T(8,128)S(1)}, f32[2,8,128]{2,1,0:T(8,128)S(1)}, u32[]{:S(2)}, u32[]{:S(2)}) collective-permute-start(f32[2,8,128]{2,1,0:T(8,128)S(1)} %pad_maximum_fusion.1.refs_0_), channel_id=1, source_target_pairs={{0,24},{4,28},{8,16},{12,20},{16,8},{20,12},{24,0},{28,4},{1,25},{... | collective-permute-start | bytes 24584 | tf_op jit(solution)/shard_map/ppermute | solution.py:474
  38.3 1.0 %collective-permute-start.15 = (f32[2,8,128]{2,1,0:T(8,128)S(1)}, f32[2,8,128]{2,1,0:T(8,128)S(1)}, u32[]{:S(2)}, u32[]{:S(2)}) collective-permute-start(f32[2,8,128]{2,1,0:T(8,128)S(1)} %pad_maximum_fusion.1.refs_0_), channel_id=1, source_target_pairs={{0,8},{4,12},{8,0},{12,4},{16,24},{20,28},{24,16},{28,20},{1,9},{5... | collective-permute-start | bytes 24584 | tf_op jit(solution)/shard_map/ppermute | solution.py:474
  39.3 0.1 collective-permute-start.16
  39.4 0.0 collective-permute-done.17.other_ref
  39.4 1.8 %shard_map.91 = (f32[225,128]{1,0:T(8,128)S(1)}, bf16[225,128]{1,0:T(8,128)(2,1)S(1)}, bf16[225,128]{1,0:T(8,128)(2,1)S(1)}, bf16[225,128]{1,0:T(8,128)(2,1)S(1)}, bf16[4,320,128]{2,1,0:T(8,128)(2,1)S(1)}) custom-call(bf16[16,160,128]{2,1,0:T(8,128)(2,1)S(1)} %shard_map.89.own_ref, bf16[16,160,128]{2,1,0:T(8,128)(2,1)S(1)} %collective-permute-done.17.other_ref, ...), custom_call_target="tpu_custom_call" | custom-call | flops 943718400 | tf_op jit(solution)/shard_map/pallas_call | solution.py:446
  41.2 3.7 %collective-permute-start.18 = (bf16[225,128]{1,0:T(8,128)(2,1)S(1)}, bf16[225,128]{1,0:T(8,128)(2,1)S(1)}, u32[]{:S(2)}, u32[]{:S(2)}) collective-permute-start(bf16[225,128]{1,0:T(8,128)(2,1)S(1)} %get-tuple-element.44), channel_id=1, source_target_pairs={{0,3},{1,2},{2,1},{3,0},{4,7},{5,6},{6,5},{7,4},{8,11},{9,10},{10,... | collective-permute-start | bytes 172808 | tf_op jit(solution)/shard_map/ppermute | solution.py:555
  44.9 0.0 collective-permute-start.19
  44.9 0.0 collective-permute-done.14.refs_1_
  44.9 0.8 %collective-permute-start.20 = (bf16[225,128]{1,0:T(8,128)(2,1)S(1)}, bf16[225,128]{1,0:T(8,128)(2,1)S(1)}, u32[]{:S(2)}, u32[]{:S(2)}) collective-permute-start(bf16[225,128]{1,0:T(8,128)(2,1)S(1)} %get-tuple-element.46), channel_id=1, source_target_pairs={{0,1},{1,0},{2,3},{3,2},{4,5},{5,4},{6,7},{7,6},{8,9},{9,8},{10,11... | collective-permute-start | bytes 172808 | tf_op jit(solution)/shard_map/ppermute | solution.py:555
  45.6 0.0 collective-permute-done.15.refs_2_
  45.6 0.0 collective-permute-done.16.refs_3_
  45.6 1.5 %shard_map.90 = bf16[2,320,128]{2,1,0:T(8,128)(2,1)} custom-call(f32[2,8,128]{2,1,0:T(8,128)S(1)} %pad_maximum_fusion.1.refs_0_, f32[2,8,128]{2,1,0:T(8,128)S(1)} %collective-permute-done.14.refs_1_, f32[2,8,128]{2,1,0:T(8,128)S(1)} %collective-permute-done.15.refs_2_, f32[2,8,128]{2,1,0:T(8,128)S(1)} %collective-permute-done.16.refs_3_, ...), custom_call_target="tpu_custom_call" | custom-call | flops 117964800 | tf_op jit(solution)/shard_map/pallas_call | solution.py:446
  47.1 1.7 %shard_map.92 = bf16[2,320,128]{2,1,0:T(8,128)(2,1)} custom-call(bf16[4,320,128]{2,1,0:T(8,128)(2,1)S(1)} %get-tuple-element.42.gz_ref, bf16[3,320,960]{2,1,0:T(8,128)(2,1)S(1)} %shard_map.85.w_ref.refs_8_), custom_call_target="tpu_custom_call" | custom-call | flops 471859200 | tf_op jit(solution)/shard_map/pallas_call | solution.py:446
  48.9 0.0 collective-permute-done.18
  48.9 1.1 %collective-permute-done.19 = bf16[225,128]{1,0:T(8,128)(2,1)S(1)} collective-permute-done((bf16[225,128]{1,0:T(8,128)(2,1)S(1)}, bf16[225,128]{1,0:T(8,128)(2,1)S(1)}, u32[]{:S(2)}, u32[]{:S(2)}) %collective-permute-start.19) | collective-permute-done | bytes 57632 | tf_op jit(solution)/shard_map/ppermute | solution.py:555
  50.0 0.0 collective-permute-done.20
  50.0 0.7 %add_bitcast_fusion = f32[28800]{0:T(1024)} fusion(bf16[225,128]{1,0:T(8,128)(2,1)S(1)} %collective-permute-done.20, bf16[225,128]{1,0:T(8,128)(2,1)S(1)} %collective-permute-done.19, f32[225,128]{1,0:T(8,128)S(1)} %get-tuple-element.43, bf16[225,128]{1,0:T(8,128)(2,1)S(1)} %collective-permute-done.18), kind=kLoop, calls=%fused_computation.1 | loop fusion | flops 172800 | bytes 403200 | tf_op jit(solution)/shard_map/reshape | solution.py:571
  (4 shorter events, 0.0 us)
Async XLA Ops:
  0.6 11.0 %collective-permute-start = (bf16[2,320,128]{2,1,0:T(8,128)(2,1)}, bf16[2,320,128]{2,1,0:T(8,128)(2,1)S(1)}, u32[]{:S(2)}, u32[]{:S(2)}) collective-permute-start(bf16[2,320,128]{2,1,0:T(8,128)(2,1)} %bitcast.19), channel_id=1, source_target_pairs={{0,8},{4,12},{8,0},{12,4},{16,24},{20,28},{24,16},{28,20},{1,9},{5... | collective-permute-start | bytes 491528 | tf_op jit(solution)/shard_map/ppermute | solution.py:474
  3.7 9.4 %collective-permute-start.1 = (bf16[2,320,128]{2,1,0:T(8,128)(2,1)}, bf16[2,320,128]{2,1,0:T(8,128)(2,1)S(1)}, u32[]{:S(2)}, u32[]{:S(2)}) collective-permute-start(bf16[2,320,128]{2,1,0:T(8,128)(2,1)} %bitcast.20), channel_id=1, source_target_pairs={{0,16},{4,20},{8,24},{12,28},{16,0},{20,4},{24,8},{28,12},{1,17},{... | collective-permute-start | bytes 491528 | tf_op jit(solution)/shard_map/ppermute | solution.py:474
  5.2 7.9 %collective-permute-start.2 = (bf16[2,320,128]{2,1,0:T(8,128)(2,1)}, bf16[2,320,128]{2,1,0:T(8,128)(2,1)S(1)}, u32[]{:S(2)}, u32[]{:S(2)}) collective-permute-start(bf16[2,320,128]{2,1,0:T(8,128)(2,1)} %bitcast.21), channel_id=1, source_target_pairs={{0,24},{4,28},{8,16},{12,20},{16,8},{20,12},{24,0},{28,4},{1,25},{... | collective-permute-start | bytes 491528 | tf_op jit(solution)/shard_map/ppermute | solution.py:474
  5.2 0.9 %copy-start.2 = (bf16[1,2,320,128]{3,2,1,0:T(8,128)(2,1)S(1)}, bf16[1,2,320,128]{3,2,1,0:T(8,128)(2,1)}, u32[]{:S(2)}) copy-start(bf16[1,2,320,128]{3,2,1,0:T(8,128)(2,1)} %param.8) | copy-start | bytes 491524
  6.1 5.5 %collective-permute-start.4 = (bf16[2,160,128]{2,1,0:T(8,128)(2,1)S(1)}, bf16[2,160,128]{2,1,0:T(8,128)(2,1)S(1)}, u32[]{:S(2)}, u32[]{:S(2)}) collective-permute-start(bf16[2,160,128]{2,1,0:T(8,128)(2,1)S(1)} %get-tuple-element.26), channel_id=1, source_target_pairs={{0,4},{4,0},{8,12},{12,8},{16,20},{20,16},{24,28},{28,24},{1,5},{5... | collective-permute-start | bytes 245768 | tf_op jit(solution)/shard_map/ppermute | solution.py:478
  7.2 4.5 %collective-permute-start.3 = (bf16[320,128]{1,0:T(8,128)(2,1)S(1)}, bf16[320,128]{1,0:T(8,128)(2,1)S(1)}, u32[]{:S(2)}, u32[]{:S(2)}) collective-permute-start(bf16[320,128]{1,0:T(8,128)(2,1)S(1)} %get-tuple-element.48), channel_id=1, source_target_pairs={{0,4},{4,8},{8,12},{12,16},{16,20},{20,24},{24,28},{1,5},{5,9},{9,... | collective-permute-start | bytes 245768 | tf_op jit(solution)/shard_map/ppermute | solution.py:482
  9.6 1.6 %copy-start = (bf16[3,3,320,320]{3,2,1,0:T(8,128)(2,1)S(1)}, bf16[3,3,320,320]{3,2,1,0:T(8,128)(2,1)}, u32[]{:S(2)}) copy-start(bf16[3,3,320,320]{3,2,1,0:T(8,128)(2,1)} %w_ref.1) | copy-start | bytes 5529604
  11.2 1.9 %copy-start.3 = (bf16[1,2,320,128]{3,2,1,0:T(8,128)(2,1)S(1)}, bf16[1,2,320,128]{3,2,1,0:T(8,128)(2,1)}, u32[]{:S(2)}) copy-start(bf16[1,2,320,128]{3,2,1,0:T(8,128)(2,1)} %param.7) | copy-start | bytes 491524
  11.2 9.1 %copy-start.1 = (bf16[1,2,320,128]{3,2,1,0:T(8,128)(2,1)S(1)}, bf16[1,2,320,128]{3,2,1,0:T(8,128)(2,1)}, u32[]{:S(2)}) copy-start(bf16[1,2,320,128]{3,2,1,0:T(8,128)(2,1)} %param.6) | copy-start | bytes 491524
  13.0 8.4 %collective-permute-start.6 = (bf16[2,320,128]{2,1,0:T(8,128)(2,1)S(1)}, bf16[2,320,128]{2,1,0:T(8,128)(2,1)S(1)}, u32[]{:S(2)}, u32[]{:S(2)}) collective-permute-start(bf16[2,320,128]{2,1,0:T(8,128)(2,1)S(1)} %bitcast.22), channel_id=1, source_target_pairs={{0,4},{4,0},{8,12},{12,8},{16,20},{20,16},{24,28},{28,24},{1,5},{5... | collective-permute-start | bytes 491528 | tf_op jit(solution)/shard_map/ppermute | solution.py:478
  13.7 10.1 %collective-permute-start.7 = (bf16[2,320,128]{2,1,0:T(8,128)(2,1)S(1)}, bf16[2,320,128]{2,1,0:T(8,128)(2,1)S(1)}, u32[]{:S(2)}, u32[]{:S(2)}) collective-permute-start(bf16[2,320,128]{2,1,0:T(8,128)(2,1)S(1)} %collective-permute-done.refs_2_), channel_id=1, source_target_pairs={{0,4},{4,0},{8,12},{12,8},{16,20},{20,16},{24,28},{28,24},{1,5},{5... | collective-permute-start | bytes 491528 | tf_op jit(solution)/shard_map/ppermute | solution.py:478
  13.7 10.3 %collective-permute-start.8 = (bf16[2,320,128]{2,1,0:T(8,128)(2,1)S(1)}, bf16[2,320,128]{2,1,0:T(8,128)(2,1)S(1)}, u32[]{:S(2)}, u32[]{:S(2)}) collective-permute-start(bf16[2,320,128]{2,1,0:T(8,128)(2,1)S(1)} %collective-permute-done.1.refs_4_), channel_id=1, source_target_pairs={{0,4},{4,0},{8,12},{12,8},{16,20},{20,16},{24,28},{28,24},{1,5},{5... | collective-permute-start | bytes 491528 | tf_op jit(solution)/shard_map/ppermute | solution.py:478
  14.2 9.8 %collective-permute-start.9 = (bf16[2,320,128]{2,1,0:T(8,128)(2,1)S(1)}, bf16[2,320,128]{2,1,0:T(8,128)(2,1)S(1)}, u32[]{:S(2)}, u32[]{:S(2)}) collective-permute-start(bf16[2,320,128]{2,1,0:T(8,128)(2,1)S(1)} %collective-permute-done.2.refs_6_), channel_id=1, source_target_pairs={{0,4},{4,0},{8,12},{12,8},{16,20},{20,16},{24,28},{28,24},{1,5},{5... | collective-permute-start | bytes 491528 | tf_op jit(solution)/shard_map/ppermute | solution.py:478
  14.2 3.2 %collective-permute-start.5 = (bf16[320,128]{1,0:T(8,128)(2,1)S(1)}, bf16[320,128]{1,0:T(8,128)(2,1)S(1)}, u32[]{:S(2)}, u32[]{:S(2)}) collective-permute-start(bf16[320,128]{1,0:T(8,128)(2,1)S(1)} %get-tuple-element.47), channel_id=1, source_target_pairs={{4,0},{8,4},{12,8},{16,12},{20,16},{24,20},{28,24},{5,1},{9,5},{13... | collective-permute-start | bytes 245768 | tf_op jit(solution)/shard_map/ppermute | solution.py:483
  17.4 11.5 %collective-permute-start.11 = (bf16[2,2,160,128]{3,2,1,0:T(8,128)(2,1)S(1)}, bf16[2,2,160,128]{3,2,1,0:T(8,128)(2,1)S(1)}, u32[]{:S(2)}, u32[]{:S(2)}) collective-permute-start(bf16[2,2,160,128]{3,2,1,0:T(8,128)(2,1)S(1)} %pad_maximum_fusion.refs_0_), channel_id=1, source_target_pairs={{0,8},{4,12},{8,0},{12,4},{16,24},{20,28},{24,16},{28,20},{1,9},{5... | collective-permute-start | bytes 491528 | tf_op jit(solution)/shard_map/ppermute | solution.py:474
  21.4 9.9 %copy-start.4 = (f32[320]{0:T(512)S(1)}, f32[320]{0:T(512)}, u32[]{:S(2)}) copy-start(f32[320]{0:T(512)} %param.10) | copy-start | bytes 3844
  21.4 10.0 %copy-start.5 = (f32[320]{0:T(512)S(1)}, f32[320]{0:T(512)}, u32[]{:S(2)}) copy-start(f32[320]{0:T(512)} %param.11) | copy-start | bytes 3844
  21.5 9.8 %collective-permute-start.12 = (bf16[2,2,160,128]{3,2,1,0:T(8,128)(2,1)S(1)}, bf16[2,2,160,128]{3,2,1,0:T(8,128)(2,1)S(1)}, u32[]{:S(2)}, u32[]{:S(2)}) collective-permute-start(bf16[2,2,160,128]{3,2,1,0:T(8,128)(2,1)S(1)} %pad_maximum_fusion.refs_0_), channel_id=1, source_target_pairs={{0,16},{4,20},{8,24},{12,28},{16,0},{20,4},{24,8},{28,12},{1,17},{... | collective-permute-start | bytes 491528 | tf_op jit(solution)/shard_map/ppermute | solution.py:474
  23.8 7.5 %collective-permute-start.13 = (bf16[2,2,160,128]{3,2,1,0:T(8,128)(2,1)S(1)}, bf16[2,2,160,128]{3,2,1,0:T(8,128)(2,1)S(1)}, u32[]{:S(2)}, u32[]{:S(2)}) collective-permute-start(bf16[2,2,160,128]{3,2,1,0:T(8,128)(2,1)S(1)} %pad_maximum_fusion.refs_0_), channel_id=1, source_target_pairs={{0,24},{4,28},{8,16},{12,20},{16,8},{20,12},{24,0},{28,4},{1,25},{... | collective-permute-start | bytes 491528 | tf_op jit(solution)/shard_map/ppermute | solution.py:474
  33.2 6.2 %collective-permute-start.17 = (bf16[16,160,128]{2,1,0:T(8,128)(2,1)S(1)}, bf16[16,160,128]{2,1,0:T(8,128)(2,1)S(1)}, u32[]{:S(2)}, u32[]{:S(2)}) collective-permute-start(bf16[16,160,128]{2,1,0:T(8,128)(2,1)S(1)} %shard_map.89.own_ref), channel_id=1, source_target_pairs={{0,4},{4,0},{8,12},{12,8},{16,20},{20,16},{24,28},{28,24},{1,5},{5... | collective-permute-start | bytes 1966088 | tf_op jit(solution)/shard_map/ppermute | solution.py:478
  34.2 1.7 %collective-permute-start.10 = (f32[8,128]{1,0:T(8,128)S(1)}, f32[8,128]{1,0:T(8,128)S(1)}, u32[]{:S(2)}, u32[]{:S(2)}) collective-permute-start(f32[8,128]{1,0:T(8,128)S(1)} %get-tuple-element.35), channel_id=1, source_target_pairs={{0,4},{4,0},{8,12},{12,8},{16,20},{20,16},{24,28},{28,24},{1,5},{5... | collective-permute-start | bytes 12296 | tf_op jit(solution)/shard_map/ppermute | solution.py:478
  35.9 8.9 %collective-permute-start.14 = (f32[2,8,128]{2,1,0:T(8,128)S(1)}, f32[2,8,128]{2,1,0:T(8,128)S(1)}, u32[]{:S(2)}, u32[]{:S(2)}) collective-permute-start(f32[2,8,128]{2,1,0:T(8,128)S(1)} %pad_maximum_fusion.1.refs_0_), channel_id=1, source_target_pairs={{0,24},{4,28},{8,16},{12,20},{16,8},{20,12},{24,0},{28,4},{1,25},{... | collective-permute-start | bytes 24584 | tf_op jit(solution)/shard_map/ppermute | solution.py:474
  38.3 7.3 %collective-permute-start.15 = (f32[2,8,128]{2,1,0:T(8,128)S(1)}, f32[2,8,128]{2,1,0:T(8,128)S(1)}, u32[]{:S(2)}, u32[]{:S(2)}) collective-permute-start(f32[2,8,128]{2,1,0:T(8,128)S(1)} %pad_maximum_fusion.1.refs_0_), channel_id=1, source_target_pairs={{0,8},{4,12},{8,0},{12,4},{16,24},{20,28},{24,16},{28,20},{1,9},{5... | collective-permute-start | bytes 24584 | tf_op jit(solution)/shard_map/ppermute | solution.py:474
  39.3 6.4 %collective-permute-start.16 = (f32[2,8,128]{2,1,0:T(8,128)S(1)}, f32[2,8,128]{2,1,0:T(8,128)S(1)}, u32[]{:S(2)}, u32[]{:S(2)}) collective-permute-start(f32[2,8,128]{2,1,0:T(8,128)S(1)} %pad_maximum_fusion.1.refs_0_), channel_id=1, source_target_pairs={{0,16},{4,20},{8,24},{12,28},{16,0},{20,4},{24,8},{28,12},{1,17},{... | collective-permute-start | bytes 24584 | tf_op jit(solution)/shard_map/ppermute | solution.py:474
  41.2 7.7 %collective-permute-start.18 = (bf16[225,128]{1,0:T(8,128)(2,1)S(1)}, bf16[225,128]{1,0:T(8,128)(2,1)S(1)}, u32[]{:S(2)}, u32[]{:S(2)}) collective-permute-start(bf16[225,128]{1,0:T(8,128)(2,1)S(1)} %get-tuple-element.44), channel_id=1, source_target_pairs={{0,3},{1,2},{2,1},{3,0},{4,7},{5,6},{6,5},{7,4},{8,11},{9,10},{10,... | collective-permute-start | bytes 172808 | tf_op jit(solution)/shard_map/ppermute | solution.py:555
  44.9 5.1 %collective-permute-start.19 = (bf16[225,128]{1,0:T(8,128)(2,1)S(1)}, bf16[225,128]{1,0:T(8,128)(2,1)S(1)}, u32[]{:S(2)}, u32[]{:S(2)}) collective-permute-start(bf16[225,128]{1,0:T(8,128)(2,1)S(1)} %get-tuple-element.45), channel_id=1, source_target_pairs={{0,2},{1,3},{2,0},{3,1},{4,6},{5,7},{6,4},{7,5},{8,10},{9,11},{10,... | collective-permute-start | bytes 172808 | tf_op jit(solution)/shard_map/ppermute | solution.py:555
  44.9 5.1 %collective-permute-start.20 = (bf16[225,128]{1,0:T(8,128)(2,1)S(1)}, bf16[225,128]{1,0:T(8,128)(2,1)S(1)}, u32[]{:S(2)}, u32[]{:S(2)}) collective-permute-start(bf16[225,128]{1,0:T(8,128)(2,1)S(1)} %get-tuple-element.46), channel_id=1, source_target_pairs={{0,1},{1,0},{2,3},{3,2},{4,5},{5,4},{6,7},{7,6},{8,9},{9,8},{10,11... | collective-permute-start | bytes 172808 | tf_op jit(solution)/shard_map/ppermute | solution.py:555
where the time goes:
time: 50.9 us; the launch traced here: 50.6 us
  starting transfers between devices  23.9 us (47%)
  Pallas kernels  13 us (26%)
  waiting for transfers between devices  8.56 us (17%)
  local copies, waits for them, and re-layouts  3.7 us (7%)
  between operations  0.8 us (2%)
  other arithmetic  0.7 us (1%)
    ppermute x9, starting transfers between devices, far(): held[k] = lax.ppermute(own, 'height', pairs(blocks, k))  13.5 us
    pallas_call x8, Pallas kernels, call(): pl.pallas_call(functools.partial(kernel, **static), out_shape=out_shape,...  13 us
    ppermute x3, starting transfers between devices, gathered(): lax.ppermute(results[s], 'dp', pairs(groups_dp, s)).astype(F32)  4.45 us
    ppermute x9, waiting for transfers between devices, far(): held[k] = lax.ppermute(own, 'height', pairs(blocks, k))  3.9 us
    unnamed x12, local copies, waits for them, and re-layouts  2.56 us
    ppermute x1, starting transfers between devices, gathered(): lax.ppermute(x_next[rows - 1], 'height', [(i, i + 1) for i in range(ends)])  2.4 us
    ppermute x7, starting transfers between devices, near(): return lax.ppermute(own, 'height', pairs(blocks, 1))  2.24 us
    ppermute x1, waiting for transfers between devices, gathered(): lax.ppermute(x_next[0], 'height', [(i + 1, i) for i in range(ends)])  1.88 us
  transfers between devices with their start and end apart: 21, of which 5 were waited for; matrix products, arithmetic and copies ran while one was open for 2% of the time, Pallas kernels for 22%

commit v1 on v0

--- a/solution.py
+++ b/solution.py
@@ -180,23 +180,28 @@
     return 1.0 / (1.0 + jnp.exp(-value))
 
 
-def weights_kernel(w_ref, flat_ref):
+def weights_kernel(w_ref, flat_ref, held, sems):
     chans = flat_ref.shape[1]
+    copies = [pltpu.make_async_copy(w_ref.at[a], held.at[a], sems.at[a]) for a in range(3)]
+    for copy in copies:
+        copy.start()
     for a in range(3):
+        copies[a].wait()
         for b in range(3):
-            flat_ref[a, :, b * chans : (b + 1) * chans] = w_ref[a, b]
-
-
-def halves_kernel(g_ref, own_ref, other_ref):
-    half = own_ref.shape[1]
+            flat_ref[a, :, b * chans : (b + 1) * chans] = held[a, b]
+
+
+def halves_kernel(own_ref, near_ref, out_ref):
+    half = out_ref.shape[2]
     core = lax.axis_index("height") & 1
-    for r in range(own_ref.shape[0]):
-        own_ref[r] = g_ref[r, pl.ds(pl.multiple_of(core * half, 16), half)]
-        other_ref[r] = g_ref[r, pl.ds(pl.multiple_of((1 - core) * half, 16), half)]
+    mine = pl.ds(pl.multiple_of(core * half, 16), half)
+    for r in range(out_ref.shape[1]):
+        out_ref[0, r] = own_ref[r, mine]
+        out_ref[1, r] = near_ref[r, mine]
 
 
 def next_conv_kernel(top_ref, x_ref, bottom_ref, w_ref, z_ref, stat_ref, *, rows):
-    cells = [top_ref[...]] + [x_ref[r] for r in range(rows)] + [bottom_ref[...]]
+    cells = [top_ref[rows - 1]] + [x_ref[r] for r in range(rows)] + [bottom_ref[0]]
     chans, width = cells[0].shape
     sides = [[moved_bf16(cell, 1) for cell in cells], cells, [moved_bf16(cell, -1) for cell in cells]]
     stacks = [jnp.concatenate([side[r] for side in sides], axis=0) for r in range(rows + 2)]
@@ -259,12 +264,11 @@
 
 def conv_kernel(*refs, blocks, rows, count, wide):
     x_refs = refs[:blocks]
-    w_ref, xs, z, norm, total_ref = refs[blocks:]
+    w_ref, xs, z, norm, lane = refs[blocks:]
     image, half, width = z.shape
     chans = x_refs[0].shape[1]
     home = lax.axis_index("height")
     mine = pl.ds(pl.multiple_of((home & 1) * half, 16), half)
-    step = 16
 
     edge = jnp.zeros((3 * chans, width), BF16)
     xs[0] = edge
@@ -277,7 +281,7 @@
             xs[base + r, :chans] = moved_bf16(cell, 1)
             xs[base + r, 2 * chans :] = moved_bf16(cell, -1)
 
-    def conv(p, carry):
+    def conv(p, start=False):
         row = p * wide
         total = None
         for a in range(3):
@@ -287,31 +291,24 @@
         parts = [total[:, i * width : (i + 1) * width] for i in range(wide)]
         for i in range(wide):
             z[row + i] = parts[i]
-        return carry
-
-    lax.fori_loop(0, image // wide, conv, 0)
+        offs = [part - (parts[0] if start else z[0]) for part in parts]
+        sums = functools.reduce(jnp.add, offs)
+        squares = functools.reduce(jnp.add, [off * off for off in offs])
+        lane[0] = sums if start else lane[0] + sums
+        lane[1] = squares if start else lane[1] + squares
+
+    conv(0, True)
+    lax.fori_loop(1, image // wide, lambda p, carry: conv(p) or carry, 0)
+
     same = same_group(half, chans)
-
-    def summed(i, carry):
-        at = pl.ds(pl.multiple_of(i * step, step), step)
-        total_ref[at] = functools.reduce(jnp.add, [z[r, at] for r in range(image)])
-        return carry
-
-    lax.fori_loop(0, half // step, summed, 0)
-    norm[0] = group_total(same, total_ref[...]) * (1.0 / count)
-
-    def squared(i, carry):
-        at = pl.ds(pl.multiple_of(i * step, step), step)
-        mean = norm[0, at]
-        total = None
-        for r in range(image):
-            off = z[r, at] - mean
-            total = off * off if total is None else total + off * off
-        total_ref[at] = total
-        return carry
-
-    lax.fori_loop(0, half // step, squared, 0)
-    norm[1] = lax.rsqrt(group_total(same, total_ref[...]) * (1.0 / count) + eps)
+    middle = lane[0] * (1.0 / image)
+    spread = lane[1] - middle * lane[0]
+    middle = z[0] + middle
+    mean = group_total(same, middle) * (float(image) / count)
+    norm[0] = mean
+    apart = middle - mean
+    var = group_total(same, spread + apart * apart * float(image)) * (1.0 / count)
+    norm[1] = lax.rsqrt(var + eps)
 
 
 def pull_kernel(*refs, blocks, rows, count):
@@ -479,16 +476,26 @@
 
     x_far = far(x_cur[0])
     ends = blocks - 1
-    top = lax.ppermute(x_next[rows - 1], "height", [(i, i + 1) for i in range(ends)])
-    bottom = lax.ppermute(x_next[0], "height", [(i + 1, i) for i in range(ends)])
-    own_half, other_half = call(halves_kernel, (shape((rows, half, width), BF16),) * 2, (grad_out,))
-    g_pair = jnp.stack((own_half, near(other_half)))
+    top = lax.ppermute(x_next, "height", [(i, i + 1) for i in range(ends)])
+    bottom = lax.ppermute(x_next, "height", [(i + 1, i) for i in range(ends)])
+    g_near = near(grad_out)
+    g_pair = call(halves_kernel, shape((2, rows, half, width), BF16), (grad_out, g_near))
     g_far = far(g_pair)
     gain = jnp.broadcast_to(gamma[:, None], (chans, width))
     shift = jnp.broadcast_to(beta[:, None], (chans, width))
-    w_flat = call(weights_kernel, shape((3, chans, 3 * chans), BF16), (kernel,))
-
-    x_far, top, w_flat, _ = lax.optimization_barrier((x_far, top, w_flat, g_pair))
+    w_flat = pl.pallas_call(
+        weights_kernel,
+        out_shape=shape((3, chans, 3 * chans), BF16),
+        in_specs=[pl.BlockSpec(memory_space=pltpu.HBM)],
+        out_specs=vmem(1)[0],
+        scratch_shapes=[pltpu.VMEM((3, 3, chans, chans), BF16), pltpu.SemaphoreType.DMA((3,))],
+        compiler_params=params(),
+        name="weights",
+    )(pltpu.with_memory_space_constraint(kernel, pltpu.HBM))
+
+    x_far, top, w_flat, gain, shift, _ = lax.optimization_barrier(
+        (x_far, top, w_flat, gain, shift, g_pair)
+    )
     x_all = []
     for k in range(0, blocks, 2):
         x_all += [x_far[k], near(x_far[k])]
@@ -499,6 +506,8 @@
         flops=rows * flops,
         rows=rows,
     )
+    stat_near = near(stat)
+    x_all, z_next = lax.optimization_barrier((x_all, z_next))
     xs, z_cur, norm = call(
         conv_kernel,
         (
@@ -507,15 +516,14 @@
             shape((2, half, width), F32),
         ),
         (*x_all, w_flat),
-        scratch=(pltpu.VMEM((half, width), F32),),
+        scratch=(pltpu.VMEM((2, half, width), F32),),
         flops=image * flops // 2,
         blocks=blocks,
         rows=rows,
         count=count,
         wide=4 if image % 4 == 0 else 2,
     )
-    stat, norm = lax.optimization_barrier((stat, norm))
-    stat_pair = jnp.stack((stat, near(stat)))
+    stat_pair = jnp.stack((stat, stat_near))
     gz_own = call(
         pull_kernel,
         shape((image, half, width), BF16),

time: 50.9 us -> 47.4 us (0.931)
  local copies, waits for them, and re-layouts: 3.7 us -> 0.21 us
  starting transfers between devices: 23.9 us -> 21.4 us
  waiting for transfers between devices: 8.56 us -> 9.96 us
  Pallas kernels: 13 us -> 14.2 us
    ppermute x9, waiting for transfers between devices: 3.9 us -> 7.25 us  [far(): held[k] = lax.ppermute(own, 'height', pairs(blocks, k))]
    unnamed x12 -> x10, local copies, waits for them, and re-layouts: 2.56 us -> 0.02 us
    ppermute x9, starting transfers between devices: 13.5 us -> 11.6 us  [far(): held[k] = lax.ppermute(own, 'height', pairs(blocks, k))]
    ppermute x2, waiting for transfers between devices: 1.88 us -> 0.01 us  [the longest x1 0.01 us: gathered(): top = lax.ppermute(x_next, 'height', [(i, i + 1) for i in range(ends)])]
    pallas_call x0 -> x1, Pallas kernels: none -> 1.78 us  [gathered(): pl.pallas_call(weights_kernel, out_shape=shape((3, chans, 3 * chans), BF1...]
    squeeze x1 -> x0, local copies, waits for them, and re-layouts: 0.94 us -> none  [gathered(): x_next[0]]
    pallas_call x8 -> x7, Pallas kernels: 13 us -> 12.4 us  [call(): pl.pallas_call(functools.partial(kernel, **static), out_shape=out_shape,...]
  transfers between devices with their start and end apart: 21 -> 21, of which waited for: 5 -> 4; matrix products, arithmetic and copies ran while one was open for 2% -> 0% of each run, Pallas kernels for 22% -> 26%
where the time goes in v1:
time: 47.4 us; the launch traced here: 47.2 us
  starting transfers between devices  21.4 us (45%)
  Pallas kernels  14.2 us (30%)
  waiting for transfers between devices  9.96 us (21%)
  between operations  0.8 us (2%)
  other arithmetic  0.68 us (1%)
    pallas_call x7, Pallas kernels, call(): pl.pallas_call(functools.partial(kernel, **static), out_shape=out_shape,...  12.4 us
    ppermute x9, starting transfers between devices, far(): held[k] = lax.ppermute(own, 'height', pairs(blocks, k))  11.6 us
    ppermute x9, waiting for transfers between devices, far(): held[k] = lax.ppermute(own, 'height', pairs(blocks, k))  7.25 us
    ppermute x3, starting transfers between devices, gathered(): lax.ppermute(results[s], 'dp', pairs(groups_dp, s)).astype(F32)  4.45 us
    ppermute x7, starting transfers between devices, near(): return lax.ppermute(own, 'height', pairs(blocks, 1))  2.21 us
    ppermute x1, starting transfers between devices, gathered(): top = lax.ppermute(x_next, 'height', [(i, i + 1) for i in range(ends)])  1.91 us
    pallas_call x1, Pallas kernels, gathered(): pl.pallas_call(weights_kernel, out_shape=shape((3, chans, 3 * chans), BF1...  1.78 us
    ppermute x7, waiting for transfers between devices, near(): return lax.ppermute(own, 'height', pairs(blocks, 1))  1.61 us
  transfers between devices with their start and end apart: 21, of which 4 were waited for; matrix products, arithmetic and copies ran while one was open for 0% of the time, Pallas kernels for 26%

profile of v1, /device:TPU:0, one launch (start us, length us, event | category | flops | bytes accessed | tf_op | source)
XLA Modules:
  0.0 47.2 jit_solution(17217044609202594184)
XLA Ops:
  0.6 0.0 copy-start.1
  0.6 0.6 %collective-permute-start.4 = (bf16[2,320,128]{2,1,0:T(8,128)(2,1)}, bf16[2,320,128]{2,1,0:T(8,128)(2,1)S(1)}, u32[]{:S(2)}, u32[]{:S(2)}) collective-permute-start(bf16[2,320,128]{2,1,0:T(8,128)(2,1)} %bitcast.12), channel_id=1, source_target_pairs={{0,4},{4,0},{8,12},{12,8},{16,20},{20,16},{24,28},{28,24},{1,5},{5... | collective-permute-start | bytes 491528 | tf_op jit(solution)/shard_map/ppermute | solution.py:475
  1.2 2.6 %collective-permute-start = (bf16[2,320,128]{2,1,0:T(8,128)(2,1)}, bf16[2,320,128]{2,1,0:T(8,128)(2,1)S(1)}, u32[]{:S(2)}, u32[]{:S(2)}) collective-permute-start(bf16[2,320,128]{2,1,0:T(8,128)(2,1)} %bitcast.15), channel_id=1, source_target_pairs={{0,8},{4,12},{8,0},{12,4},{16,24},{20,28},{24,16},{28,20},{1,9},{5... | collective-permute-start | bytes 491528 | tf_op jit(solution)/shard_map/ppermute | solution.py:471
  3.8 1.5 %collective-permute-start.1 = (bf16[2,320,128]{2,1,0:T(8,128)(2,1)}, bf16[2,320,128]{2,1,0:T(8,128)(2,1)S(1)}, u32[]{:S(2)}, u32[]{:S(2)}) collective-permute-start(bf16[2,320,128]{2,1,0:T(8,128)(2,1)} %bitcast.16), channel_id=1, source_target_pairs={{0,16},{4,20},{8,24},{12,28},{16,0},{20,4},{24,8},{28,12},{1,17},{... | collective-permute-start | bytes 491528 | tf_op jit(solution)/shard_map/ppermute | solution.py:471
  5.3 0.0 collective-permute-start.2
  5.3 0.0 copy-start.3
  5.3 0.0 copy-start.4
  5.3 0.0 copy-start.2
  5.3 0.0 copy-start
  5.3 1.9 %collective-permute-start.3 = (bf16[2,320,128]{2,1,0:T(8,128)(2,1)}, bf16[2,320,128]{2,1,0:T(8,128)(2,1)S(1)}, u32[]{:S(2)}, u32[]{:S(2)}) collective-permute-start(bf16[2,320,128]{2,1,0:T(8,128)(2,1)} %bitcast.9), channel_id=1, source_target_pairs={{0,4},{4,8},{8,12},{12,16},{16,20},{20,24},{24,28},{1,5},{5,9},{9,... | collective-permute-start | bytes 491528 | tf_op jit(solution)/shard_map/ppermute | solution.py:479
  7.2 0.0 collective-permute-done.4.near_ref
  7.2 1.3 %collective-permute-start.5 = (bf16[2,320,128]{2,1,0:T(8,128)(2,1)}, bf16[2,320,128]{2,1,0:T(8,128)(2,1)S(1)}, u32[]{:S(2)}, u32[]{:S(2)}) collective-permute-start(bf16[2,320,128]{2,1,0:T(8,128)(2,1)} %bitcast.10), channel_id=1, source_target_pairs={{4,0},{8,4},{12,8},{16,12},{20,16},{24,20},{28,24},{5,1},{9,5},{13... | collective-permute-start | bytes 491528 | tf_op jit(solution)/shard_map/ppermute | solution.py:480
  8.5 1.8 %weights.1.w_ref.refs_8_ = bf16[3,320,960]{2,1,0:T(8,128)(2,1)S(1)} custom-call(bf16[3,3,320,320]{3,2,1,0:T(8,128)(2,1)} %w_ref.1), custom_call_target="tpu_custom_call" | custom-call | tf_op jit(solution)/shard_map/weights/pallas_call | solution.py:486
  10.3 0.0 copy-done.1
  10.4 0.0 collective-permute-done.refs_2_
  10.4 4.3 %collective-permute-done.1.refs_4_ = bf16[2,320,128]{2,1,0:T(8,128)(2,1)S(1)} collective-permute-done((bf16[2,320,128]{2,1,0:T(8,128)(2,1)}, bf16[2,320,128]{2,1,0:T(8,128)(2,1)S(1)}, u32[]{:S(2)}, u32[]{:S(2)}) %collective-permute-start.1) | collective-permute-done | bytes 163872 | tf_op jit(solution)/shard_map/ppermute | solution.py:471
  14.6 0.0 collective-permute-done.2.refs_6_
  14.6 0.0 collective-permute-done.3.top_ref
  14.6 0.0 copy-done.3
  14.6 0.1 broadcast_in_dim.8.refs_6_.refs_5_
  14.7 0.0 copy-done.4
  14.8 0.1 broadcast_in_dim.9.refs_7_.refs_6_
  14.9 0.0 copy-done.2
  14.9 0.1 collective-permute-start.10
  14.9 0.5 %collective-permute-start.11 = (bf16[2,320,128]{2,1,0:T(8,128)(2,1)S(1)}, bf16[2,320,128]{2,1,0:T(8,128)(2,1)S(1)}, u32[]{:S(2)}, u32[]{:S(2)}) collective-permute-start(bf16[2,320,128]{2,1,0:T(8,128)(2,1)S(1)} %collective-permute-done.refs_2_), channel_id=1, source_target_pairs={{0,4},{4,0},{8,12},{12,8},{16,20},{20,16},{24,28},{28,24},{1,5},{5... | collective-permute-start | bytes 491528 | tf_op jit(solution)/shard_map/ppermute | solution.py:475
  15.4 0.1 collective-permute-start.12
  15.5 0.4 collective-permute-start.13
  16.0 0.0 collective-permute-done.5.bottom_ref
  16.0 1.2 %collective-permute-start.7 = (bf16[2,2,160,128]{3,2,1,0:T(8,128)(2,1)S(1)}, bf16[2,2,160,128]{3,2,1,0:T(8,128)(2,1)S(1)}, u32[]{:S(2)}, u32[]{:S(2)}) collective-permute-start(bf16[2,2,160,128]{3,2,1,0:T(8,128)(2,1)S(1)} %shard_map.85.refs_0_), channel_id=1, source_target_pairs={{0,8},{4,12},{8,0},{12,4},{16,24},{20,28},{24,16},{28,20},{1,9},{5... | collective-permute-start | bytes 491528 | tf_op jit(solution)/shard_map/ppermute | solution.py:471
  17.1 0.0 copy-done
  17.1 1.2 %shard_map.86 = (f32[2,320,128]{2,1,0:T(8,128)S(1)}, f32[8,128]{1,0:T(8,128)S(1)}) custom-call(bf16[2,320,128]{2,1,0:T(8,128)(2,1)S(1)} %collective-permute-done.3.top_ref, bf16[2,320,128]{2,1,0:T(8,128)(2,1)S(1)} %bitcast.11, bf16[2,320,128]{2,1,0:T(8,128)(2,1)S(1)} %collective-permute-done.5.bottom_ref, bf16[3,320,960]{2,1,0:T(8,128)(2,1)S(1)} %weights.1.w_ref.refs_8_), custom_call_target="tpu_custom_call" | custom-call | flops 471859200 | tf_op jit(solution)/shard_map/pallas_call | solution.py:443
  18.3 0.0 collective-permute-done.10.refs_1_
  18.3 1.5 %collective-permute-start.8 = (bf16[2,2,160,128]{3,2,1,0:T(8,128)(2,1)S(1)}, bf16[2,2,160,128]{3,2,1,0:T(8,128)(2,1)S(1)}, u32[]{:S(2)}, u32[]{:S(2)}) collective-permute-start(bf16[2,2,160,128]{3,2,1,0:T(8,128)(2,1)S(1)} %shard_map.85.refs_0_), channel_id=1, source_target_pairs={{0,16},{4,20},{8,24},{12,28},{16,0},{20,4},{24,8},{28,12},{1,17},{... | collective-permute-start | bytes 491528 | tf_op jit(solution)/shard_map/ppermute | solution.py:471
  19.8 0.0 collective-permute-done.11.refs_3_
  19.8 1.3 %collective-permute-start.9 = (bf16[2,2,160,128]{3,2,1,0:T(8,128)(2,1)S(1)}, bf16[2,2,160,128]{3,2,1,0:T(8,128)(2,1)S(1)}, u32[]{:S(2)}, u32[]{:S(2)}) collective-permute-start(bf16[2,2,160,128]{3,2,1,0:T(8,128)(2,1)S(1)} %shard_map.85.refs_0_), channel_id=1, source_target_pairs={{0,24},{4,28},{8,16},{12,20},{16,8},{20,12},{24,0},{28,4},{1,25},{... | collective-permute-start | bytes 491528 | tf_op jit(solution)/shard_map/ppermute | solution.py:471
  21.1 0.0 collective-permute-done.12.refs_5_
  21.1 0.0 collective-permute-done.13.refs_7_
  21.1 4.6 %shard_map.87 = (bf16[18,960,128]{2,1,0:T(8,128)(2,1)S(1)}, f32[16,160,128]{2,1,0:T(8,128)S(1)}, f32[2,160,128]{2,1,0:T(8,128)S(1)}) custom-call(bf16[2,320,128]{2,1,0:T(8,128)(2,1)S(1)} %bitcast.19, bf16[2,320,128]{2,1,0:T(8,128)(2,1)S(1)} %collective-permute-done.10.refs_1_, bf16[2,320,128]{2,1,0:T(8,128)(2,1)S(1)} %collective-permute-done.refs_2_, ...), custom_call_target="tpu_custom_call" | custom-call | flops 1887436800 | tf_op jit(solution)/shard_map/pallas_call | solution.py:443
  25.7 0.0 collective-permute-done.7.refs_1_
  25.7 3.0 %collective-permute-done.8.refs_2_ = bf16[2,2,160,128]{3,2,1,0:T(8,128)(2,1)S(1)} collective-permute-done((bf16[2,2,160,128]{3,2,1,0:T(8,128)(2,1)S(1)}, bf16[2,2,160,128]{3,2,1,0:T(8,128)(2,1)S(1)}, u32[]{:S(2)}, u32[]{:S(2)}) %collective-permute-start.8) | collective-permute-done | bytes 163872 | tf_op jit(solution)/shard_map/ppermute | solution.py:471
  28.7 0.0 collective-permute-done.9.refs_3_
  28.7 1.7 %shard_map.88.own_ref = bf16[16,160,128]{2,1,0:T(8,128)(2,1)S(1)} custom-call(bf16[2,2,160,128]{3,2,1,0:T(8,128)(2,1)S(1)} %shard_map.85.refs_0_, bf16[2,2,160,128]{3,2,1,0:T(8,128)(2,1)S(1)} %collective-permute-done.7.refs_1_, bf16[2,2,160,128]{3,2,1,0:T(8,128)(2,1)S(1)} %collective-permute-done.8.refs_2_, ...), custom_call_target="tpu_custom_call" | custom-call | flops 471859200 | tf_op jit(solution)/shard_map/pallas_call | solution.py:443
  30.3 0.2 collective-permute-start.17
  30.5 0.4 collective-permute-start.6
  30.9 1.6 %collective-permute-done.6 = f32[8,128]{1,0:T(8,128)S(1)} collective-permute-done((f32[8,128]{1,0:T(8,128)S(1)}, f32[8,128]{1,0:T(8,128)S(1)}, u32[]{:S(2)}, u32[]{:S(2)}) %collective-permute-start.6) | collective-permute-done | bytes 4128 | tf_op jit(solution)/shard_map/ppermute | solution.py:475
  32.5 1.8 %collective-permute-start.14 = (f32[2,8,128]{2,1,0:T(8,128)S(1)}, f32[2,8,128]{2,1,0:T(8,128)S(1)}, u32[]{:S(2)}, u32[]{:S(2)}) collective-permute-start(f32[2,8,128]{2,1,0:T(8,128)S(1)} %pad_maximum_fusion.refs_0_), channel_id=1, source_target_pairs={{0,24},{4,28},{8,16},{12,20},{16,8},{20,12},{24,0},{28,4},{1,25},{... | collective-permute-start | bytes 24584 | tf_op jit(solution)/shard_map/ppermute | solution.py:471
  34.3 0.5 %collective-permute-start.15 = (f32[2,8,128]{2,1,0:T(8,128)S(1)}, f32[2,8,128]{2,1,0:T(8,128)S(1)}, u32[]{:S(2)}, u32[]{:S(2)}) collective-permute-start(f32[2,8,128]{2,1,0:T(8,128)S(1)} %pad_maximum_fusion.refs_0_), channel_id=1, source_target_pairs={{0,8},{4,12},{8,0},{12,4},{16,24},{20,28},{24,16},{28,20},{1,9},{5... | collective-permute-start | bytes 24584 | tf_op jit(solution)/shard_map/ppermute | solution.py:471
  34.8 1.2 %collective-permute-start.16 = (f32[2,8,128]{2,1,0:T(8,128)S(1)}, f32[2,8,128]{2,1,0:T(8,128)S(1)}, u32[]{:S(2)}, u32[]{:S(2)}) collective-permute-start(f32[2,8,128]{2,1,0:T(8,128)S(1)} %pad_maximum_fusion.refs_0_), channel_id=1, source_target_pairs={{0,16},{4,20},{8,24},{12,28},{16,0},{20,4},{24,8},{28,12},{1,17},{... | collective-permute-start | bytes 24584 | tf_op jit(solution)/shard_map/ppermute | solution.py:471
  36.0 0.0 collective-permute-done.17.other_ref
  36.0 1.8 %shard_map.90 = (f32[225,128]{1,0:T(8,128)S(1)}, bf16[225,128]{1,0:T(8,128)(2,1)S(1)}, bf16[225,128]{1,0:T(8,128)(2,1)S(1)}, bf16[225,128]{1,0:T(8,128)(2,1)S(1)}, bf16[4,320,128]{2,1,0:T(8,128)(2,1)S(1)}) custom-call(bf16[16,160,128]{2,1,0:T(8,128)(2,1)S(1)} %shard_map.88.own_ref, bf16[16,160,128]{2,1,0:T(8,128)(2,1)S(1)} %collective-permute-done.17.other_ref, ...), custom_call_target="tpu_custom_call" | custom-call | flops 943718400 | tf_op jit(solution)/shard_map/pallas_call | solution.py:443
  37.8 3.7 %collective-permute-start.18 = (bf16[225,128]{1,0:T(8,128)(2,1)S(1)}, bf16[225,128]{1,0:T(8,128)(2,1)S(1)}, u32[]{:S(2)}, u32[]{:S(2)}) collective-permute-start(bf16[225,128]{1,0:T(8,128)(2,1)S(1)} %get-tuple-element.58), channel_id=1, source_target_pairs={{0,3},{1,2},{2,1},{3,0},{4,7},{5,6},{6,5},{7,4},{8,11},{9,10},{10,... | collective-permute-start | bytes 172808 | tf_op jit(solution)/shard_map/ppermute | solution.py:563
  41.4 0.0 collective-permute-start.19
  41.4 0.0 collective-permute-done.14.refs_1_
  41.4 0.8 %collective-permute-start.20 = (bf16[225,128]{1,0:T(8,128)(2,1)S(1)}, bf16[225,128]{1,0:T(8,128)(2,1)S(1)}, u32[]{:S(2)}, u32[]{:S(2)}) collective-permute-start(bf16[225,128]{1,0:T(8,128)(2,1)S(1)} %get-tuple-element.60), channel_id=1, source_target_pairs={{0,1},{1,0},{2,3},{3,2},{4,5},{5,4},{6,7},{7,6},{8,9},{9,8},{10,11... | collective-permute-start | bytes 172808 | tf_op jit(solution)/shard_map/ppermute | solution.py:563
  42.2 0.0 collective-permute-done.15.refs_2_
  42.2 0.0 collective-permute-done.16.refs_3_
  42.2 1.5 %shard_map.89 = bf16[2,320,128]{2,1,0:T(8,128)(2,1)} custom-call(f32[2,8,128]{2,1,0:T(8,128)S(1)} %pad_maximum_fusion.refs_0_, f32[2,8,128]{2,1,0:T(8,128)S(1)} %collective-permute-done.14.refs_1_, f32[2,8,128]{2,1,0:T(8,128)S(1)} %collective-permute-done.15.refs_2_, f32[2,8,128]{2,1,0:T(8,128)S(1)} %collective-permute-done.16.refs_3_, ...), custom_call_target="tpu_custom_call" | custom-call | flops 117964800 | tf_op jit(solution)/shard_map/pallas_call | solution.py:443
  43.7 1.7 %shard_map.91 = bf16[2,320,128]{2,1,0:T(8,128)(2,1)} custom-call(bf16[4,320,128]{2,1,0:T(8,128)(2,1)S(1)} %get-tuple-element.56.gz_ref, bf16[3,320,960]{2,1,0:T(8,128)(2,1)S(1)} %weights.1.w_ref.refs_8_), custom_call_target="tpu_custom_call" | custom-call | flops 471859200 | tf_op jit(solution)/shard_map/pallas_call | solution.py:443
  45.5 0.0 collective-permute-done.18
  45.5 1.1 %collective-permute-done.19 = bf16[225,128]{1,0:T(8,128)(2,1)S(1)} collective-permute-done((bf16[225,128]{1,0:T(8,128)(2,1)S(1)}, bf16[225,128]{1,0:T(8,128)(2,1)S(1)}, u32[]{:S(2)}, u32[]{:S(2)}) %collective-permute-start.19) | collective-permute-done | bytes 57632 | tf_op jit(solution)/shard_map/ppermute | solution.py:563
  46.5 0.0 collective-permute-done.20
  46.6 0.7 %add_bitcast_fusion = f32[28800]{0:T(1024)} fusion(bf16[225,128]{1,0:T(8,128)(2,1)S(1)} %collective-permute-done.20, bf16[225,128]{1,0:T(8,128)(2,1)S(1)} %collective-permute-done.19, f32[225,128]{1,0:T(8,128)S(1)} %get-tuple-element.57, bf16[225,128]{1,0:T(8,128)(2,1)S(1)} %collective-permute-done.18), kind=kLoop, calls=%fused_computation | loop fusion | flops 172800 | bytes 403200 | tf_op jit(solution)/shard_map/reshape | solution.py:579
  (2 shorter events, 0.0 us)
Async XLA Ops:
  0.6 9.7 %copy-start.1 = (bf16[1,2,320,128]{3,2,1,0:T(8,128)(2,1)S(1)}, bf16[1,2,320,128]{3,2,1,0:T(8,128)(2,1)}, u32[]{:S(2)}) copy-start(bf16[1,2,320,128]{3,2,1,0:T(8,128)(2,1)} %param.8) | copy-start | bytes 491524
  0.6 6.6 %collective-permute-start.4 = (bf16[2,320,128]{2,1,0:T(8,128)(2,1)}, bf16[2,320,128]{2,1,0:T(8,128)(2,1)S(1)}, u32[]{:S(2)}, u32[]{:S(2)}) collective-permute-start(bf16[2,320,128]{2,1,0:T(8,128)(2,1)} %bitcast.12), channel_id=1, source_target_pairs={{0,4},{4,0},{8,12},{12,8},{16,20},{20,16},{24,28},{28,24},{1,5},{5... | collective-permute-start | bytes 491528 | tf_op jit(solution)/shard_map/ppermute | solution.py:475
  1.2 9.2 %collective-permute-start = (bf16[2,320,128]{2,1,0:T(8,128)(2,1)}, bf16[2,320,128]{2,1,0:T(8,128)(2,1)S(1)}, u32[]{:S(2)}, u32[]{:S(2)}) collective-permute-start(bf16[2,320,128]{2,1,0:T(8,128)(2,1)} %bitcast.15), channel_id=1, source_target_pairs={{0,8},{4,12},{8,0},{12,4},{16,24},{20,28},{24,16},{28,20},{1,9},{5... | collective-permute-start | bytes 491528 | tf_op jit(solution)/shard_map/ppermute | solution.py:471
  3.8 10.9 %collective-permute-start.1 = (bf16[2,320,128]{2,1,0:T(8,128)(2,1)}, bf16[2,320,128]{2,1,0:T(8,128)(2,1)S(1)}, u32[]{:S(2)}, u32[]{:S(2)}) collective-permute-start(bf16[2,320,128]{2,1,0:T(8,128)(2,1)} %bitcast.16), channel_id=1, source_target_pairs={{0,16},{4,20},{8,24},{12,28},{16,0},{20,4},{24,8},{28,12},{1,17},{... | collective-permute-start | bytes 491528 | tf_op jit(solution)/shard_map/ppermute | solution.py:471
  5.3 9.4 %collective-permute-start.2 = (bf16[2,320,128]{2,1,0:T(8,128)(2,1)}, bf16[2,320,128]{2,1,0:T(8,128)(2,1)S(1)}, u32[]{:S(2)}, u32[]{:S(2)}) collective-permute-start(bf16[2,320,128]{2,1,0:T(8,128)(2,1)} %bitcast.17), channel_id=1, source_target_pairs={{0,24},{4,28},{8,16},{12,20},{16,8},{20,12},{24,0},{28,4},{1,25},{... | collective-permute-start | bytes 491528 | tf_op jit(solution)/shard_map/ppermute | solution.py:471
  5.3 9.3 %copy-start.3 = (f32[320]{0:T(512)S(1)}, f32[320]{0:T(512)}, u32[]{:S(2)}) copy-start(f32[320]{0:T(512)} %param.10) | copy-start | bytes 3844
  5.3 9.5 %copy-start.4 = (f32[320]{0:T(512)S(1)}, f32[320]{0:T(512)}, u32[]{:S(2)}) copy-start(f32[320]{0:T(512)} %param.11) | copy-start | bytes 3844
  5.3 9.6 %copy-start.2 = (bf16[1,2,320,128]{3,2,1,0:T(8,128)(2,1)S(1)}, bf16[1,2,320,128]{3,2,1,0:T(8,128)(2,1)}, u32[]{:S(2)}) copy-start(bf16[1,2,320,128]{3,2,1,0:T(8,128)(2,1)} %param.7) | copy-start | bytes 491524
  5.3 11.8 %copy-start = (bf16[1,2,320,128]{3,2,1,0:T(8,128)(2,1)S(1)}, bf16[1,2,320,128]{3,2,1,0:T(8,128)(2,1)}, u32[]{:S(2)}) copy-start(bf16[1,2,320,128]{3,2,1,0:T(8,128)(2,1)} %param.6) | copy-start | bytes 491524
  5.3 9.3 %collective-permute-start.3 = (bf16[2,320,128]{2,1,0:T(8,128)(2,1)}, bf16[2,320,128]{2,1,0:T(8,128)(2,1)S(1)}, u32[]{:S(2)}, u32[]{:S(2)}) collective-permute-start(bf16[2,320,128]{2,1,0:T(8,128)(2,1)} %bitcast.9), channel_id=1, source_target_pairs={{0,4},{4,8},{8,12},{12,16},{16,20},{20,24},{24,28},{1,5},{5,9},{9,... | collective-permute-start | bytes 491528 | tf_op jit(solution)/shard_map/ppermute | solution.py:479
  7.2 8.7 %collective-permute-start.5 = (bf16[2,320,128]{2,1,0:T(8,128)(2,1)}, bf16[2,320,128]{2,1,0:T(8,128)(2,1)S(1)}, u32[]{:S(2)}, u32[]{:S(2)}) collective-permute-start(bf16[2,320,128]{2,1,0:T(8,128)(2,1)} %bitcast.10), channel_id=1, source_target_pairs={{4,0},{8,4},{12,8},{16,12},{20,16},{24,20},{28,24},{5,1},{9,5},{13... | collective-permute-start | bytes 491528 | tf_op jit(solution)/shard_map/ppermute | solution.py:480
  14.9 3.4 %collective-permute-start.10 = (bf16[2,320,128]{2,1,0:T(8,128)(2,1)S(1)}, bf16[2,320,128]{2,1,0:T(8,128)(2,1)S(1)}, u32[]{:S(2)}, u32[]{:S(2)}) collective-permute-start(bf16[2,320,128]{2,1,0:T(8,128)(2,1)S(1)} %bitcast.18), channel_id=1, source_target_pairs={{0,4},{4,0},{8,12},{12,8},{16,20},{20,16},{24,28},{28,24},{1,5},{5... | collective-permute-start | bytes 491528 | tf_op jit(solution)/shard_map/ppermute | solution.py:475
  14.9 4.9 %collective-permute-start.11 = (bf16[2,320,128]{2,1,0:T(8,128)(2,1)S(1)}, bf16[2,320,128]{2,1,0:T(8,128)(2,1)S(1)}, u32[]{:S(2)}, u32[]{:S(2)}) collective-permute-start(bf16[2,320,128]{2,1,0:T(8,128)(2,1)S(1)} %collective-permute-done.refs_2_), channel_id=1, source_target_pairs={{0,4},{4,0},{8,12},{12,8},{16,20},{20,16},{24,28},{28,24},{1,5},{5... | collective-permute-start | bytes 491528 | tf_op jit(solution)/shard_map/ppermute | solution.py:475
  15.4 5.7 %collective-permute-start.12 = (bf16[2,320,128]{2,1,0:T(8,128)(2,1)S(1)}, bf16[2,320,128]{2,1,0:T(8,128)(2,1)S(1)}, u32[]{:S(2)}, u32[]{:S(2)}) collective-permute-start(bf16[2,320,128]{2,1,0:T(8,128)(2,1)S(1)} %collective-permute-done.1.refs_4_), channel_id=1, source_target_pairs={{0,4},{4,0},{8,12},{12,8},{16,20},{20,16},{24,28},{28,24},{1,5},{5... | collective-permute-start | bytes 491528 | tf_op jit(solution)/shard_map/ppermute | solution.py:475
  15.5 5.6 %collective-permute-start.13 = (bf16[2,320,128]{2,1,0:T(8,128)(2,1)S(1)}, bf16[2,320,128]{2,1,0:T(8,128)(2,1)S(1)}, u32[]{:S(2)}, u32[]{:S(2)}) collective-permute-start(bf16[2,320,128]{2,1,0:T(8,128)(2,1)S(1)} %collective-permute-done.2.refs_6_), channel_id=1, source_target_pairs={{0,4},{4,0},{8,12},{12,8},{16,20},{20,16},{24,28},{28,24},{1,5},{5... | collective-permute-start | bytes 491528 | tf_op jit(solution)/shard_map/ppermute | solution.py:475
  16.0 9.7 %collective-permute-start.7 = (bf16[2,2,160,128]{3,2,1,0:T(8,128)(2,1)S(1)}, bf16[2,2,160,128]{3,2,1,0:T(8,128)(2,1)S(1)}, u32[]{:S(2)}, u32[]{:S(2)}) collective-permute-start(bf16[2,2,160,128]{3,2,1,0:T(8,128)(2,1)S(1)} %shard_map.85.refs_0_), channel_id=1, source_target_pairs={{0,8},{4,12},{8,0},{12,4},{16,24},{20,28},{24,16},{28,20},{1,9},{5... | collective-permute-start | bytes 491528 | tf_op jit(solution)/shard_map/ppermute | solution.py:471
  18.3 10.4 %collective-permute-start.8 = (bf16[2,2,160,128]{3,2,1,0:T(8,128)(2,1)S(1)}, bf16[2,2,160,128]{3,2,1,0:T(8,128)(2,1)S(1)}, u32[]{:S(2)}, u32[]{:S(2)}) collective-permute-start(bf16[2,2,160,128]{3,2,1,0:T(8,128)(2,1)S(1)} %shard_map.85.refs_0_), channel_id=1, source_target_pairs={{0,16},{4,20},{8,24},{12,28},{16,0},{20,4},{24,8},{28,12},{1,17},{... | collective-permute-start | bytes 491528 | tf_op jit(solution)/shard_map/ppermute | solution.py:471
  19.8 8.8 %collective-permute-start.9 = (bf16[2,2,160,128]{3,2,1,0:T(8,128)(2,1)S(1)}, bf16[2,2,160,128]{3,2,1,0:T(8,128)(2,1)S(1)}, u32[]{:S(2)}, u32[]{:S(2)}) collective-permute-start(bf16[2,2,160,128]{3,2,1,0:T(8,128)(2,1)S(1)} %shard_map.85.refs_0_), channel_id=1, source_target_pairs={{0,24},{4,28},{8,16},{12,20},{16,8},{20,12},{24,0},{28,4},{1,25},{... | collective-permute-start | bytes 491528 | tf_op jit(solution)/shard_map/ppermute | solution.py:471
  30.3 5.7 %collective-permute-start.17 = (bf16[16,160,128]{2,1,0:T(8,128)(2,1)S(1)}, bf16[16,160,128]{2,1,0:T(8,128)(2,1)S(1)}, u32[]{:S(2)}, u32[]{:S(2)}) collective-permute-start(bf16[16,160,128]{2,1,0:T(8,128)(2,1)S(1)} %shard_map.88.own_ref), channel_id=1, source_target_pairs={{0,4},{4,0},{8,12},{12,8},{16,20},{20,16},{24,28},{28,24},{1,5},{5... | collective-permute-start | bytes 1966088 | tf_op jit(solution)/shard_map/ppermute | solution.py:475
  30.5 2.0 %collective-permute-start.6 = (f32[8,128]{1,0:T(8,128)S(1)}, f32[8,128]{1,0:T(8,128)S(1)}, u32[]{:S(2)}, u32[]{:S(2)}) collective-permute-start(f32[8,128]{1,0:T(8,128)S(1)} %get-tuple-element.34), channel_id=1, source_target_pairs={{0,4},{4,0},{8,12},{12,8},{16,20},{20,16},{24,28},{28,24},{1,5},{5... | collective-permute-start | bytes 12296 | tf_op jit(solution)/shard_map/ppermute | solution.py:475
  32.5 8.9 %collective-permute-start.14 = (f32[2,8,128]{2,1,0:T(8,128)S(1)}, f32[2,8,128]{2,1,0:T(8,128)S(1)}, u32[]{:S(2)}, u32[]{:S(2)}) collective-permute-start(f32[2,8,128]{2,1,0:T(8,128)S(1)} %pad_maximum_fusion.refs_0_), channel_id=1, source_target_pairs={{0,24},{4,28},{8,16},{12,20},{16,8},{20,12},{24,0},{28,4},{1,25},{... | collective-permute-start | bytes 24584 | tf_op jit(solution)/shard_map/ppermute | solution.py:471
  34.3 7.9 %collective-permute-start.15 = (f32[2,8,128]{2,1,0:T(8,128)S(1)}, f32[2,8,128]{2,1,0:T(8,128)S(1)}, u32[]{:S(2)}, u32[]{:S(2)}) collective-permute-start(f32[2,8,128]{2,1,0:T(8,128)S(1)} %pad_maximum_fusion.refs_0_), channel_id=1, source_target_pairs={{0,8},{4,12},{8,0},{12,4},{16,24},{20,28},{24,16},{28,20},{1,9},{5... | collective-permute-start | bytes 24584 | tf_op jit(solution)/shard_map/ppermute | solution.py:471
  34.8 7.4 %collective-permute-start.16 = (f32[2,8,128]{2,1,0:T(8,128)S(1)}, f32[2,8,128]{2,1,0:T(8,128)S(1)}, u32[]{:S(2)}, u32[]{:S(2)}) collective-permute-start(f32[2,8,128]{2,1,0:T(8,128)S(1)} %pad_maximum_fusion.refs_0_), channel_id=1, source_target_pairs={{0,16},{4,20},{8,24},{12,28},{16,0},{20,4},{24,8},{28,12},{1,17},{... | collective-permute-start | bytes 24584 | tf_op jit(solution)/shard_map/ppermute | solution.py:471
  37.8 7.7 %collective-permute-start.18 = (bf16[225,128]{1,0:T(8,128)(2,1)S(1)}, bf16[225,128]{1,0:T(8,128)(2,1)S(1)}, u32[]{:S(2)}, u32[]{:S(2)}) collective-permute-start(bf16[225,128]{1,0:T(8,128)(2,1)S(1)} %get-tuple-element.58), channel_id=1, source_target_pairs={{0,3},{1,2},{2,1},{3,0},{4,7},{5,6},{6,5},{7,4},{8,11},{9,10},{10,... | collective-permute-start | bytes 172808 | tf_op jit(solution)/shard_map/ppermute | solution.py:563
  41.4 5.1 %collective-permute-start.19 = (bf16[225,128]{1,0:T(8,128)(2,1)S(1)}, bf16[225,128]{1,0:T(8,128)(2,1)S(1)}, u32[]{:S(2)}, u32[]{:S(2)}) collective-permute-start(bf16[225,128]{1,0:T(8,128)(2,1)S(1)} %get-tuple-element.59), channel_id=1, source_target_pairs={{0,2},{1,3},{2,0},{3,1},{4,6},{5,7},{6,4},{7,5},{8,10},{9,11},{10,... | collective-permute-start | bytes 172808 | tf_op jit(solution)/shard_map/ppermute | solution.py:563
  41.4 5.1 %collective-permute-start.20 = (bf16[225,128]{1,0:T(8,128)(2,1)S(1)}, bf16[225,128]{1,0:T(8,128)(2,1)S(1)}, u32[]{:S(2)}, u32[]{:S(2)}) collective-permute-start(bf16[225,128]{1,0:T(8,128)(2,1)S(1)} %get-tuple-element.60), channel_id=1, source_target_pairs={{0,1},{1,0},{2,3},{3,2},{4,5},{5,4},{6,7},{7,6},{8,9},{9,8},{10,11... | collective-permute-start | bytes 172808 | tf_op jit(solution)/shard_map/ppermute | solution.py:563

commit v2 on v1

--- a/solution.py
+++ b/solution.py
@@ -180,15 +180,11 @@
     return 1.0 / (1.0 + jnp.exp(-value))
 
 
-def weights_kernel(w_ref, flat_ref, held, sems):
+def weights_kernel(w_ref, flat_ref):
     chans = flat_ref.shape[1]
-    copies = [pltpu.make_async_copy(w_ref.at[a], held.at[a], sems.at[a]) for a in range(3)]
-    for copy in copies:
-        copy.start()
     for a in range(3):
-        copies[a].wait()
         for b in range(3):
-            flat_ref[a, :, b * chans : (b + 1) * chans] = held[a, b]
+            flat_ref[a, :, b * chans : (b + 1) * chans] = w_ref[a, b]
 
 
 def halves_kernel(own_ref, near_ref, out_ref):
@@ -200,8 +196,12 @@
         out_ref[1, r] = near_ref[r, mine]
 
 
-def next_conv_kernel(top_ref, x_ref, bottom_ref, w_ref, z_ref, stat_ref, *, rows):
-    cells = [top_ref[rows - 1]] + [x_ref[r] for r in range(rows)] + [bottom_ref[0]]
+def next_conv_kernel(edge_ref, near_ref, x_ref, w_ref, z_ref, stat_ref, *, rows):
+    even = (lax.axis_index("height") & 1) == 0
+    side = edge_ref[...].astype(F32)
+    top = jnp.where(even, side, near_ref[rows - 1].astype(F32)).astype(BF16)
+    bottom = jnp.where(even, near_ref[0].astype(F32), side).astype(BF16)
+    cells = [top] + [x_ref[r] for r in range(rows)] + [bottom]
     chans, width = cells[0].shape
     sides = [[moved_bf16(cell, 1) for cell in cells], cells, [moved_bf16(cell, -1) for cell in cells]]
     stacks = [jnp.concatenate([side[r] for side in sides], axis=0) for r in range(rows + 2)]
@@ -475,34 +475,28 @@
         return lax.ppermute(own, "height", pairs(blocks, 1))
 
     x_far = far(x_cur[0])
-    ends = blocks - 1
-    top = lax.ppermute(x_next, "height", [(i, i + 1) for i in range(ends)])
-    bottom = lax.ppermute(x_next, "height", [(i + 1, i) for i in range(ends)])
+    even = (lax.axis_index("height") & 1) == 0
+    edge = lax.dynamic_index_in_dim(x_next, jnp.where(even, 0, rows - 1), 0, keepdims=False)
+    next_near = near(x_next)
+    swaps = [(i, i + 1) for i in range(1, blocks - 1, 2)]
+    edge = lax.ppermute(edge, "height", swaps + [(j, i) for i, j in swaps])
     g_near = near(grad_out)
-    g_pair = call(halves_kernel, shape((2, rows, half, width), BF16), (grad_out, g_near))
+    g_pair = call(
+        halves_kernel, shape((2, rows, half, width), BF16), (grad_out, g_near), flops=image * flops
+    )
     g_far = far(g_pair)
     gain = jnp.broadcast_to(gamma[:, None], (chans, width))
     shift = jnp.broadcast_to(beta[:, None], (chans, width))
-    w_flat = pl.pallas_call(
-        weights_kernel,
-        out_shape=shape((3, chans, 3 * chans), BF16),
-        in_specs=[pl.BlockSpec(memory_space=pltpu.HBM)],
-        out_specs=vmem(1)[0],
-        scratch_shapes=[pltpu.VMEM((3, 3, chans, chans), BF16), pltpu.SemaphoreType.DMA((3,))],
-        compiler_params=params(),
-        name="weights",
-    )(pltpu.with_memory_space_constraint(kernel, pltpu.HBM))
-
-    x_far, top, w_flat, gain, shift, _ = lax.optimization_barrier(
-        (x_far, top, w_flat, gain, shift, g_pair)
-    )
+    w_flat = call(weights_kernel, shape((3, chans, 3 * chans), BF16), (kernel,))
+
+    x_far, w_flat, gain, shift, _ = lax.optimization_barrier((x_far, w_flat, gain, shift, g_pair))
     x_all = []
     for k in range(0, blocks, 2):
         x_all += [x_far[k], near(x_far[k])]
     z_next, stat = call(
         next_conv_kernel,
         (shape((rows, chans, width), F32), shape((8 * -(-2 * len(lane_tiles(chans)) // 8), LANES), F32)),
-        (top, x_next, bottom, w_flat),
+        (edge, next_near, x_next, w_flat),
         flops=rows * flops,
         rows=rows,
     )

time: 47.4 us -> 46.7 us (0.985)
  starting transfers between devices: 21.4 us -> 18.9 us
  local copies, waits for them, and re-layouts: 0.21 us -> 2.37 us
  Pallas kernels: 14.2 us -> 12.8 us
  waiting for transfers between devices: 9.96 us -> 11 us
    ppermute x2 -> x1, starting transfers between devices: 3.2 us -> 0.8 us  [gathered(): edge = lax.ppermute(edge, 'height', swaps + [(j, i) for i, j in swaps])]
    unnamed x10 -> x12, local copies, waits for them, and re-layouts: 0.02 us -> 2.17 us
    pallas_call x1 -> x0, Pallas kernels: 1.78 us -> none  [gathered(): pl.pallas_call(weights_kernel, out_shape=shape((3, chans, 3 * chans), BF1...]
    ppermute x9, waiting for transfers between devices: 7.25 us -> 8.3 us  [far(): held[k] = lax.ppermute(own, 'height', pairs(blocks, k))]
    pallas_call x7 -> x8, Pallas kernels: 12.4 us -> 12.8 us  [call(): pl.pallas_call(functools.partial(kernel, **static), out_shape=out_shape,...]
    ppermute x7 -> x8, starting transfers between devices: 2.21 us -> 2.21 us  [near(): return lax.ppermute(own, 'height', pairs(blocks, 1))]
    ppermute x7 -> x8, waiting for transfers between devices: 1.61 us -> 1.61 us  [near(): return lax.ppermute(own, 'height', pairs(blocks, 1))]
  transfers between devices with their start and end apart: 21 -> 21, of which waited for: 4 -> 5; matrix products, arithmetic and copies ran while one was open for 0% -> 0% of each run, Pallas kernels for 26% -> 24%
where the time goes in v2:
time: 46.7 us; the launch traced here: 46.5 us
  starting transfers between devices  18.9 us (40%)
  Pallas kernels  12.8 us (27%)
  waiting for transfers between devices  11 us (24%)
  local copies, waits for them, and re-layouts  2.37 us (5%)
  between operations  0.8 us (2%)
  other arithmetic  0.68 us (1%)
    pallas_call x8, Pallas kernels, call(): pl.pallas_call(functools.partial(kernel, **static), out_shape=out_shape,...  12.8 us
    ppermute x9, starting transfers between devices, far(): held[k] = lax.ppermute(own, 'height', pairs(blocks, k))  11.4 us
    ppermute x9, waiting for transfers between devices, far(): held[k] = lax.ppermute(own, 'height', pairs(blocks, k))  8.3 us
    ppermute x3, starting transfers between devices, gathered(): lax.ppermute(results[s], 'dp', pairs(groups_dp, s)).astype(F32)  4.45 us
    ppermute x8, starting transfers between devices, near(): return lax.ppermute(own, 'height', pairs(blocks, 1))  2.21 us
    unnamed x12, local copies, waits for them, and re-layouts  2.17 us
    ppermute x8, waiting for transfers between devices, near(): return lax.ppermute(own, 'height', pairs(blocks, 1))  1.61 us
    ppermute x3, waiting for transfers between devices, gathered(): lax.ppermute(results[s], 'dp', pairs(groups_dp, s)).astype(F32)  1.09 us
  transfers between devices with their start and end apart: 21, of which 5 were waited for; matrix products, arithmetic and copies ran while one was open for 0% of the time, Pallas kernels for 24%

profile of v2, /device:TPU:0, one launch (start us, length us, event | category | flops | bytes accessed | tf_op | source)
XLA Modules:
  0.0 46.5 jit_solution(7473789494681379178)
XLA Ops:
  0.6 0.6 %collective-permute-start.5 = (bf16[2,320,128]{2,1,0:T(8,128)(2,1)}, bf16[2,320,128]{2,1,0:T(8,128)(2,1)S(1)}, u32[]{:S(2)}, u32[]{:S(2)}) collective-permute-start(bf16[2,320,128]{2,1,0:T(8,128)(2,1)} %bitcast.14), channel_id=1, source_target_pairs={{0,4},{4,0},{8,12},{12,8},{16,20},{20,16},{24,28},{28,24},{1,5},{5... | collective-permute-start | bytes 491528 | tf_op jit(solution)/shard_map/ppermute | solution.py:475
  1.2 2.6 %collective-permute-start.2 = (bf16[2,320,128]{2,1,0:T(8,128)(2,1)}, bf16[2,320,128]{2,1,0:T(8,128)(2,1)S(1)}, u32[]{:S(2)}, u32[]{:S(2)}) collective-permute-start(bf16[2,320,128]{2,1,0:T(8,128)(2,1)} %bitcast.16), channel_id=1, source_target_pairs={{0,8},{4,12},{8,0},{12,4},{16,24},{20,28},{24,16},{28,20},{1,9},{5... | collective-permute-start | bytes 491528 | tf_op jit(solution)/shard_map/ppermute | solution.py:471
  3.7 1.5 %collective-permute-start.3 = (bf16[2,320,128]{2,1,0:T(8,128)(2,1)}, bf16[2,320,128]{2,1,0:T(8,128)(2,1)S(1)}, u32[]{:S(2)}, u32[]{:S(2)}) collective-permute-start(bf16[2,320,128]{2,1,0:T(8,128)(2,1)} %bitcast.17), channel_id=1, source_target_pairs={{0,16},{4,20},{8,24},{12,28},{16,0},{20,4},{24,8},{28,12},{1,17},{... | collective-permute-start | bytes 491528 | tf_op jit(solution)/shard_map/ppermute | solution.py:471
  5.3 0.0 collective-permute-start.4
  5.3 0.0 collective-permute-start.1
  5.3 0.0 copy-start
  5.3 1.6 %copy-done = bf16[3,3,320,320]{3,2,1,0:T(8,128)(2,1)S(1)} copy-done((bf16[3,3,320,320]{3,2,1,0:T(8,128)(2,1)S(1)}, bf16[3,3,320,320]{3,2,1,0:T(8,128)(2,1)}, u32[]{:S(2)}) %copy-start) | copy-done | bytes 1843224
  6.9 0.0 copy-start.1
  6.9 0.0 copy-start.2
  6.9 0.4 shard_map.85.w_ref.refs_8_
  7.3 0.5 %copy-done.1 = bf16[1,2,320,128]{3,2,1,0:T(8,128)(2,1)S(1)} copy-done((bf16[1,2,320,128]{3,2,1,0:T(8,128)(2,1)S(1)}, bf16[1,2,320,128]{3,2,1,0:T(8,128)(2,1)}, u32[]{:S(2)}) %copy-start.1) | copy-done | bytes 163864
  7.8 0.0 copy-start.4
  7.8 0.0 copy-start.5
  7.9 0.0 copy-start.3
  7.9 0.0 collective-permute-done.5.near_ref
  7.9 0.8 %collective-permute-start = (bf16[320,128]{1,0:T(8,128)(2,1)S(1)}, bf16[320,128]{1,0:T(8,128)(2,1)S(1)}, u32[]{:S(2)}, u32[]{:S(2)}) collective-permute-start(bf16[320,128]{1,0:T(8,128)(2,1)S(1)} %dynamic-slice_bitcast_fusion), channel_id=1, source_target_pairs={{4,8},{12,16},{20,24},{8,4},{16,12},{24,20},{5,9},{13,17},{21,25},... | collective-permute-start | bytes 245768 | tf_op jit(solution)/shard_map/ppermute | solution.py:482
  8.7 0.0 copy-done.2
  8.7 0.3 collective-permute-done.2.refs_2_
  9.0 4.7 %collective-permute-done.3.refs_4_ = bf16[2,320,128]{2,1,0:T(8,128)(2,1)S(1)} collective-permute-done((bf16[2,320,128]{2,1,0:T(8,128)(2,1)}, bf16[2,320,128]{2,1,0:T(8,128)(2,1)S(1)}, u32[]{:S(2)}, u32[]{:S(2)}) %collective-permute-start.3) | collective-permute-done | bytes 163872 | tf_op jit(solution)/shard_map/ppermute | solution.py:471
  13.7 0.0 collective-permute-done.4.refs_6_
  13.7 0.0 copy-done.4
  13.7 0.1 broadcast_in_dim.8.refs_6_.refs_5_
  13.8 0.0 copy-done.5
  13.8 0.1 broadcast_in_dim.9.refs_7_.refs_6_
  13.9 0.0 copy-done.3
  14.0 0.1 collective-permute-start.10
  14.0 0.5 %collective-permute-start.11 = (bf16[2,320,128]{2,1,0:T(8,128)(2,1)S(1)}, bf16[2,320,128]{2,1,0:T(8,128)(2,1)S(1)}, u32[]{:S(2)}, u32[]{:S(2)}) collective-permute-start(bf16[2,320,128]{2,1,0:T(8,128)(2,1)S(1)} %collective-permute-done.2.refs_2_), channel_id=1, source_target_pairs={{0,4},{4,0},{8,12},{12,8},{16,20},{20,16},{24,28},{28,24},{1,5},{5... | collective-permute-start | bytes 491528 | tf_op jit(solution)/shard_map/ppermute | solution.py:475
  14.5 0.1 collective-permute-start.12
  14.6 0.0 collective-permute-done.edge_ref
  14.6 0.4 collective-permute-start.13
  15.0 0.0 collective-permute-done.1.near_ref
  15.0 2.3 %collective-permute-start.7 = (bf16[2,2,160,128]{3,2,1,0:T(8,128)(2,1)S(1)}, bf16[2,2,160,128]{3,2,1,0:T(8,128)(2,1)S(1)}, u32[]{:S(2)}, u32[]{:S(2)}) collective-permute-start(bf16[2,2,160,128]{3,2,1,0:T(8,128)(2,1)S(1)} %shard_map.86.refs_0_), channel_id=1, source_target_pairs={{0,8},{4,12},{8,0},{12,4},{16,24},{20,28},{24,16},{28,20},{1,9},{5... | collective-permute-start | bytes 491528 | tf_op jit(solution)/shard_map/ppermute | solution.py:471
  17.4 1.2 %shard_map.87 = (f32[2,320,128]{2,1,0:T(8,128)S(1)}, f32[8,128]{1,0:T(8,128)S(1)}) custom-call(bf16[320,128]{1,0:T(8,128)(2,1)S(1)} %collective-permute-done.edge_ref, bf16[2,320,128]{2,1,0:T(8,128)(2,1)S(1)} %collective-permute-done.1.near_ref, bf16[2,320,128]{2,1,0:T(8,128)(2,1)S(1)} %bitcast.12, bf16[3,320,960]{2,1,0:T(8,128)(2,1)S(1)} %shard_map.85.w_ref.refs_8_), custom_call_target="tpu_custom_call" | custom-call | flops 471859200 | tf_op jit(solution)/shard_map/pallas_call | solution.py:443
  18.5 0.0 collective-permute-done.10.refs_1_
  18.5 0.2 collective-permute-start.8
  18.7 0.0 collective-permute-done.11.refs_3_
  18.7 1.4 %collective-permute-start.9 = (bf16[2,2,160,128]{3,2,1,0:T(8,128)(2,1)S(1)}, bf16[2,2,160,128]{3,2,1,0:T(8,128)(2,1)S(1)}, u32[]{:S(2)}, u32[]{:S(2)}) collective-permute-start(bf16[2,2,160,128]{3,2,1,0:T(8,128)(2,1)S(1)} %shard_map.86.refs_0_), channel_id=1, source_target_pairs={{0,24},{4,28},{8,16},{12,20},{16,8},{20,12},{24,0},{28,4},{1,25},{... | collective-permute-start | bytes 491528 | tf_op jit(solution)/shard_map/ppermute | solution.py:471
  20.1 0.0 collective-permute-done.12.refs_5_
  20.1 0.0 collective-permute-done.13.refs_7_
  20.1 4.6 %shard_map.88 = (bf16[18,960,128]{2,1,0:T(8,128)(2,1)S(1)}, f32[16,160,128]{2,1,0:T(8,128)S(1)}, f32[2,160,128]{2,1,0:T(8,128)S(1)}) custom-call(bf16[2,320,128]{2,1,0:T(8,128)(2,1)S(1)} %bitcast.20, bf16[2,320,128]{2,1,0:T(8,128)(2,1)S(1)} %collective-permute-done.10.refs_1_, bf16[2,320,128]{2,1,0:T(8,128)(2,1)S(1)} %collective-permute-done.2.refs_2_, ...), custom_call_target="tpu_custom_call" | custom-call | flops 1887436800 | tf_op jit(solution)/shard_map/pallas_call | solution.py:443
  24.6 0.0 collective-permute-done.7.refs_1_
  24.6 3.3 %collective-permute-done.8.refs_2_ = bf16[2,2,160,128]{3,2,1,0:T(8,128)(2,1)S(1)} collective-permute-done((bf16[2,2,160,128]{3,2,1,0:T(8,128)(2,1)S(1)}, bf16[2,2,160,128]{3,2,1,0:T(8,128)(2,1)S(1)}, u32[]{:S(2)}, u32[]{:S(2)}) %collective-permute-start.8) | collective-permute-done | bytes 163872 | tf_op jit(solution)/shard_map/ppermute | solution.py:471
  27.9 0.0 collective-permute-done.9.refs_3_
  27.9 1.7 %shard_map.89.own_ref = bf16[16,160,128]{2,1,0:T(8,128)(2,1)S(1)} custom-call(bf16[2,2,160,128]{3,2,1,0:T(8,128)(2,1)S(1)} %shard_map.86.refs_0_, bf16[2,2,160,128]{3,2,1,0:T(8,128)(2,1)S(1)} %collective-permute-done.7.refs_1_, bf16[2,2,160,128]{3,2,1,0:T(8,128)(2,1)S(1)} %collective-permute-done.8.refs_2_, ...), custom_call_target="tpu_custom_call" | custom-call | flops 471859200 | tf_op jit(solution)/shard_map/pallas_call | solution.py:443
  29.6 0.1 collective-permute-start.17
  29.7 0.5 %collective-permute-start.6 = (f32[8,128]{1,0:T(8,128)S(1)}, f32[8,128]{1,0:T(8,128)S(1)}, u32[]{:S(2)}, u32[]{:S(2)}) collective-permute-start(f32[8,128]{1,0:T(8,128)S(1)} %get-tuple-element.32), channel_id=1, source_target_pairs={{0,4},{4,0},{8,12},{12,8},{16,20},{20,16},{24,28},{28,24},{1,5},{5... | collective-permute-start | bytes 12296 | tf_op jit(solution)/shard_map/ppermute | solution.py:475
  30.2 1.6 %collective-permute-done.6 = f32[8,128]{1,0:T(8,128)S(1)} collective-permute-done((f32[8,128]{1,0:T(8,128)S(1)}, f32[8,128]{1,0:T(8,128)S(1)}, u32[]{:S(2)}, u32[]{:S(2)}) %collective-permute-start.6) | collective-permute-done | bytes 4128 | tf_op jit(solution)/shard_map/ppermute | solution.py:475
  31.8 1.4 %collective-permute-start.14 = (f32[2,8,128]{2,1,0:T(8,128)S(1)}, f32[2,8,128]{2,1,0:T(8,128)S(1)}, u32[]{:S(2)}, u32[]{:S(2)}) collective-permute-start(f32[2,8,128]{2,1,0:T(8,128)S(1)} %pad_maximum_fusion.refs_0_), channel_id=1, source_target_pairs={{0,24},{4,28},{8,16},{12,20},{16,8},{20,12},{24,0},{28,4},{1,25},{... | collective-permute-start | bytes 24584 | tf_op jit(solution)/shard_map/ppermute | solution.py:471
  33.2 0.7 %collective-permute-start.15 = (f32[2,8,128]{2,1,0:T(8,128)S(1)}, f32[2,8,128]{2,1,0:T(8,128)S(1)}, u32[]{:S(2)}, u32[]{:S(2)}) collective-permute-start(f32[2,8,128]{2,1,0:T(8,128)S(1)} %pad_maximum_fusion.refs_0_), channel_id=1, source_target_pairs={{0,8},{4,12},{8,0},{12,4},{16,24},{20,28},{24,16},{28,20},{1,9},{5... | collective-permute-start | bytes 24584 | tf_op jit(solution)/shard_map/ppermute | solution.py:471
  33.9 1.4 %collective-permute-start.16 = (f32[2,8,128]{2,1,0:T(8,128)S(1)}, f32[2,8,128]{2,1,0:T(8,128)S(1)}, u32[]{:S(2)}, u32[]{:S(2)}) collective-permute-start(f32[2,8,128]{2,1,0:T(8,128)S(1)} %pad_maximum_fusion.refs_0_), channel_id=1, source_target_pairs={{0,16},{4,20},{8,24},{12,28},{16,0},{20,4},{24,8},{28,12},{1,17},{... | collective-permute-start | bytes 24584 | tf_op jit(solution)/shard_map/ppermute | solution.py:471
  35.3 0.0 collective-permute-done.17.other_ref
  35.3 1.8 %shard_map.91 = (f32[225,128]{1,0:T(8,128)S(1)}, bf16[225,128]{1,0:T(8,128)(2,1)S(1)}, bf16[225,128]{1,0:T(8,128)(2,1)S(1)}, bf16[225,128]{1,0:T(8,128)(2,1)S(1)}, bf16[4,320,128]{2,1,0:T(8,128)(2,1)S(1)}) custom-call(bf16[16,160,128]{2,1,0:T(8,128)(2,1)S(1)} %shard_map.89.own_ref, bf16[16,160,128]{2,1,0:T(8,128)(2,1)S(1)} %collective-permute-done.17.other_ref, ...), custom_call_target="tpu_custom_call" | custom-call | flops 943718400 | tf_op jit(solution)/shard_map/pallas_call | solution.py:443
  37.0 3.7 %collective-permute-start.18 = (bf16[225,128]{1,0:T(8,128)(2,1)S(1)}, bf16[225,128]{1,0:T(8,128)(2,1)S(1)}, u32[]{:S(2)}, u32[]{:S(2)}) collective-permute-start(bf16[225,128]{1,0:T(8,128)(2,1)S(1)} %get-tuple-element.56), channel_id=1, source_target_pairs={{0,3},{1,2},{2,1},{3,0},{4,7},{5,6},{6,5},{7,4},{8,11},{9,10},{10,... | collective-permute-start | bytes 172808 | tf_op jit(solution)/shard_map/ppermute | solution.py:557
  40.7 0.0 collective-permute-start.19
  40.7 0.0 collective-permute-done.14.refs_1_
  40.7 0.8 %collective-permute-start.20 = (bf16[225,128]{1,0:T(8,128)(2,1)S(1)}, bf16[225,128]{1,0:T(8,128)(2,1)S(1)}, u32[]{:S(2)}, u32[]{:S(2)}) collective-permute-start(bf16[225,128]{1,0:T(8,128)(2,1)S(1)} %get-tuple-element.58), channel_id=1, source_target_pairs={{0,1},{1,0},{2,3},{3,2},{4,5},{5,4},{6,7},{7,6},{8,9},{9,8},{10,11... | collective-permute-start | bytes 172808 | tf_op jit(solution)/shard_map/ppermute | solution.py:557
  41.5 0.0 collective-permute-done.15.refs_2_
  41.5 0.0 collective-permute-done.16.refs_3_
  41.5 1.5 %shard_map.90 = bf16[2,320,128]{2,1,0:T(8,128)(2,1)} custom-call(f32[2,8,128]{2,1,0:T(8,128)S(1)} %pad_maximum_fusion.refs_0_, f32[2,8,128]{2,1,0:T(8,128)S(1)} %collective-permute-done.14.refs_1_, f32[2,8,128]{2,1,0:T(8,128)S(1)} %collective-permute-done.15.refs_2_, f32[2,8,128]{2,1,0:T(8,128)S(1)} %collective-permute-done.16.refs_3_, ...), custom_call_target="tpu_custom_call" | custom-call | flops 117964800 | tf_op jit(solution)/shard_map/pallas_call | solution.py:443
  43.0 1.7 %shard_map.92 = bf16[2,320,128]{2,1,0:T(8,128)(2,1)} custom-call(bf16[4,320,128]{2,1,0:T(8,128)(2,1)S(1)} %get-tuple-element.54.gz_ref, bf16[3,320,960]{2,1,0:T(8,128)(2,1)S(1)} %shard_map.85.w_ref.refs_8_), custom_call_target="tpu_custom_call" | custom-call | flops 471859200 | tf_op jit(solution)/shard_map/pallas_call | solution.py:443
  44.7 0.0 collective-permute-done.18
  44.7 1.1 %collective-permute-done.19 = bf16[225,128]{1,0:T(8,128)(2,1)S(1)} collective-permute-done((bf16[225,128]{1,0:T(8,128)(2,1)S(1)}, bf16[225,128]{1,0:T(8,128)(2,1)S(1)}, u32[]{:S(2)}, u32[]{:S(2)}) %collective-permute-start.19) | collective-permute-done | bytes 57632 | tf_op jit(solution)/shard_map/ppermute | solution.py:557
  45.8 0.0 collective-permute-done.20
  45.8 0.7 %add_bitcast_fusion = f32[28800]{0:T(1024)} fusion(bf16[225,128]{1,0:T(8,128)(2,1)S(1)} %collective-permute-done.20, bf16[225,128]{1,0:T(8,128)(2,1)S(1)} %collective-permute-done.19, f32[225,128]{1,0:T(8,128)S(1)} %get-tuple-element.55, bf16[225,128]{1,0:T(8,128)(2,1)S(1)} %collective-permute-done.18), kind=kLoop, calls=%fused_computation | loop fusion | flops 172800 | bytes 403200 | tf_op jit(solution)/shard_map/reshape | solution.py:573
  (3 shorter events, 0.0 us)
Async XLA Ops:
  0.6 7.2 %collective-permute-start.5 = (bf16[2,320,128]{2,1,0:T(8,128)(2,1)}, bf16[2,320,128]{2,1,0:T(8,128)(2,1)S(1)}, u32[]{:S(2)}, u32[]{:S(2)}) collective-permute-start(bf16[2,320,128]{2,1,0:T(8,128)(2,1)} %bitcast.14), channel_id=1, source_target_pairs={{0,4},{4,0},{8,12},{12,8},{16,20},{20,16},{24,28},{28,24},{1,5},{5... | collective-permute-start | bytes 491528 | tf_op jit(solution)/shard_map/ppermute | solution.py:475
  1.2 7.8 %collective-permute-start.2 = (bf16[2,320,128]{2,1,0:T(8,128)(2,1)}, bf16[2,320,128]{2,1,0:T(8,128)(2,1)S(1)}, u32[]{:S(2)}, u32[]{:S(2)}) collective-permute-start(bf16[2,320,128]{2,1,0:T(8,128)(2,1)} %bitcast.16), channel_id=1, source_target_pairs={{0,8},{4,12},{8,0},{12,4},{16,24},{20,28},{24,16},{28,20},{1,9},{5... | collective-permute-start | bytes 491528 | tf_op jit(solution)/shard_map/ppermute | solution.py:471
  3.7 10.0 %collective-permute-start.3 = (bf16[2,320,128]{2,1,0:T(8,128)(2,1)}, bf16[2,320,128]{2,1,0:T(8,128)(2,1)S(1)}, u32[]{:S(2)}, u32[]{:S(2)}) collective-permute-start(bf16[2,320,128]{2,1,0:T(8,128)(2,1)} %bitcast.17), channel_id=1, source_target_pairs={{0,16},{4,20},{8,24},{12,28},{16,0},{20,4},{24,8},{28,12},{1,17},{... | collective-permute-start | bytes 491528 | tf_op jit(solution)/shard_map/ppermute | solution.py:471
  5.3 8.5 %collective-permute-start.4 = (bf16[2,320,128]{2,1,0:T(8,128)(2,1)}, bf16[2,320,128]{2,1,0:T(8,128)(2,1)S(1)}, u32[]{:S(2)}, u32[]{:S(2)}) collective-permute-start(bf16[2,320,128]{2,1,0:T(8,128)(2,1)} %bitcast.18), channel_id=1, source_target_pairs={{0,24},{4,28},{8,16},{12,20},{16,8},{20,12},{24,0},{28,4},{1,25},{... | collective-permute-start | bytes 491528 | tf_op jit(solution)/shard_map/ppermute | solution.py:471
  5.3 9.8 %collective-permute-start.1 = (bf16[2,320,128]{2,1,0:T(8,128)(2,1)}, bf16[2,320,128]{2,1,0:T(8,128)(2,1)S(1)}, u32[]{:S(2)}, u32[]{:S(2)}) collective-permute-start(bf16[2,320,128]{2,1,0:T(8,128)(2,1)} %bitcast.11), channel_id=1, source_target_pairs={{0,4},{4,0},{8,12},{12,8},{16,20},{20,16},{24,28},{28,24},{1,5},{5... | collective-permute-start | bytes 491528 | tf_op jit(solution)/shard_map/ppermute | solution.py:475
  5.3 1.6 %copy-start = (bf16[3,3,320,320]{3,2,1,0:T(8,128)(2,1)S(1)}, bf16[3,3,320,320]{3,2,1,0:T(8,128)(2,1)}, u32[]{:S(2)}) copy-start(bf16[3,3,320,320]{3,2,1,0:T(8,128)(2,1)} %w_ref.1) | copy-start | bytes 5529604
  6.9 0.9 %copy-start.1 = (bf16[1,2,320,128]{3,2,1,0:T(8,128)(2,1)S(1)}, bf16[1,2,320,128]{3,2,1,0:T(8,128)(2,1)}, u32[]{:S(2)}) copy-start(bf16[1,2,320,128]{3,2,1,0:T(8,128)(2,1)} %param.6) | copy-start | bytes 491524
  6.9 1.8 %copy-start.2 = (bf16[1,2,320,128]{3,2,1,0:T(8,128)(2,1)S(1)}, bf16[1,2,320,128]{3,2,1,0:T(8,128)(2,1)}, u32[]{:S(2)}) copy-start(bf16[1,2,320,128]{3,2,1,0:T(8,128)(2,1)} %param.8) | copy-start | bytes 491524
  7.8 5.9 %copy-start.4 = (f32[320]{0:T(512)S(1)}, f32[320]{0:T(512)}, u32[]{:S(2)}) copy-start(f32[320]{0:T(512)} %param.10) | copy-start | bytes 3844
  7.8 6.0 %copy-start.5 = (f32[320]{0:T(512)S(1)}, f32[320]{0:T(512)}, u32[]{:S(2)}) copy-start(f32[320]{0:T(512)} %param.11) | copy-start | bytes 3844
  7.9 6.1 %copy-start.3 = (bf16[1,2,320,128]{3,2,1,0:T(8,128)(2,1)S(1)}, bf16[1,2,320,128]{3,2,1,0:T(8,128)(2,1)}, u32[]{:S(2)}) copy-start(bf16[1,2,320,128]{3,2,1,0:T(8,128)(2,1)} %param.7) | copy-start | bytes 491524
  7.9 6.7 %collective-permute-start = (bf16[320,128]{1,0:T(8,128)(2,1)S(1)}, bf16[320,128]{1,0:T(8,128)(2,1)S(1)}, u32[]{:S(2)}, u32[]{:S(2)}) collective-permute-start(bf16[320,128]{1,0:T(8,128)(2,1)S(1)} %dynamic-slice_bitcast_fusion), channel_id=1, source_target_pairs={{4,8},{12,16},{20,24},{8,4},{16,12},{24,20},{5,9},{13,17},{21,25},... | collective-permute-start | bytes 245768 | tf_op jit(solution)/shard_map/ppermute | solution.py:482
  14.0 4.6 %collective-permute-start.10 = (bf16[2,320,128]{2,1,0:T(8,128)(2,1)S(1)}, bf16[2,320,128]{2,1,0:T(8,128)(2,1)S(1)}, u32[]{:S(2)}, u32[]{:S(2)}) collective-permute-start(bf16[2,320,128]{2,1,0:T(8,128)(2,1)S(1)} %bitcast.19), channel_id=1, source_target_pairs={{0,4},{4,0},{8,12},{12,8},{16,20},{20,16},{24,28},{28,24},{1,5},{5... | collective-permute-start | bytes 491528 | tf_op jit(solution)/shard_map/ppermute | solution.py:475
  14.0 4.7 %collective-permute-start.11 = (bf16[2,320,128]{2,1,0:T(8,128)(2,1)S(1)}, bf16[2,320,128]{2,1,0:T(8,128)(2,1)S(1)}, u32[]{:S(2)}, u32[]{:S(2)}) collective-permute-start(bf16[2,320,128]{2,1,0:T(8,128)(2,1)S(1)} %collective-permute-done.2.refs_2_), channel_id=1, source_target_pairs={{0,4},{4,0},{8,12},{12,8},{16,20},{20,16},{24,28},{28,24},{1,5},{5... | collective-permute-start | bytes 491528 | tf_op jit(solution)/shard_map/ppermute | solution.py:475
  14.5 5.5 %collective-permute-start.12 = (bf16[2,320,128]{2,1,0:T(8,128)(2,1)S(1)}, bf16[2,320,128]{2,1,0:T(8,128)(2,1)S(1)}, u32[]{:S(2)}, u32[]{:S(2)}) collective-permute-start(bf16[2,320,128]{2,1,0:T(8,128)(2,1)S(1)} %collective-permute-done.3.refs_4_), channel_id=1, source_target_pairs={{0,4},{4,0},{8,12},{12,8},{16,20},{20,16},{24,28},{28,24},{1,5},{5... | collective-permute-start | bytes 491528 | tf_op jit(solution)/shard_map/ppermute | solution.py:475
  14.6 5.5 %collective-permute-start.13 = (bf16[2,320,128]{2,1,0:T(8,128)(2,1)S(1)}, bf16[2,320,128]{2,1,0:T(8,128)(2,1)S(1)}, u32[]{:S(2)}, u32[]{:S(2)}) collective-permute-start(bf16[2,320,128]{2,1,0:T(8,128)(2,1)S(1)} %collective-permute-done.4.refs_6_), channel_id=1, source_target_pairs={{0,4},{4,0},{8,12},{12,8},{16,20},{20,16},{24,28},{28,24},{1,5},{5... | collective-permute-start | bytes 491528 | tf_op jit(solution)/shard_map/ppermute | solution.py:475
  15.0 9.6 %collective-permute-start.7 = (bf16[2,2,160,128]{3,2,1,0:T(8,128)(2,1)S(1)}, bf16[2,2,160,128]{3,2,1,0:T(8,128)(2,1)S(1)}, u32[]{:S(2)}, u32[]{:S(2)}) collective-permute-start(bf16[2,2,160,128]{3,2,1,0:T(8,128)(2,1)S(1)} %shard_map.86.refs_0_), channel_id=1, source_target_pairs={{0,8},{4,12},{8,0},{12,4},{16,24},{20,28},{24,16},{28,20},{1,9},{5... | collective-permute-start | bytes 491528 | tf_op jit(solution)/shard_map/ppermute | solution.py:471
  18.5 9.4 %collective-permute-start.8 = (bf16[2,2,160,128]{3,2,1,0:T(8,128)(2,1)S(1)}, bf16[2,2,160,128]{3,2,1,0:T(8,128)(2,1)S(1)}, u32[]{:S(2)}, u32[]{:S(2)}) collective-permute-start(bf16[2,2,160,128]{3,2,1,0:T(8,128)(2,1)S(1)} %shard_map.86.refs_0_), channel_id=1, source_target_pairs={{0,16},{4,20},{8,24},{12,28},{16,0},{20,4},{24,8},{28,12},{1,17},{... | collective-permute-start | bytes 491528 | tf_op jit(solution)/shard_map/ppermute | solution.py:471
  18.7 9.2 %collective-permute-start.9 = (bf16[2,2,160,128]{3,2,1,0:T(8,128)(2,1)S(1)}, bf16[2,2,160,128]{3,2,1,0:T(8,128)(2,1)S(1)}, u32[]{:S(2)}, u32[]{:S(2)}) collective-permute-start(bf16[2,2,160,128]{3,2,1,0:T(8,128)(2,1)S(1)} %shard_map.86.refs_0_), channel_id=1, source_target_pairs={{0,24},{4,28},{8,16},{12,20},{16,8},{20,12},{24,0},{28,4},{1,25},{... | collective-permute-start | bytes 491528 | tf_op jit(solution)/shard_map/ppermute | solution.py:471
  29.6 5.7 %collective-permute-start.17 = (bf16[16,160,128]{2,1,0:T(8,128)(2,1)S(1)}, bf16[16,160,128]{2,1,0:T(8,128)(2,1)S(1)}, u32[]{:S(2)}, u32[]{:S(2)}) collective-permute-start(bf16[16,160,128]{2,1,0:T(8,128)(2,1)S(1)} %shard_map.89.own_ref), channel_id=1, source_target_pairs={{0,4},{4,0},{8,12},{12,8},{16,20},{20,16},{24,28},{28,24},{1,5},{5... | collective-permute-start | bytes 1966088 | tf_op jit(solution)/shard_map/ppermute | solution.py:475
  29.7 2.1 %collective-permute-start.6 = (f32[8,128]{1,0:T(8,128)S(1)}, f32[8,128]{1,0:T(8,128)S(1)}, u32[]{:S(2)}, u32[]{:S(2)}) collective-permute-start(f32[8,128]{1,0:T(8,128)S(1)} %get-tuple-element.32), channel_id=1, source_target_pairs={{0,4},{4,0},{8,12},{12,8},{16,20},{20,16},{24,28},{28,24},{1,5},{5... | collective-permute-start | bytes 12296 | tf_op jit(solution)/shard_map/ppermute | solution.py:475
  31.8 8.9 %collective-permute-start.14 = (f32[2,8,128]{2,1,0:T(8,128)S(1)}, f32[2,8,128]{2,1,0:T(8,128)S(1)}, u32[]{:S(2)}, u32[]{:S(2)}) collective-permute-start(f32[2,8,128]{2,1,0:T(8,128)S(1)} %pad_maximum_fusion.refs_0_), channel_id=1, source_target_pairs={{0,24},{4,28},{8,16},{12,20},{16,8},{20,12},{24,0},{28,4},{1,25},{... | collective-permute-start | bytes 24584 | tf_op jit(solution)/shard_map/ppermute | solution.py:471
  33.2 8.3 %collective-permute-start.15 = (f32[2,8,128]{2,1,0:T(8,128)S(1)}, f32[2,8,128]{2,1,0:T(8,128)S(1)}, u32[]{:S(2)}, u32[]{:S(2)}) collective-permute-start(f32[2,8,128]{2,1,0:T(8,128)S(1)} %pad_maximum_fusion.refs_0_), channel_id=1, source_target_pairs={{0,8},{4,12},{8,0},{12,4},{16,24},{20,28},{24,16},{28,20},{1,9},{5... | collective-permute-start | bytes 24584 | tf_op jit(solution)/shard_map/ppermute | solution.py:471
  33.9 7.6 %collective-permute-start.16 = (f32[2,8,128]{2,1,0:T(8,128)S(1)}, f32[2,8,128]{2,1,0:T(8,128)S(1)}, u32[]{:S(2)}, u32[]{:S(2)}) collective-permute-start(f32[2,8,128]{2,1,0:T(8,128)S(1)} %pad_maximum_fusion.refs_0_), channel_id=1, source_target_pairs={{0,16},{4,20},{8,24},{12,28},{16,0},{20,4},{24,8},{28,12},{1,17},{... | collective-permute-start | bytes 24584 | tf_op jit(solution)/shard_map/ppermute | solution.py:471
  37.0 7.7 %collective-permute-start.18 = (bf16[225,128]{1,0:T(8,128)(2,1)S(1)}, bf16[225,128]{1,0:T(8,128)(2,1)S(1)}, u32[]{:S(2)}, u32[]{:S(2)}) collective-permute-start(bf16[225,128]{1,0:T(8,128)(2,1)S(1)} %get-tuple-element.56), channel_id=1, source_target_pairs={{0,3},{1,2},{2,1},{3,0},{4,7},{5,6},{6,5},{7,4},{8,11},{9,10},{10,... | collective-permute-start | bytes 172808 | tf_op jit(solution)/shard_map/ppermute | solution.py:557
  40.7 5.1 %collective-permute-start.19 = (bf16[225,128]{1,0:T(8,128)(2,1)S(1)}, bf16[225,128]{1,0:T(8,128)(2,1)S(1)}, u32[]{:S(2)}, u32[]{:S(2)}) collective-permute-start(bf16[225,128]{1,0:T(8,128)(2,1)S(1)} %get-tuple-element.57), channel_id=1, source_target_pairs={{0,2},{1,3},{2,0},{3,1},{4,6},{5,7},{6,4},{7,5},{8,10},{9,11},{10,... | collective-permute-start | bytes 172808 | tf_op jit(solution)/shard_map/ppermute | solution.py:557
  40.7 5.1 %collective-permute-start.20 = (bf16[225,128]{1,0:T(8,128)(2,1)S(1)}, bf16[225,128]{1,0:T(8,128)(2,1)S(1)}, u32[]{:S(2)}, u32[]{:S(2)}) collective-permute-start(bf16[225,128]{1,0:T(8,128)(2,1)S(1)} %get-tuple-element.58), channel_id=1, source_target_pairs={{0,1},{1,0},{2,3},{3,2},{4,5},{5,4},{6,7},{7,6},{8,9},{9,8},{10,11... | collective-permute-start | bytes 172808 | tf_op jit(solution)/shard_map/ppermute | solution.py:557

commit v3 on v2

--- a/solution.py
+++ b/solution.py
@@ -493,15 +493,6 @@
     x_all = []
     for k in range(0, blocks, 2):
         x_all += [x_far[k], near(x_far[k])]
-    z_next, stat = call(
-        next_conv_kernel,
-        (shape((rows, chans, width), F32), shape((8 * -(-2 * len(lane_tiles(chans)) // 8), LANES), F32)),
-        (edge, next_near, x_next, w_flat),
-        flops=rows * flops,
-        rows=rows,
-    )
-    stat_near = near(stat)
-    x_all, z_next = lax.optimization_barrier((x_all, z_next))
     xs, z_cur, norm = call(
         conv_kernel,
         (
@@ -517,7 +508,6 @@
         count=count,
         wide=4 if image % 4 == 0 else 2,
     )
-    stat_pair = jnp.stack((stat, stat_near))
     gz_own = call(
         pull_kernel,
         shape((image, half, width), BF16),
@@ -533,8 +523,16 @@
         count=count,
     )
     gz_other = near(gz_own)
-    stat_pair, gz_own = lax.optimization_barrier((stat_pair, gz_own))
-    stat_far = far(stat_pair)
+    edge, gz_own = lax.optimization_barrier((edge, gz_own))
+    z_next, stat = call(
+        next_conv_kernel,
+        (shape((rows, chans, width), F32), shape((8 * -(-2 * len(lane_tiles(chans)) // 8), LANES), F32)),
+        (edge, next_near, x_next, w_flat),
+        flops=rows * flops,
+        rows=rows,
+    )
+    stat_near = near(stat)
+    gz_other, z_next = lax.optimization_barrier((gz_other, z_next))
     results = call(
         filter_kernel,
         (shape((piece, LANES), F32),)
@@ -555,10 +553,13 @@
     total = results[0]
     for s in range(groups_dp - 1, 0, -1):
         total = total + lax.ppermute(results[s], "dp", pairs(groups_dp, s)).astype(F32)
+    stat_near, gz_rows = lax.optimization_barrier((stat_near, results[groups_dp]))
+    stat_pair = jnp.stack((stat, stat_near))
+    stat_far = far(stat_pair)
     grad_x = call(
         grad_x_kernel,
         shape((rows, chans, width), BF16),
-        (results[groups_dp], w_flat),
+        (gz_rows, w_flat),
         flops=rows * flops,
         rows=rows,
     )

time: 46.7 us -> 54.7 us (1.17)
  local copies, waits for them, and re-layouts: 2.37 us -> 6.62 us
  starting transfers between devices: 18.9 us -> 23.1 us
  waiting for transfers between devices: 11 us -> 9.33 us
  Pallas kernels: 12.8 us -> 13.9 us
    ppermute x8, starting transfers between devices: 2.21 us -> 6.95 us  [near(): return lax.ppermute(own, 'height', pairs(blocks, 1))]
    unnamed x12 -> x16, local copies, waits for them, and re-layouts: 2.17 us -> 6.42 us
    pallas_call x8, Pallas kernels: 12.8 us -> 13.9 us  [call(): pl.pallas_call(functools.partial(kernel, **static), out_shape=out_shape,...]
    ppermute x3, waiting for transfers between devices: 1.09 us -> 0.01 us  [gathered(): lax.ppermute(results[s], 'dp', pairs(groups_dp, s)).astype(F32)]
  transfers between devices with their start and end apart: 21 -> 21, of which waited for: 5 -> 6; matrix products, arithmetic and copies ran while one was open for 0% -> 0% of each run, Pallas kernels for 24% -> 22%
where the time goes in v3:
time: 54.7 us; the launch traced here: 54.5 us
  starting transfers between devices  23.1 us (42%)
  Pallas kernels  13.9 us (25%)
  waiting for transfers between devices  9.33 us (17%)
  local copies, waits for them, and re-layouts  6.62 us (12%)
  between operations  0.81 us (1%)
  other arithmetic  0.68 us (1%)
    pallas_call x8, Pallas kernels, call(): pl.pallas_call(functools.partial(kernel, **static), out_shape=out_shape,...  13.9 us
    ppermute x9, starting transfers between devices, far(): held[k] = lax.ppermute(own, 'height', pairs(blocks, k))  11.1 us
    ppermute x9, waiting for transfers between devices, far(): held[k] = lax.ppermute(own, 'height', pairs(blocks, k))  8.16 us
    ppermute x8, starting transfers between devices, near(): return lax.ppermute(own, 'height', pairs(blocks, 1))  6.95 us
    unnamed x16, local copies, waits for them, and re-layouts  6.42 us
    ppermute x3, starting transfers between devices, gathered(): lax.ppermute(results[s], 'dp', pairs(groups_dp, s)).astype(F32)  4.39 us
    ppermute x8, waiting for transfers between devices, near(): return lax.ppermute(own, 'height', pairs(blocks, 1))  1.16 us
  transfers between devices with their start and end apart: 21, of which 6 were waited for; matrix products, arithmetic and copies ran while one was open for 0% of the time, Pallas kernels for 22%

profile of v3, /device:TPU:0, one launch (start us, length us, event | category | flops | bytes accessed | tf_op | source)
XLA Modules:
  0.0 54.5 jit_solution(8723733073939012551)
XLA Ops:
  0.6 0.6 %collective-permute-start.1 = (bf16[2,320,128]{2,1,0:T(8,128)(2,1)}, bf16[2,320,128]{2,1,0:T(8,128)(2,1)S(1)}, u32[]{:S(2)}, u32[]{:S(2)}) collective-permute-start(bf16[2,320,128]{2,1,0:T(8,128)(2,1)} %bitcast.14), channel_id=1, source_target_pairs={{0,4},{4,0},{8,12},{12,8},{16,20},{20,16},{24,28},{28,24},{1,5},{5... | collective-permute-start | bytes 491528 | tf_op jit(solution)/shard_map/ppermute | solution.py:475
  1.2 2.6 %collective-permute-start.5 = (bf16[2,320,128]{2,1,0:T(8,128)(2,1)}, bf16[2,320,128]{2,1,0:T(8,128)(2,1)S(1)}, u32[]{:S(2)}, u32[]{:S(2)}) collective-permute-start(bf16[2,320,128]{2,1,0:T(8,128)(2,1)} %bitcast.16), channel_id=1, source_target_pairs={{0,8},{4,12},{8,0},{12,4},{16,24},{20,28},{24,16},{28,20},{1,9},{5... | collective-permute-start | bytes 491528 | tf_op jit(solution)/shard_map/ppermute | solution.py:471
  3.7 1.5 %collective-permute-start.6 = (bf16[2,320,128]{2,1,0:T(8,128)(2,1)}, bf16[2,320,128]{2,1,0:T(8,128)(2,1)S(1)}, u32[]{:S(2)}, u32[]{:S(2)}) collective-permute-start(bf16[2,320,128]{2,1,0:T(8,128)(2,1)} %bitcast.17), channel_id=1, source_target_pairs={{0,16},{4,20},{8,24},{12,28},{16,0},{20,4},{24,8},{28,12},{1,17},{... | collective-permute-start | bytes 491528 | tf_op jit(solution)/shard_map/ppermute | solution.py:471
  5.3 0.0 collective-permute-start.7
  5.3 1.6 %copy-done.2 = bf16[3,3,320,320]{3,2,1,0:T(8,128)(2,1)S(1)} copy-done((bf16[3,3,320,320]{3,2,1,0:T(8,128)(2,1)S(1)}, bf16[3,3,320,320]{3,2,1,0:T(8,128)(2,1)}, u32[]{:S(2)}) %copy-start.2) | copy-done | bytes 1843224
  6.9 0.4 shard_map.86.refs_8_.w_ref
  7.3 0.0 copy-start.6
  7.3 0.0 copy-start.7
  7.3 0.0 copy-start.5
  7.3 0.0 collective-permute-done.1.near_ref
  7.3 0.5 copy-done.4
  7.8 1.2 %collective-permute-done.5.refs_2_ = bf16[2,320,128]{2,1,0:T(8,128)(2,1)S(1)} collective-permute-done((bf16[2,320,128]{2,1,0:T(8,128)(2,1)}, bf16[2,320,128]{2,1,0:T(8,128)(2,1)S(1)}, u32[]{:S(2)}, u32[]{:S(2)}) %collective-permute-start.5) | collective-permute-done | bytes 163872 | tf_op jit(solution)/shard_map/ppermute | solution.py:471
  9.0 4.7 %collective-permute-done.6.refs_4_ = bf16[2,320,128]{2,1,0:T(8,128)(2,1)S(1)} collective-permute-done((bf16[2,320,128]{2,1,0:T(8,128)(2,1)}, bf16[2,320,128]{2,1,0:T(8,128)(2,1)S(1)}, u32[]{:S(2)}, u32[]{:S(2)}) %collective-permute-start.6) | collective-permute-done | bytes 163872 | tf_op jit(solution)/shard_map/ppermute | solution.py:471
  13.7 0.0 collective-permute-done.7.refs_6_
  13.7 0.0 copy-done.6
  13.7 0.1 broadcast_in_dim.8.refs_6_.refs_5_
  13.8 0.0 copy-done.7
  13.8 0.1 broadcast_in_dim.9.refs_7_.refs_6_
  13.9 0.1 collective-permute-start.10
  14.0 0.5 collective-permute-start.11
  14.5 0.0 copy-done.5
  14.5 0.1 collective-permute-start.8
  14.6 0.4 collective-permute-start.9
  15.0 1.2 %collective-permute-start.2 = (bf16[2,2,160,128]{3,2,1,0:T(8,128)(2,1)S(1)}, bf16[2,2,160,128]{3,2,1,0:T(8,128)(2,1)S(1)}, u32[]{:S(2)}, u32[]{:S(2)}) collective-permute-start(bf16[2,2,160,128]{3,2,1,0:T(8,128)(2,1)S(1)} %shard_map.85.refs_0_), channel_id=1, source_target_pairs={{0,8},{4,12},{8,0},{12,4},{16,24},{20,28},{24,16},{28,20},{1,9},{5... | collective-permute-start | bytes 491528 | tf_op jit(solution)/shard_map/ppermute | solution.py:471
  16.3 0.0 collective-permute-done.10.refs_5_
  16.3 0.8 %collective-permute-start.3 = (bf16[2,2,160,128]{3,2,1,0:T(8,128)(2,1)S(1)}, bf16[2,2,160,128]{3,2,1,0:T(8,128)(2,1)S(1)}, u32[]{:S(2)}, u32[]{:S(2)}) collective-permute-start(bf16[2,2,160,128]{3,2,1,0:T(8,128)(2,1)S(1)} %shard_map.85.refs_0_), channel_id=1, source_target_pairs={{0,16},{4,20},{8,24},{12,28},{16,0},{20,4},{24,8},{28,12},{1,17},{... | collective-permute-start | bytes 491528 | tf_op jit(solution)/shard_map/ppermute | solution.py:471
  17.1 0.0 collective-permute-done.11.refs_7_
  17.1 1.4 %collective-permute-start.4 = (bf16[2,2,160,128]{3,2,1,0:T(8,128)(2,1)S(1)}, bf16[2,2,160,128]{3,2,1,0:T(8,128)(2,1)S(1)}, u32[]{:S(2)}, u32[]{:S(2)}) collective-permute-start(bf16[2,2,160,128]{3,2,1,0:T(8,128)(2,1)S(1)} %shard_map.85.refs_0_), channel_id=1, source_target_pairs={{0,24},{4,28},{8,16},{12,20},{16,8},{20,12},{24,0},{28,4},{1,25},{... | collective-permute-start | bytes 491528 | tf_op jit(solution)/shard_map/ppermute | solution.py:471
  18.5 0.0 collective-permute-done.8.refs_1_
  18.5 0.0 collective-permute-done.9.refs_3_
  18.5 4.6 %shard_map.87 = (bf16[18,960,128]{2,1,0:T(8,128)(2,1)S(1)}, f32[16,160,128]{2,1,0:T(8,128)S(1)}, f32[2,160,128]{2,1,0:T(8,128)S(1)}) custom-call(bf16[2,320,128]{2,1,0:T(8,128)(2,1)S(1)} %bitcast.20, bf16[2,320,128]{2,1,0:T(8,128)(2,1)S(1)} %collective-permute-done.8.refs_1_, bf16[2,320,128]{2,1,0:T(8,128)(2,1)S(1)} %collective-permute-done.5.refs_2_, ...), custom_call_target="tpu_custom_call" | custom-call | flops 1887436800 | tf_op jit(solution)/shard_map/pallas_call | solution.py:443
  23.1 0.0 copy-start
  23.1 2.0 %copy-done = bf16[18,960,128]{2,1,0:T(8,128)(2,1)} copy-done((bf16[18,960,128]{2,1,0:T(8,128)(2,1)}, bf16[18,960,128]{2,1,0:T(8,128)(2,1)S(1)}, u32[]{:S(2)}) %copy-start) | copy-done | bytes 4423704
  25.1 0.0 collective-permute-done.2.refs_1_
  25.1 0.0 collective-permute-done.3.refs_2_
  25.2 0.5 collective-permute-done.4.refs_3_
  25.7 1.7 %shard_map.88.own_ref = bf16[16,160,128]{2,1,0:T(8,128)(2,1)S(1)} custom-call(bf16[2,2,160,128]{3,2,1,0:T(8,128)(2,1)S(1)} %shard_map.85.refs_0_, bf16[2,2,160,128]{3,2,1,0:T(8,128)(2,1)S(1)} %collective-permute-done.2.refs_1_, bf16[2,2,160,128]{3,2,1,0:T(8,128)(2,1)S(1)} %collective-permute-done.3.refs_2_, ...), custom_call_target="tpu_custom_call" | custom-call | flops 471859200 | tf_op jit(solution)/shard_map/pallas_call | solution.py:443
  27.4 0.1 collective-permute-start.14
  27.4 0.0 copy-done.3
  27.4 0.5 collective-permute-start.12
  27.9 0.7 %collective-permute-start = (bf16[320,128]{1,0:T(8,128)(2,1)S(1)}, bf16[320,128]{1,0:T(8,128)(2,1)S(1)}, u32[]{:S(2)}, u32[]{:S(2)}) collective-permute-start(bf16[320,128]{1,0:T(8,128)(2,1)S(1)} %dynamic-slice_bitcast_fusion), channel_id=1, source_target_pairs={{4,8},{12,16},{20,24},{8,4},{16,12},{24,20},{5,9},{13,17},{21,25},... | collective-permute-start | bytes 245768 | tf_op jit(solution)/shard_map/ppermute | solution.py:482
  28.6 0.0 collective-permute-done.edge_ref
  28.6 1.1 %collective-permute-done.12.near_ref = bf16[2,320,128]{2,1,0:T(8,128)(2,1)S(1)} collective-permute-done((bf16[2,320,128]{2,1,0:T(8,128)(2,1)S(1)}, bf16[2,320,128]{2,1,0:T(8,128)(2,1)S(1)}, u32[]{:S(2)}, u32[]{:S(2)}) %collective-permute-start.12) | collective-permute-done | bytes 163872 | tf_op jit(solution)/shard_map/ppermute | solution.py:475
  29.8 1.2 %shard_map.89 = (f32[2,320,128]{2,1,0:T(8,128)S(1)}, f32[8,128]{1,0:T(8,128)S(1)}) custom-call(bf16[320,128]{1,0:T(8,128)(2,1)S(1)} %collective-permute-done.edge_ref, bf16[2,320,128]{2,1,0:T(8,128)(2,1)S(1)} %collective-permute-done.12.near_ref, bf16[2,320,128]{2,1,0:T(8,128)(2,1)S(1)} %bitcast.12, bf16[3,320,960]{2,1,0:T(8,128)(2,1)S(1)} %shard_map.86.refs_8_.w_ref), custom_call_target="tpu_custom_call" | custom-call | flops 471859200 | tf_op jit(solution)/shard_map/pallas_call | solution.py:443
  30.9 4.8 %collective-permute-start.13 = (f32[8,128]{1,0:T(8,128)S(1)}, f32[8,128]{1,0:T(8,128)S(1)}, u32[]{:S(2)}, u32[]{:S(2)}) collective-permute-start(f32[8,128]{1,0:T(8,128)S(1)} %get-tuple-element.36), channel_id=1, source_target_pairs={{0,4},{4,0},{8,12},{12,8},{16,20},{20,16},{24,28},{28,24},{1,5},{5... | collective-permute-start | bytes 12296 | tf_op jit(solution)/shard_map/ppermute | solution.py:475
  35.7 0.0 collective-permute-done.14.other_ref
  35.7 2.3 %copy-done.1 = bf16[18,960,128]{2,1,0:T(8,128)(2,1)S(1)} copy-done((bf16[18,960,128]{2,1,0:T(8,128)(2,1)S(1)}, bf16[18,960,128]{2,1,0:T(8,128)(2,1)}, u32[]{:S(2)}) %copy-start.1) | copy-done | bytes 4423704
  37.9 2.9 %shard_map.90 = (f32[225,128]{1,0:T(8,128)S(1)}, bf16[225,128]{1,0:T(8,128)(2,1)S(1)}, bf16[225,128]{1,0:T(8,128)(2,1)S(1)}, bf16[225,128]{1,0:T(8,128)(2,1)S(1)}, bf16[4,320,128]{2,1,0:T(8,128)(2,1)S(1)}) custom-call(bf16[16,160,128]{2,1,0:T(8,128)(2,1)S(1)} %shard_map.88.own_ref, bf16[16,160,128]{2,1,0:T(8,128)(2,1)} %collective-permute-done.14.other_ref, ...), custom_call_target="tpu_custom_call" | custom-call | flops 943718400 | tf_op jit(solution)/shard_map/pallas_call | solution.py:443
  40.8 0.0 collective-permute-done.13
  40.9 1.7 %collective-permute-start.15 = (f32[2,8,128]{2,1,0:T(8,128)S(1)}, f32[2,8,128]{2,1,0:T(8,128)S(1)}, u32[]{:S(2)}, u32[]{:S(2)}) collective-permute-start(f32[2,8,128]{2,1,0:T(8,128)S(1)} %pad_maximum_fusion.refs_0_), channel_id=1, source_target_pairs={{0,24},{4,28},{8,16},{12,20},{16,8},{20,12},{24,0},{28,4},{1,25},{... | collective-permute-start | bytes 24584 | tf_op jit(solution)/shard_map/ppermute | solution.py:471
  42.6 3.6 %collective-permute-start.18 = (bf16[225,128]{1,0:T(8,128)(2,1)S(1)}, bf16[225,128]{1,0:T(8,128)(2,1)S(1)}, u32[]{:S(2)}, u32[]{:S(2)}) collective-permute-start(bf16[225,128]{1,0:T(8,128)(2,1)S(1)} %get-tuple-element.46), channel_id=1, source_target_pairs={{0,3},{1,2},{2,1},{3,0},{4,7},{5,6},{6,5},{7,4},{8,11},{9,10},{10,... | collective-permute-start | bytes 172808 | tf_op jit(solution)/shard_map/ppermute | solution.py:555
  46.2 0.0 collective-permute-start.19
  46.2 0.8 %collective-permute-start.20 = (bf16[225,128]{1,0:T(8,128)(2,1)S(1)}, bf16[225,128]{1,0:T(8,128)(2,1)S(1)}, u32[]{:S(2)}, u32[]{:S(2)}) collective-permute-start(bf16[225,128]{1,0:T(8,128)(2,1)S(1)} %get-tuple-element.48), channel_id=1, source_target_pairs={{0,1},{1,0},{2,3},{3,2},{4,5},{5,4},{6,7},{7,6},{8,9},{9,8},{10,11... | collective-permute-start | bytes 172808 | tf_op jit(solution)/shard_map/ppermute | solution.py:555
  47.0 1.6 %collective-permute-start.16 = (f32[2,8,128]{2,1,0:T(8,128)S(1)}, f32[2,8,128]{2,1,0:T(8,128)S(1)}, u32[]{:S(2)}, u32[]{:S(2)}) collective-permute-start(f32[2,8,128]{2,1,0:T(8,128)S(1)} %pad_maximum_fusion.refs_0_), channel_id=1, source_target_pairs={{0,8},{4,12},{8,0},{12,4},{16,24},{20,28},{24,16},{28,20},{1,9},{5... | collective-permute-start | bytes 24584 | tf_op jit(solution)/shard_map/ppermute | solution.py:471
  48.6 0.0 collective-permute-done.15.refs_1_
  48.6 0.2 collective-permute-start.17
  48.8 1.7 %shard_map.92 = bf16[2,320,128]{2,1,0:T(8,128)(2,1)} custom-call(bf16[4,320,128]{2,1,0:T(8,128)(2,1)S(1)} %get-tuple-element.44.gz_ref, bf16[3,320,960]{2,1,0:T(8,128)(2,1)S(1)} %shard_map.86.refs_8_.w_ref), custom_call_target="tpu_custom_call" | custom-call | flops 471859200 | tf_op jit(solution)/shard_map/pallas_call | solution.py:443
  50.5 0.1 collective-permute-done.16.refs_2_
  50.6 1.7 %collective-permute-done.17.refs_3_ = f32[2,8,128]{2,1,0:T(8,128)S(1)} collective-permute-done((f32[2,8,128]{2,1,0:T(8,128)S(1)}, f32[2,8,128]{2,1,0:T(8,128)S(1)}, u32[]{:S(2)}, u32[]{:S(2)}) %collective-permute-start.17) | collective-permute-done | bytes 8224 | tf_op jit(solution)/shard_map/ppermute | solution.py:471
  52.3 1.5 %shard_map.91 = bf16[2,320,128]{2,1,0:T(8,128)(2,1)} custom-call(f32[2,8,128]{2,1,0:T(8,128)S(1)} %pad_maximum_fusion.refs_0_, f32[2,8,128]{2,1,0:T(8,128)S(1)} %collective-permute-done.15.refs_1_, f32[2,8,128]{2,1,0:T(8,128)S(1)} %collective-permute-done.16.refs_2_, f32[2,8,128]{2,1,0:T(8,128)S(1)} %collective-permute-done.17.refs_3_, ...), custom_call_target="tpu_custom_call" | custom-call | flops 117964800 | tf_op jit(solution)/shard_map/pallas_call | solution.py:443
  53.8 0.0 collective-permute-done.18
  53.8 0.0 collective-permute-done.19
  53.8 0.0 collective-permute-done.20
  53.8 0.7 %add_bitcast_fusion = f32[28800]{0:T(1024)} fusion(bf16[225,128]{1,0:T(8,128)(2,1)S(1)} %collective-permute-done.20, bf16[225,128]{1,0:T(8,128)(2,1)S(1)} %collective-permute-done.19, f32[225,128]{1,0:T(8,128)S(1)} %get-tuple-element.45, bf16[225,128]{1,0:T(8,128)(2,1)S(1)} %collective-permute-done.18), kind=kLoop, calls=%fused_computation | loop fusion | flops 172800 | bytes 403200 | tf_op jit(solution)/shard_map/reshape | solution.py:574
  (7 shorter events, 0.0 us)
Async XLA Ops:
  0.6 6.7 %collective-permute-start.1 = (bf16[2,320,128]{2,1,0:T(8,128)(2,1)}, bf16[2,320,128]{2,1,0:T(8,128)(2,1)S(1)}, u32[]{:S(2)}, u32[]{:S(2)}) collective-permute-start(bf16[2,320,128]{2,1,0:T(8,128)(2,1)} %bitcast.14), channel_id=1, source_target_pairs={{0,4},{4,0},{8,12},{12,8},{16,20},{20,16},{24,28},{28,24},{1,5},{5... | collective-permute-start | bytes 491528 | tf_op jit(solution)/shard_map/ppermute | solution.py:475
  1.2 7.8 %collective-permute-start.5 = (bf16[2,320,128]{2,1,0:T(8,128)(2,1)}, bf16[2,320,128]{2,1,0:T(8,128)(2,1)S(1)}, u32[]{:S(2)}, u32[]{:S(2)}) collective-permute-start(bf16[2,320,128]{2,1,0:T(8,128)(2,1)} %bitcast.16), channel_id=1, source_target_pairs={{0,8},{4,12},{8,0},{12,4},{16,24},{20,28},{24,16},{28,20},{1,9},{5... | collective-permute-start | bytes 491528 | tf_op jit(solution)/shard_map/ppermute | solution.py:471
  3.7 10.0 %collective-permute-start.6 = (bf16[2,320,128]{2,1,0:T(8,128)(2,1)}, bf16[2,320,128]{2,1,0:T(8,128)(2,1)S(1)}, u32[]{:S(2)}, u32[]{:S(2)}) collective-permute-start(bf16[2,320,128]{2,1,0:T(8,128)(2,1)} %bitcast.17), channel_id=1, source_target_pairs={{0,16},{4,20},{8,24},{12,28},{16,0},{20,4},{24,8},{28,12},{1,17},{... | collective-permute-start | bytes 491528 | tf_op jit(solution)/shard_map/ppermute | solution.py:471
  5.3 8.5 %collective-permute-start.7 = (bf16[2,320,128]{2,1,0:T(8,128)(2,1)}, bf16[2,320,128]{2,1,0:T(8,128)(2,1)S(1)}, u32[]{:S(2)}, u32[]{:S(2)}) collective-permute-start(bf16[2,320,128]{2,1,0:T(8,128)(2,1)} %bitcast.18), channel_id=1, source_target_pairs={{0,24},{4,28},{8,16},{12,20},{16,8},{20,12},{24,0},{28,4},{1,25},{... | collective-permute-start | bytes 491528 | tf_op jit(solution)/shard_map/ppermute | solution.py:471
  5.3 1.6 %copy-start.2 = (bf16[3,3,320,320]{3,2,1,0:T(8,128)(2,1)S(1)}, bf16[3,3,320,320]{3,2,1,0:T(8,128)(2,1)}, u32[]{:S(2)}) copy-start(bf16[3,3,320,320]{3,2,1,0:T(8,128)(2,1)} %w_ref.1) | copy-start | bytes 5529604
  6.9 0.9 %copy-start.4 = (bf16[1,2,320,128]{3,2,1,0:T(8,128)(2,1)S(1)}, bf16[1,2,320,128]{3,2,1,0:T(8,128)(2,1)}, u32[]{:S(2)}) copy-start(bf16[1,2,320,128]{3,2,1,0:T(8,128)(2,1)} %param.8) | copy-start | bytes 491524
  7.3 6.4 %copy-start.6 = (f32[320]{0:T(512)S(1)}, f32[320]{0:T(512)}, u32[]{:S(2)}) copy-start(f32[320]{0:T(512)} %param.10) | copy-start | bytes 3844
  7.3 6.5 %copy-start.7 = (f32[320]{0:T(512)S(1)}, f32[320]{0:T(512)}, u32[]{:S(2)}) copy-start(f32[320]{0:T(512)} %param.11) | copy-start | bytes 3844
  7.3 7.2 %copy-start.5 = (bf16[1,2,320,128]{3,2,1,0:T(8,128)(2,1)S(1)}, bf16[1,2,320,128]{3,2,1,0:T(8,128)(2,1)}, u32[]{:S(2)}) copy-start(bf16[1,2,320,128]{3,2,1,0:T(8,128)(2,1)} %param.7) | copy-start | bytes 491524
  13.9 2.3 %collective-permute-start.10 = (bf16[2,320,128]{2,1,0:T(8,128)(2,1)S(1)}, bf16[2,320,128]{2,1,0:T(8,128)(2,1)S(1)}, u32[]{:S(2)}, u32[]{:S(2)}) collective-permute-start(bf16[2,320,128]{2,1,0:T(8,128)(2,1)S(1)} %collective-permute-done.6.refs_4_), channel_id=1, source_target_pairs={{0,4},{4,0},{8,12},{12,8},{16,20},{20,16},{24,28},{28,24},{1,5},{5... | collective-permute-start | bytes 491528 | tf_op jit(solution)/shard_map/ppermute | solution.py:475
  14.0 3.1 %collective-permute-start.11 = (bf16[2,320,128]{2,1,0:T(8,128)(2,1)S(1)}, bf16[2,320,128]{2,1,0:T(8,128)(2,1)S(1)}, u32[]{:S(2)}, u32[]{:S(2)}) collective-permute-start(bf16[2,320,128]{2,1,0:T(8,128)(2,1)S(1)} %collective-permute-done.7.refs_6_), channel_id=1, source_target_pairs={{0,4},{4,0},{8,12},{12,8},{16,20},{20,16},{24,28},{28,24},{1,5},{5... | collective-permute-start | bytes 491528 | tf_op jit(solution)/shard_map/ppermute | solution.py:475
  14.5 4.0 %collective-permute-start.8 = (bf16[2,320,128]{2,1,0:T(8,128)(2,1)S(1)}, bf16[2,320,128]{2,1,0:T(8,128)(2,1)S(1)}, u32[]{:S(2)}, u32[]{:S(2)}) collective-permute-start(bf16[2,320,128]{2,1,0:T(8,128)(2,1)S(1)} %bitcast.19), channel_id=1, source_target_pairs={{0,4},{4,0},{8,12},{12,8},{16,20},{20,16},{24,28},{28,24},{1,5},{5... | collective-permute-start | bytes 491528 | tf_op jit(solution)/shard_map/ppermute | solution.py:475
  14.6 3.9 %collective-permute-start.9 = (bf16[2,320,128]{2,1,0:T(8,128)(2,1)S(1)}, bf16[2,320,128]{2,1,0:T(8,128)(2,1)S(1)}, u32[]{:S(2)}, u32[]{:S(2)}) collective-permute-start(bf16[2,320,128]{2,1,0:T(8,128)(2,1)S(1)} %collective-permute-done.5.refs_2_), channel_id=1, source_target_pairs={{0,4},{4,0},{8,12},{12,8},{16,20},{20,16},{24,28},{28,24},{1,5},{5... | collective-permute-start | bytes 491528 | tf_op jit(solution)/shard_map/ppermute | solution.py:475
  15.0 10.1 %collective-permute-start.2 = (bf16[2,2,160,128]{3,2,1,0:T(8,128)(2,1)S(1)}, bf16[2,2,160,128]{3,2,1,0:T(8,128)(2,1)S(1)}, u32[]{:S(2)}, u32[]{:S(2)}) collective-permute-start(bf16[2,2,160,128]{3,2,1,0:T(8,128)(2,1)S(1)} %shard_map.85.refs_0_), channel_id=1, source_target_pairs={{0,8},{4,12},{8,0},{12,4},{16,24},{20,28},{24,16},{28,20},{1,9},{5... | collective-permute-start | bytes 491528 | tf_op jit(solution)/shard_map/ppermute | solution.py:471
  16.3 8.9 %collective-permute-start.3 = (bf16[2,2,160,128]{3,2,1,0:T(8,128)(2,1)S(1)}, bf16[2,2,160,128]{3,2,1,0:T(8,128)(2,1)S(1)}, u32[]{:S(2)}, u32[]{:S(2)}) collective-permute-start(bf16[2,2,160,128]{3,2,1,0:T(8,128)(2,1)S(1)} %shard_map.85.refs_0_), channel_id=1, source_target_pairs={{0,16},{4,20},{8,24},{12,28},{16,0},{20,4},{24,8},{28,12},{1,17},{... | collective-permute-start | bytes 491528 | tf_op jit(solution)/shard_map/ppermute | solution.py:471
  17.1 8.6 %collective-permute-start.4 = (bf16[2,2,160,128]{3,2,1,0:T(8,128)(2,1)S(1)}, bf16[2,2,160,128]{3,2,1,0:T(8,128)(2,1)S(1)}, u32[]{:S(2)}, u32[]{:S(2)}) collective-permute-start(bf16[2,2,160,128]{3,2,1,0:T(8,128)(2,1)S(1)} %shard_map.85.refs_0_), channel_id=1, source_target_pairs={{0,24},{4,28},{8,16},{12,20},{16,8},{20,12},{24,0},{28,4},{1,25},{... | collective-permute-start | bytes 491528 | tf_op jit(solution)/shard_map/ppermute | solution.py:471
  23.1 2.0 %copy-start = (bf16[18,960,128]{2,1,0:T(8,128)(2,1)}, bf16[18,960,128]{2,1,0:T(8,128)(2,1)S(1)}, u32[]{:S(2)}) copy-start(bf16[18,960,128]{2,1,0:T(8,128)(2,1)S(1)} %get-tuple-element.40.xs) | copy-start | bytes 13271044
  25.1 2.3 %copy-start.3 = (bf16[1,2,320,128]{3,2,1,0:T(8,128)(2,1)S(1)}, bf16[1,2,320,128]{3,2,1,0:T(8,128)(2,1)}, u32[]{:S(2)}) copy-start(bf16[1,2,320,128]{3,2,1,0:T(8,128)(2,1)} %param.6) | copy-start | bytes 491524
  27.4 8.3 %collective-permute-start.14 = (bf16[16,160,128]{2,1,0:T(8,128)(2,1)S(1)}, bf16[16,160,128]{2,1,0:T(8,128)(2,1)}, u32[]{:S(2)}, u32[]{:S(2)}) collective-permute-start(bf16[16,160,128]{2,1,0:T(8,128)(2,1)S(1)} %shard_map.88.own_ref), channel_id=1, source_target_pairs={{0,4},{4,0},{8,12},{12,8},{16,20},{20,16},{24,28},{28,24},{1,5},{5... | collective-permute-start | bytes 1966088 | tf_op jit(solution)/shard_map/ppermute | solution.py:475
  27.4 2.3 %collective-permute-start.12 = (bf16[2,320,128]{2,1,0:T(8,128)(2,1)S(1)}, bf16[2,320,128]{2,1,0:T(8,128)(2,1)S(1)}, u32[]{:S(2)}, u32[]{:S(2)}) collective-permute-start(bf16[2,320,128]{2,1,0:T(8,128)(2,1)S(1)} %bitcast.11), channel_id=1, source_target_pairs={{0,4},{4,0},{8,12},{12,8},{16,20},{20,16},{24,28},{28,24},{1,5},{5... | collective-permute-start | bytes 491528 | tf_op jit(solution)/shard_map/ppermute | solution.py:475
  27.9 0.7 %collective-permute-start = (bf16[320,128]{1,0:T(8,128)(2,1)S(1)}, bf16[320,128]{1,0:T(8,128)(2,1)S(1)}, u32[]{:S(2)}, u32[]{:S(2)}) collective-permute-start(bf16[320,128]{1,0:T(8,128)(2,1)S(1)} %dynamic-slice_bitcast_fusion), channel_id=1, source_target_pairs={{4,8},{12,16},{20,24},{8,4},{16,12},{24,20},{5,9},{13,17},{21,25},... | collective-permute-start | bytes 245768 | tf_op jit(solution)/shard_map/ppermute | solution.py:482
  30.9 9.9 %collective-permute-start.13 = (f32[8,128]{1,0:T(8,128)S(1)}, f32[8,128]{1,0:T(8,128)S(1)}, u32[]{:S(2)}, u32[]{:S(2)}) collective-permute-start(f32[8,128]{1,0:T(8,128)S(1)} %get-tuple-element.36), channel_id=1, source_target_pairs={{0,4},{4,0},{8,12},{12,8},{16,20},{20,16},{24,28},{28,24},{1,5},{5... | collective-permute-start | bytes 12296 | tf_op jit(solution)/shard_map/ppermute | solution.py:475
  35.7 2.3 %copy-start.1 = (bf16[18,960,128]{2,1,0:T(8,128)(2,1)S(1)}, bf16[18,960,128]{2,1,0:T(8,128)(2,1)}, u32[]{:S(2)}) copy-start(bf16[18,960,128]{2,1,0:T(8,128)(2,1)} %copy-done) | copy-start | bytes 13271044
  40.9 7.8 %collective-permute-start.15 = (f32[2,8,128]{2,1,0:T(8,128)S(1)}, f32[2,8,128]{2,1,0:T(8,128)S(1)}, u32[]{:S(2)}, u32[]{:S(2)}) collective-permute-start(f32[2,8,128]{2,1,0:T(8,128)S(1)} %pad_maximum_fusion.refs_0_), channel_id=1, source_target_pairs={{0,24},{4,28},{8,16},{12,20},{16,8},{20,12},{24,0},{28,4},{1,25},{... | collective-permute-start | bytes 24584 | tf_op jit(solution)/shard_map/ppermute | solution.py:471
  42.6 11.2 %collective-permute-start.18 = (bf16[225,128]{1,0:T(8,128)(2,1)S(1)}, bf16[225,128]{1,0:T(8,128)(2,1)S(1)}, u32[]{:S(2)}, u32[]{:S(2)}) collective-permute-start(bf16[225,128]{1,0:T(8,128)(2,1)S(1)} %get-tuple-element.46), channel_id=1, source_target_pairs={{0,3},{1,2},{2,1},{3,0},{4,7},{5,6},{6,5},{7,4},{8,11},{9,10},{10,... | collective-permute-start | bytes 172808 | tf_op jit(solution)/shard_map/ppermute | solution.py:555
  46.2 7.6 %collective-permute-start.19 = (bf16[225,128]{1,0:T(8,128)(2,1)S(1)}, bf16[225,128]{1,0:T(8,128)(2,1)S(1)}, u32[]{:S(2)}, u32[]{:S(2)}) collective-permute-start(bf16[225,128]{1,0:T(8,128)(2,1)S(1)} %get-tuple-element.47), channel_id=1, source_target_pairs={{0,2},{1,3},{2,0},{3,1},{4,6},{5,7},{6,4},{7,5},{8,10},{9,11},{10,... | collective-permute-start | bytes 172808 | tf_op jit(solution)/shard_map/ppermute | solution.py:555
  46.2 7.6 %collective-permute-start.20 = (bf16[225,128]{1,0:T(8,128)(2,1)S(1)}, bf16[225,128]{1,0:T(8,128)(2,1)S(1)}, u32[]{:S(2)}, u32[]{:S(2)}) collective-permute-start(bf16[225,128]{1,0:T(8,128)(2,1)S(1)} %get-tuple-element.48), channel_id=1, source_target_pairs={{0,1},{1,0},{2,3},{3,2},{4,5},{5,4},{6,7},{7,6},{8,9},{9,8},{10,11... | collective-permute-start | bytes 172808 | tf_op jit(solution)/shard_map/ppermute | solution.py:555
  47.0 3.7 %collective-permute-start.16 = (f32[2,8,128]{2,1,0:T(8,128)S(1)}, f32[2,8,128]{2,1,0:T(8,128)S(1)}, u32[]{:S(2)}, u32[]{:S(2)}) collective-permute-start(f32[2,8,128]{2,1,0:T(8,128)S(1)} %pad_maximum_fusion.refs_0_), channel_id=1, source_target_pairs={{0,8},{4,12},{8,0},{12,4},{16,24},{20,28},{24,16},{28,20},{1,9},{5... | collective-permute-start | bytes 24584 | tf_op jit(solution)/shard_map/ppermute | solution.py:471
  48.6 3.7 %collective-permute-start.17 = (f32[2,8,128]{2,1,0:T(8,128)S(1)}, f32[2,8,128]{2,1,0:T(8,128)S(1)}, u32[]{:S(2)}, u32[]{:S(2)}) collective-permute-start(f32[2,8,128]{2,1,0:T(8,128)S(1)} %pad_maximum_fusion.refs_0_), channel_id=1, source_target_pairs={{0,16},{4,20},{8,24},{12,28},{16,0},{20,4},{24,8},{28,12},{1,17},{... | collective-permute-start | bytes 24584 | tf_op jit(solution)/shard_map/ppermute | solution.py:471

commit v4 on v2

--- a/solution.py
+++ b/solution.py
@@ -187,6 +187,13 @@
             flat_ref[a, :, b * chans : (b + 1) * chans] = w_ref[a, b]
 
 
+def edge_kernel(x_ref, edge_ref, sem):
+    row = (lax.axis_index("height") & 1) * (x_ref.shape[0] - 1)
+    copy = pltpu.make_async_copy(x_ref.at[row], edge_ref, sem)
+    copy.start()
+    copy.wait()
+
+
 def halves_kernel(own_ref, near_ref, out_ref):
     half = out_ref.shape[2]
     core = lax.axis_index("height") & 1
@@ -465,18 +472,26 @@
     x_next, grad_out = x_next[0], grad_out[0]
     shape = jax.ShapeDtypeStruct
 
-    def far(own):
-        held = {0: own}
-        for k in sorted(range(2, blocks, 2), key=lambda k: -bin(k).count("1")):
-            held[k] = lax.ppermute(own, "height", pairs(blocks, k))
-        return held
+    chips = sorted(range(2, blocks, 2), key=lambda k: -bin(k).count("1"))
+    last = chips[:1]
+
+    def far(own, offsets):
+        return {k: lax.ppermute(own, "height", pairs(blocks, k)) for k in offsets}
 
     def near(own):
         return lax.ppermute(own, "height", pairs(blocks, 1))
 
-    x_far = far(x_cur[0])
-    even = (lax.axis_index("height") & 1) == 0
-    edge = lax.dynamic_index_in_dim(x_next, jnp.where(even, 0, rows - 1), 0, keepdims=False)
+    x_far = {0: x_cur[0]} | far(x_cur[0], chips)
+    edge = pl.pallas_call(
+        edge_kernel,
+        out_shape=shape((chans, width), BF16),
+        in_specs=[pl.BlockSpec(memory_space=pltpu.HBM)],
+        out_specs=vmem(1)[0],
+        scratch_shapes=[pltpu.SemaphoreType.DMA],
+        compiler_params=params(),
+        cost_estimate=pl.CostEstimate(flops=image * flops, bytes_accessed=0, transcendentals=0),
+        name="edge",
+    )(pltpu.with_memory_space_constraint(x_next, pltpu.HBM))
     next_near = near(x_next)
     swaps = [(i, i + 1) for i in range(1, blocks - 1, 2)]
     edge = lax.ppermute(edge, "height", swaps + [(j, i) for i, j in swaps])
@@ -484,7 +499,7 @@
     g_pair = call(
         halves_kernel, shape((2, rows, half, width), BF16), (grad_out, g_near), flops=image * flops
     )
-    g_far = far(g_pair)
+    g_far = {0: g_pair} | far(g_pair, chips)
     gain = jnp.broadcast_to(gamma[:, None], (chans, width))
     shift = jnp.broadcast_to(beta[:, None], (chans, width))
     w_flat = call(weights_kernel, shape((3, chans, 3 * chans), BF16), (kernel,))
@@ -534,7 +549,7 @@
     )
     gz_other = near(gz_own)
     stat_pair, gz_own = lax.optimization_barrier((stat_pair, gz_own))
-    stat_far = far(stat_pair)
+    stat_far = far(stat_pair, last)
     results = call(
         filter_kernel,
         (shape((piece, LANES), F32),)
@@ -555,6 +570,7 @@
     total = results[0]
     for s in range(groups_dp - 1, 0, -1):
         total = total + lax.ppermute(results[s], "dp", pairs(groups_dp, s)).astype(F32)
+    stat_far |= far(stat_pair, [k for k in chips if k not in last])
     grad_x = call(
         grad_x_kernel,
         shape((rows, chans, width), BF16),
@@ -565,7 +581,7 @@
     y_next = call(
         next_out_kernel,
         shape((rows, chans, width), BF16),
-        (*stat_far.values(), z_next, gain, shift),
+        (stat_pair, *stat_far.values(), z_next, gain, shift),
         flops=rows * flops // 4,
         rows=rows,
         count=count,

time: 46.7 us -> 46.1 us (0.987)
  local copies, waits for them, and re-layouts: 2.37 us -> 0.28 us
  Pallas kernels: 12.8 us -> 13.8 us
  starting transfers between devices: 18.9 us -> 19.4 us
    unnamed x12, local copies, waits for them, and re-layouts: 2.17 us -> 0.09 us
    pallas_call x0 -> x1, Pallas kernels: none -> 1.05 us  [gathered(): pl.pallas_call(edge_kernel, out_shape=shape((chans, width), BF16), in_spe...]
    ppermute x9, starting transfers between devices: 11.4 us -> 12 us  [far(): return {k: lax.ppermute(own, 'height', pairs(blocks, k)) for k in offsets}]
  transfers between devices with their start and end apart: 21 -> 21, of which waited for: 5 -> 5; matrix products, arithmetic and copies ran while one was open for 0% -> 0% of each run, Pallas kernels for 24% -> 26%
where the time goes in v4:
time: 46.1 us; the launch traced here: 45.9 us
  starting transfers between devices  19.4 us (42%)
  Pallas kernels  13.8 us (30%)
  waiting for transfers between devices  10.9 us (24%)
  between operations  0.81 us (2%)
  other arithmetic  0.68 us (1%)
    pallas_call x8, Pallas kernels, call(): pl.pallas_call(functools.partial(kernel, **static), out_shape=out_shape,...  12.8 us
    ppermute x9, starting transfers between devices, far(): return {k: lax.ppermute(own, 'height', pairs(blocks, k)) for k in offsets}  12 us
    ppermute x9, waiting for transfers between devices, far(): return {k: lax.ppermute(own, 'height', pairs(blocks, k)) for k in offsets}  8.22 us
    ppermute x3, starting transfers between devices, gathered(): lax.ppermute(results[s], 'dp', pairs(groups_dp, s)).astype(F32)  4.45 us
    ppermute x8, starting transfers between devices, near(): return lax.ppermute(own, 'height', pairs(blocks, 1))  2.16 us
    ppermute x8, waiting for transfers between devices, near(): return lax.ppermute(own, 'height', pairs(blocks, 1))  1.61 us
    ppermute x3, waiting for transfers between devices, gathered(): lax.ppermute(results[s], 'dp', pairs(groups_dp, s)).astype(F32)  1.09 us
    pallas_call x1, Pallas kernels, gathered(): pl.pallas_call(edge_kernel, out_shape=shape((chans, width), BF16), in_spe...  1.05 us
  transfers between devices with their start and end apart: 21, of which 5 were waited for; matrix products, arithmetic and copies ran while one was open for 0% of the time, Pallas kernels for 26%

profile of v4, /device:TPU:0, one launch (start us, length us, event | category | flops | bytes accessed | tf_op | source)
XLA Modules:
  0.0 45.9 jit_solution(5367627504557719822)
XLA Ops:
  0.6 3.0 %collective-permute-start.2 = (bf16[2,320,128]{2,1,0:T(8,128)(2,1)}, bf16[2,320,128]{2,1,0:T(8,128)(2,1)S(1)}, u32[]{:S(2)}, u32[]{:S(2)}) collective-permute-start(bf16[2,320,128]{2,1,0:T(8,128)(2,1)} %bitcast.15), channel_id=1, source_target_pairs={{0,8},{4,12},{8,0},{12,4},{16,24},{20,28},{24,16},{28,20},{1,9},{5... | collective-permute-start | bytes 491528 | tf_op jit(solution)/shard_map/ppermute | solution.py:479
  3.7 1.5 %collective-permute-start.3 = (bf16[2,320,128]{2,1,0:T(8,128)(2,1)}, bf16[2,320,128]{2,1,0:T(8,128)(2,1)S(1)}, u32[]{:S(2)}, u32[]{:S(2)}) collective-permute-start(bf16[2,320,128]{2,1,0:T(8,128)(2,1)} %bitcast.16), channel_id=1, source_target_pairs={{0,16},{4,20},{8,24},{12,28},{16,0},{20,4},{24,8},{28,12},{1,17},{... | collective-permute-start | bytes 491528 | tf_op jit(solution)/shard_map/ppermute | solution.py:479
  5.2 0.0 collective-permute-start.4
  5.2 0.0 collective-permute-start.5
  5.2 0.5 %collective-permute-start.1 = (bf16[2,320,128]{2,1,0:T(8,128)(2,1)}, bf16[2,320,128]{2,1,0:T(8,128)(2,1)S(1)}, u32[]{:S(2)}, u32[]{:S(2)}) collective-permute-start(bf16[2,320,128]{2,1,0:T(8,128)(2,1)} %bitcast.9), channel_id=1, source_target_pairs={{0,4},{4,0},{8,12},{12,8},{16,20},{20,16},{24,28},{28,24},{1,5},{5... | collective-permute-start | bytes 491528 | tf_op jit(solution)/shard_map/ppermute | solution.py:482
  5.7 1.1 %edge.1 = bf16[320,128]{1,0:T(8,128)(2,1)S(1)} custom-call(bf16[2,320,128]{2,1,0:T(8,128)(2,1)} %bitcast.10), custom_call_target="tpu_custom_call" | custom-call | flops 3774873600 | tf_op jit(solution)/shard_map/edge/pallas_call | solution.py:485
  6.8 0.1 copy-done
  6.8 0.0 copy-start.2
  6.8 0.4 shard_map.85.w_ref.refs_8_
  7.2 0.0 copy-start.4
  7.2 0.0 copy-start.5
  7.2 0.0 copy-start.3
  7.3 0.0 copy-start.1
  7.3 0.0 collective-permute-done.5.near_ref
  7.3 0.8 %collective-permute-start = (bf16[320,128]{1,0:T(8,128)(2,1)S(1)}, bf16[320,128]{1,0:T(8,128)(2,1)S(1)}, u32[]{:S(2)}, u32[]{:S(2)}) collective-permute-start(bf16[320,128]{1,0:T(8,128)(2,1)S(1)} %edge.1), channel_id=1, source_target_pairs={{4,8},{12,16},{20,24},{8,4},{16,12},{24,20},{5,9},{13,17},{21,25},... | collective-permute-start | bytes 245768 | tf_op jit(solution)/shard_map/ppermute | solution.py:497
  8.1 0.0 copy-done.2
  8.1 0.8 %collective-permute-done.2.refs_2_ = bf16[2,320,128]{2,1,0:T(8,128)(2,1)S(1)} collective-permute-done((bf16[2,320,128]{2,1,0:T(8,128)(2,1)}, bf16[2,320,128]{2,1,0:T(8,128)(2,1)S(1)}, u32[]{:S(2)}, u32[]{:S(2)}) %collective-permute-start.2) | collective-permute-done | bytes 163872 | tf_op jit(solution)/shard_map/ppermute | solution.py:479
  8.9 4.1 %collective-permute-done.3.refs_4_ = bf16[2,320,128]{2,1,0:T(8,128)(2,1)S(1)} collective-permute-done((bf16[2,320,128]{2,1,0:T(8,128)(2,1)}, bf16[2,320,128]{2,1,0:T(8,128)(2,1)S(1)}, u32[]{:S(2)}, u32[]{:S(2)}) %collective-permute-start.3) | collective-permute-done | bytes 163872 | tf_op jit(solution)/shard_map/ppermute | solution.py:479
  13.0 0.0 collective-permute-done.4.refs_6_
  13.0 0.0 copy-done.4
  13.0 0.1 broadcast_in_dim.8.refs_6_.refs_5_
  13.2 0.0 copy-done.5
  13.2 0.1 broadcast_in_dim.9.refs_7_.refs_6_
  13.3 0.0 copy-done.3
  13.3 0.1 collective-permute-start.10
  13.4 0.5 %collective-permute-start.11 = (bf16[2,320,128]{2,1,0:T(8,128)(2,1)S(1)}, bf16[2,320,128]{2,1,0:T(8,128)(2,1)S(1)}, u32[]{:S(2)}, u32[]{:S(2)}) collective-permute-start(bf16[2,320,128]{2,1,0:T(8,128)(2,1)S(1)} %collective-permute-done.2.refs_2_), channel_id=1, source_target_pairs={{0,4},{4,0},{8,12},{12,8},{16,20},{20,16},{24,28},{28,24},{1,5},{5... | collective-permute-start | bytes 491528 | tf_op jit(solution)/shard_map/ppermute | solution.py:482
  13.9 0.1 collective-permute-start.12
  13.9 0.0 collective-permute-done.edge_ref
  13.9 0.4 collective-permute-start.13
  14.4 0.0 collective-permute-done.1.near_ref
  14.4 2.4 %collective-permute-start.7 = (bf16[2,2,160,128]{3,2,1,0:T(8,128)(2,1)S(1)}, bf16[2,2,160,128]{3,2,1,0:T(8,128)(2,1)S(1)}, u32[]{:S(2)}, u32[]{:S(2)}) collective-permute-start(bf16[2,2,160,128]{3,2,1,0:T(8,128)(2,1)S(1)} %shard_map.86.refs_0_), channel_id=1, source_target_pairs={{0,8},{4,12},{8,0},{12,4},{16,24},{20,28},{24,16},{28,20},{1,9},{5... | collective-permute-start | bytes 491528 | tf_op jit(solution)/shard_map/ppermute | solution.py:479
  16.8 0.0 copy-done.1
  16.8 1.2 %shard_map.87 = (f32[2,320,128]{2,1,0:T(8,128)S(1)}, f32[8,128]{1,0:T(8,128)S(1)}) custom-call(bf16[320,128]{1,0:T(8,128)(2,1)S(1)} %collective-permute-done.edge_ref, bf16[2,320,128]{2,1,0:T(8,128)(2,1)S(1)} %collective-permute-done.1.near_ref, bf16[2,320,128]{2,1,0:T(8,128)(2,1)S(1)} %bitcast.11, bf16[3,320,960]{2,1,0:T(8,128)(2,1)S(1)} %shard_map.85.w_ref.refs_8_), custom_call_target="tpu_custom_call" | custom-call | flops 471859200 | tf_op jit(solution)/shard_map/pallas_call | solution.py:450
  17.9 0.0 collective-permute-done.10.refs_1_
  17.9 0.1 collective-permute-start.8
  18.1 0.0 collective-permute-done.11.refs_3_
  18.1 1.4 %collective-permute-start.9 = (bf16[2,2,160,128]{3,2,1,0:T(8,128)(2,1)S(1)}, bf16[2,2,160,128]{3,2,1,0:T(8,128)(2,1)S(1)}, u32[]{:S(2)}, u32[]{:S(2)}) collective-permute-start(bf16[2,2,160,128]{3,2,1,0:T(8,128)(2,1)S(1)} %shard_map.86.refs_0_), channel_id=1, source_target_pairs={{0,24},{4,28},{8,16},{12,20},{16,8},{20,12},{24,0},{28,4},{1,25},{... | collective-permute-start | bytes 491528 | tf_op jit(solution)/shard_map/ppermute | solution.py:479
  19.5 0.0 collective-permute-done.12.refs_5_
  19.5 0.0 collective-permute-done.13.refs_7_
  19.5 4.6 %shard_map.88 = (bf16[18,960,128]{2,1,0:T(8,128)(2,1)S(1)}, f32[16,160,128]{2,1,0:T(8,128)S(1)}, f32[2,160,128]{2,1,0:T(8,128)S(1)}) custom-call(bf16[2,320,128]{2,1,0:T(8,128)(2,1)S(1)} %bitcast.19, bf16[2,320,128]{2,1,0:T(8,128)(2,1)S(1)} %collective-permute-done.10.refs_1_, bf16[2,320,128]{2,1,0:T(8,128)(2,1)S(1)} %collective-permute-done.2.refs_2_, ...), custom_call_target="tpu_custom_call" | custom-call | flops 1887436800 | tf_op jit(solution)/shard_map/pallas_call | solution.py:450
  24.0 0.0 collective-permute-done.7.refs_1_
  24.1 3.3 %collective-permute-done.8.refs_2_ = bf16[2,2,160,128]{3,2,1,0:T(8,128)(2,1)S(1)} collective-permute-done((bf16[2,2,160,128]{3,2,1,0:T(8,128)(2,1)S(1)}, bf16[2,2,160,128]{3,2,1,0:T(8,128)(2,1)S(1)}, u32[]{:S(2)}, u32[]{:S(2)}) %collective-permute-start.8) | collective-permute-done | bytes 163872 | tf_op jit(solution)/shard_map/ppermute | solution.py:479
  27.3 0.0 collective-permute-done.9.refs_3_
  27.3 1.7 %shard_map.89.own_ref = bf16[16,160,128]{2,1,0:T(8,128)(2,1)S(1)} custom-call(bf16[2,2,160,128]{3,2,1,0:T(8,128)(2,1)S(1)} %shard_map.86.refs_0_, bf16[2,2,160,128]{3,2,1,0:T(8,128)(2,1)S(1)} %collective-permute-done.7.refs_1_, bf16[2,2,160,128]{3,2,1,0:T(8,128)(2,1)S(1)} %collective-permute-done.8.refs_2_, ...), custom_call_target="tpu_custom_call" | custom-call | flops 471859200 | tf_op jit(solution)/shard_map/pallas_call | solution.py:450
  29.0 0.1 collective-permute-start.17
  29.1 0.5 %collective-permute-start.6 = (f32[8,128]{1,0:T(8,128)S(1)}, f32[8,128]{1,0:T(8,128)S(1)}, u32[]{:S(2)}, u32[]{:S(2)}) collective-permute-start(f32[8,128]{1,0:T(8,128)S(1)} %get-tuple-element.32), channel_id=1, source_target_pairs={{0,4},{4,0},{8,12},{12,8},{16,20},{20,16},{24,28},{28,24},{1,5},{5... | collective-permute-start | bytes 12296 | tf_op jit(solution)/shard_map/ppermute | solution.py:482
  29.6 1.6 %collective-permute-done.6 = f32[8,128]{1,0:T(8,128)S(1)} collective-permute-done((f32[8,128]{1,0:T(8,128)S(1)}, f32[8,128]{1,0:T(8,128)S(1)}, u32[]{:S(2)}, u32[]{:S(2)}) %collective-permute-start.6) | collective-permute-done | bytes 4128 | tf_op jit(solution)/shard_map/ppermute | solution.py:482
  31.2 1.4 %collective-permute-start.14 = (f32[2,8,128]{2,1,0:T(8,128)S(1)}, f32[2,8,128]{2,1,0:T(8,128)S(1)}, u32[]{:S(2)}, u32[]{:S(2)}) collective-permute-start(f32[2,8,128]{2,1,0:T(8,128)S(1)} %pad_maximum_fusion.refs_0_), channel_id=1, source_target_pairs={{0,24},{4,28},{8,16},{12,20},{16,8},{20,12},{24,0},{28,4},{1,25},{... | collective-permute-start | bytes 24584 | tf_op jit(solution)/shard_map/ppermute | solution.py:479
  32.6 0.6 %collective-permute-start.15 = (f32[2,8,128]{2,1,0:T(8,128)S(1)}, f32[2,8,128]{2,1,0:T(8,128)S(1)}, u32[]{:S(2)}, u32[]{:S(2)}) collective-permute-start(f32[2,8,128]{2,1,0:T(8,128)S(1)} %pad_maximum_fusion.refs_0_), channel_id=1, source_target_pairs={{0,8},{4,12},{8,0},{12,4},{16,24},{20,28},{24,16},{28,20},{1,9},{5... | collective-permute-start | bytes 24584 | tf_op jit(solution)/shard_map/ppermute | solution.py:479
  33.2 1.4 %collective-permute-start.16 = (f32[2,8,128]{2,1,0:T(8,128)S(1)}, f32[2,8,128]{2,1,0:T(8,128)S(1)}, u32[]{:S(2)}, u32[]{:S(2)}) collective-permute-start(f32[2,8,128]{2,1,0:T(8,128)S(1)} %pad_maximum_fusion.refs_0_), channel_id=1, source_target_pairs={{0,16},{4,20},{8,24},{12,28},{16,0},{20,4},{24,8},{28,12},{1,17},{... | collective-permute-start | bytes 24584 | tf_op jit(solution)/shard_map/ppermute | solution.py:479
  34.7 0.0 collective-permute-done.17.other_ref
  34.7 1.8 %shard_map.91 = (f32[225,128]{1,0:T(8,128)S(1)}, bf16[225,128]{1,0:T(8,128)(2,1)S(1)}, bf16[225,128]{1,0:T(8,128)(2,1)S(1)}, bf16[225,128]{1,0:T(8,128)(2,1)S(1)}, bf16[4,320,128]{2,1,0:T(8,128)(2,1)S(1)}) custom-call(bf16[16,160,128]{2,1,0:T(8,128)(2,1)S(1)} %shard_map.89.own_ref, bf16[16,160,128]{2,1,0:T(8,128)(2,1)S(1)} %collective-permute-done.17.other_ref, ...), custom_call_target="tpu_custom_call" | custom-call | flops 943718400 | tf_op jit(solution)/shard_map/pallas_call | solution.py:450
  36.4 3.7 %collective-permute-start.18 = (bf16[225,128]{1,0:T(8,128)(2,1)S(1)}, bf16[225,128]{1,0:T(8,128)(2,1)S(1)}, u32[]{:S(2)}, u32[]{:S(2)}) collective-permute-start(bf16[225,128]{1,0:T(8,128)(2,1)S(1)} %get-tuple-element.56), channel_id=1, source_target_pairs={{0,3},{1,2},{2,1},{3,0},{4,7},{5,6},{6,5},{7,4},{8,11},{9,10},{10,... | collective-permute-start | bytes 172808 | tf_op jit(solution)/shard_map/ppermute | solution.py:572
  40.1 0.0 collective-permute-start.19
  40.1 0.0 collective-permute-done.14.refs_1_
  40.1 0.8 %collective-permute-start.20 = (bf16[225,128]{1,0:T(8,128)(2,1)S(1)}, bf16[225,128]{1,0:T(8,128)(2,1)S(1)}, u32[]{:S(2)}, u32[]{:S(2)}) collective-permute-start(bf16[225,128]{1,0:T(8,128)(2,1)S(1)} %get-tuple-element.58), channel_id=1, source_target_pairs={{0,1},{1,0},{2,3},{3,2},{4,5},{5,4},{6,7},{7,6},{8,9},{9,8},{10,11... | collective-permute-start | bytes 172808 | tf_op jit(solution)/shard_map/ppermute | solution.py:572
  40.9 0.0 collective-permute-done.15.refs_2_
  40.9 0.0 collective-permute-done.16.refs_3_
  40.9 1.5 %shard_map.90 = bf16[2,320,128]{2,1,0:T(8,128)(2,1)} custom-call(f32[2,8,128]{2,1,0:T(8,128)S(1)} %pad_maximum_fusion.refs_0_, f32[2,8,128]{2,1,0:T(8,128)S(1)} %collective-permute-done.14.refs_1_, f32[2,8,128]{2,1,0:T(8,128)S(1)} %collective-permute-done.15.refs_2_, f32[2,8,128]{2,1,0:T(8,128)S(1)} %collective-permute-done.16.refs_3_, ...), custom_call_target="tpu_custom_call" | custom-call | flops 117964800 | tf_op jit(solution)/shard_map/pallas_call | solution.py:450
  42.4 1.7 %shard_map.92 = bf16[2,320,128]{2,1,0:T(8,128)(2,1)} custom-call(bf16[4,320,128]{2,1,0:T(8,128)(2,1)S(1)} %get-tuple-element.54.gz_ref, bf16[3,320,960]{2,1,0:T(8,128)(2,1)S(1)} %shard_map.85.w_ref.refs_8_), custom_call_target="tpu_custom_call" | custom-call | flops 471859200 | tf_op jit(solution)/shard_map/pallas_call | solution.py:450
  44.1 0.0 collective-permute-done.18
  44.1 1.1 %collective-permute-done.19 = bf16[225,128]{1,0:T(8,128)(2,1)S(1)} collective-permute-done((bf16[225,128]{1,0:T(8,128)(2,1)S(1)}, bf16[225,128]{1,0:T(8,128)(2,1)S(1)}, u32[]{:S(2)}, u32[]{:S(2)}) %collective-permute-start.19) | collective-permute-done | bytes 57632 | tf_op jit(solution)/shard_map/ppermute | solution.py:572
  45.2 0.0 collective-permute-done.20
  45.2 0.7 %add_bitcast_fusion = f32[28800]{0:T(1024)} fusion(bf16[225,128]{1,0:T(8,128)(2,1)S(1)} %collective-permute-done.20, bf16[225,128]{1,0:T(8,128)(2,1)S(1)} %collective-permute-done.19, f32[225,128]{1,0:T(8,128)S(1)} %get-tuple-element.55, bf16[225,128]{1,0:T(8,128)(2,1)S(1)} %collective-permute-done.18), kind=kLoop, calls=%fused_computation | loop fusion | flops 172800 | bytes 403200 | tf_op jit(solution)/shard_map/reshape | solution.py:589
  (3 shorter events, 0.0 us)
Async XLA Ops:
  0.6 8.3 %collective-permute-start.2 = (bf16[2,320,128]{2,1,0:T(8,128)(2,1)}, bf16[2,320,128]{2,1,0:T(8,128)(2,1)S(1)}, u32[]{:S(2)}, u32[]{:S(2)}) collective-permute-start(bf16[2,320,128]{2,1,0:T(8,128)(2,1)} %bitcast.15), channel_id=1, source_target_pairs={{0,8},{4,12},{8,0},{12,4},{16,24},{20,28},{24,16},{28,20},{1,9},{5... | collective-permute-start | bytes 491528 | tf_op jit(solution)/shard_map/ppermute | solution.py:479
  3.7 9.4 %collective-permute-start.3 = (bf16[2,320,128]{2,1,0:T(8,128)(2,1)}, bf16[2,320,128]{2,1,0:T(8,128)(2,1)S(1)}, u32[]{:S(2)}, u32[]{:S(2)}) collective-permute-start(bf16[2,320,128]{2,1,0:T(8,128)(2,1)} %bitcast.16), channel_id=1, source_target_pairs={{0,16},{4,20},{8,24},{12,28},{16,0},{20,4},{24,8},{28,12},{1,17},{... | collective-permute-start | bytes 491528 | tf_op jit(solution)/shard_map/ppermute | solution.py:479
  5.2 7.9 %collective-permute-start.4 = (bf16[2,320,128]{2,1,0:T(8,128)(2,1)}, bf16[2,320,128]{2,1,0:T(8,128)(2,1)S(1)}, u32[]{:S(2)}, u32[]{:S(2)}) collective-permute-start(bf16[2,320,128]{2,1,0:T(8,128)(2,1)} %bitcast.17), channel_id=1, source_target_pairs={{0,24},{4,28},{8,16},{12,20},{16,8},{20,12},{24,0},{28,4},{1,25},{... | collective-permute-start | bytes 491528 | tf_op jit(solution)/shard_map/ppermute | solution.py:479
  5.2 2.1 %collective-permute-start.5 = (bf16[2,320,128]{2,1,0:T(8,128)(2,1)}, bf16[2,320,128]{2,1,0:T(8,128)(2,1)S(1)}, u32[]{:S(2)}, u32[]{:S(2)}) collective-permute-start(bf16[2,320,128]{2,1,0:T(8,128)(2,1)} %bitcast.13), channel_id=1, source_target_pairs={{0,4},{4,0},{8,12},{12,8},{16,20},{20,16},{24,28},{28,24},{1,5},{5... | collective-permute-start | bytes 491528 | tf_op jit(solution)/shard_map/ppermute | solution.py:482
  5.2 1.6 %copy-start = (bf16[3,3,320,320]{3,2,1,0:T(8,128)(2,1)S(1)}, bf16[3,3,320,320]{3,2,1,0:T(8,128)(2,1)}, u32[]{:S(2)}) copy-start(bf16[3,3,320,320]{3,2,1,0:T(8,128)(2,1)} %w_ref.1) | copy-start | bytes 5529604
  5.2 9.2 %collective-permute-start.1 = (bf16[2,320,128]{2,1,0:T(8,128)(2,1)}, bf16[2,320,128]{2,1,0:T(8,128)(2,1)S(1)}, u32[]{:S(2)}, u32[]{:S(2)}) collective-permute-start(bf16[2,320,128]{2,1,0:T(8,128)(2,1)} %bitcast.9), channel_id=1, source_target_pairs={{0,4},{4,0},{8,12},{12,8},{16,20},{20,16},{24,28},{28,24},{1,5},{5... | collective-permute-start | bytes 491528 | tf_op jit(solution)/shard_map/ppermute | solution.py:482
  6.8 1.2 %copy-start.2 = (bf16[1,2,320,128]{3,2,1,0:T(8,128)(2,1)S(1)}, bf16[1,2,320,128]{3,2,1,0:T(8,128)(2,1)}, u32[]{:S(2)}) copy-start(bf16[1,2,320,128]{3,2,1,0:T(8,128)(2,1)} %param.8) | copy-start | bytes 491524
  7.2 5.8 %copy-start.4 = (f32[320]{0:T(512)S(1)}, f32[320]{0:T(512)}, u32[]{:S(2)}) copy-start(f32[320]{0:T(512)} %param.10) | copy-start | bytes 3844
  7.2 5.9 %copy-start.5 = (f32[320]{0:T(512)S(1)}, f32[320]{0:T(512)}, u32[]{:S(2)}) copy-start(f32[320]{0:T(512)} %param.11) | copy-start | bytes 3844
  7.2 6.0 %copy-start.3 = (bf16[1,2,320,128]{3,2,1,0:T(8,128)(2,1)S(1)}, bf16[1,2,320,128]{3,2,1,0:T(8,128)(2,1)}, u32[]{:S(2)}) copy-start(bf16[1,2,320,128]{3,2,1,0:T(8,128)(2,1)} %param.7) | copy-start | bytes 491524
  7.3 9.5 %copy-start.1 = (bf16[1,2,320,128]{3,2,1,0:T(8,128)(2,1)S(1)}, bf16[1,2,320,128]{3,2,1,0:T(8,128)(2,1)}, u32[]{:S(2)}) copy-start(bf16[1,2,320,128]{3,2,1,0:T(8,128)(2,1)} %param.6) | copy-start | bytes 491524
  7.3 6.7 %collective-permute-start = (bf16[320,128]{1,0:T(8,128)(2,1)S(1)}, bf16[320,128]{1,0:T(8,128)(2,1)S(1)}, u32[]{:S(2)}, u32[]{:S(2)}) collective-permute-start(bf16[320,128]{1,0:T(8,128)(2,1)S(1)} %edge.1), channel_id=1, source_target_pairs={{4,8},{12,16},{20,24},{8,4},{16,12},{24,20},{5,9},{13,17},{21,25},... | collective-permute-start | bytes 245768 | tf_op jit(solution)/shard_map/ppermute | solution.py:497
  13.3 4.7 %collective-permute-start.10 = (bf16[2,320,128]{2,1,0:T(8,128)(2,1)S(1)}, bf16[2,320,128]{2,1,0:T(8,128)(2,1)S(1)}, u32[]{:S(2)}, u32[]{:S(2)}) collective-permute-start(bf16[2,320,128]{2,1,0:T(8,128)(2,1)S(1)} %bitcast.18), channel_id=1, source_target_pairs={{0,4},{4,0},{8,12},{12,8},{16,20},{20,16},{24,28},{28,24},{1,5},{5... | collective-permute-start | bytes 491528 | tf_op jit(solution)/shard_map/ppermute | solution.py:482
  13.4 4.7 %collective-permute-start.11 = (bf16[2,320,128]{2,1,0:T(8,128)(2,1)S(1)}, bf16[2,320,128]{2,1,0:T(8,128)(2,1)S(1)}, u32[]{:S(2)}, u32[]{:S(2)}) collective-permute-start(bf16[2,320,128]{2,1,0:T(8,128)(2,1)S(1)} %collective-permute-done.2.refs_2_), channel_id=1, source_target_pairs={{0,4},{4,0},{8,12},{12,8},{16,20},{20,16},{24,28},{28,24},{1,5},{5... | collective-permute-start | bytes 491528 | tf_op jit(solution)/shard_map/ppermute | solution.py:482
  13.9 5.6 %collective-permute-start.12 = (bf16[2,320,128]{2,1,0:T(8,128)(2,1)S(1)}, bf16[2,320,128]{2,1,0:T(8,128)(2,1)S(1)}, u32[]{:S(2)}, u32[]{:S(2)}) collective-permute-start(bf16[2,320,128]{2,1,0:T(8,128)(2,1)S(1)} %collective-permute-done.3.refs_4_), channel_id=1, source_target_pairs={{0,4},{4,0},{8,12},{12,8},{16,20},{20,16},{24,28},{28,24},{1,5},{5... | collective-permute-start | bytes 491528 | tf_op jit(solution)/shard_map/ppermute | solution.py:482
  13.9 5.5 %collective-permute-start.13 = (bf16[2,320,128]{2,1,0:T(8,128)(2,1)S(1)}, bf16[2,320,128]{2,1,0:T(8,128)(2,1)S(1)}, u32[]{:S(2)}, u32[]{:S(2)}) collective-permute-start(bf16[2,320,128]{2,1,0:T(8,128)(2,1)S(1)} %collective-permute-done.4.refs_6_), channel_id=1, source_target_pairs={{0,4},{4,0},{8,12},{12,8},{16,20},{20,16},{24,28},{28,24},{1,5},{5... | collective-permute-start | bytes 491528 | tf_op jit(solution)/shard_map/ppermute | solution.py:482
  14.4 9.7 %collective-permute-start.7 = (bf16[2,2,160,128]{3,2,1,0:T(8,128)(2,1)S(1)}, bf16[2,2,160,128]{3,2,1,0:T(8,128)(2,1)S(1)}, u32[]{:S(2)}, u32[]{:S(2)}) collective-permute-start(bf16[2,2,160,128]{3,2,1,0:T(8,128)(2,1)S(1)} %shard_map.86.refs_0_), channel_id=1, source_target_pairs={{0,8},{4,12},{8,0},{12,4},{16,24},{20,28},{24,16},{28,20},{1,9},{5... | collective-permute-start | bytes 491528 | tf_op jit(solution)/shard_map/ppermute | solution.py:479
  17.9 9.4 %collective-permute-start.8 = (bf16[2,2,160,128]{3,2,1,0:T(8,128)(2,1)S(1)}, bf16[2,2,160,128]{3,2,1,0:T(8,128)(2,1)S(1)}, u32[]{:S(2)}, u32[]{:S(2)}) collective-permute-start(bf16[2,2,160,128]{3,2,1,0:T(8,128)(2,1)S(1)} %shard_map.86.refs_0_), channel_id=1, source_target_pairs={{0,16},{4,20},{8,24},{12,28},{16,0},{20,4},{24,8},{28,12},{1,17},{... | collective-permute-start | bytes 491528 | tf_op jit(solution)/shard_map/ppermute | solution.py:479
  18.1 9.3 %collective-permute-start.9 = (bf16[2,2,160,128]{3,2,1,0:T(8,128)(2,1)S(1)}, bf16[2,2,160,128]{3,2,1,0:T(8,128)(2,1)S(1)}, u32[]{:S(2)}, u32[]{:S(2)}) collective-permute-start(bf16[2,2,160,128]{3,2,1,0:T(8,128)(2,1)S(1)} %shard_map.86.refs_0_), channel_id=1, source_target_pairs={{0,24},{4,28},{8,16},{12,20},{16,8},{20,12},{24,0},{28,4},{1,25},{... | collective-permute-start | bytes 491528 | tf_op jit(solution)/shard_map/ppermute | solution.py:479
  29.0 5.7 %collective-permute-start.17 = (bf16[16,160,128]{2,1,0:T(8,128)(2,1)S(1)}, bf16[16,160,128]{2,1,0:T(8,128)(2,1)S(1)}, u32[]{:S(2)}, u32[]{:S(2)}) collective-permute-start(bf16[16,160,128]{2,1,0:T(8,128)(2,1)S(1)} %shard_map.89.own_ref), channel_id=1, source_target_pairs={{0,4},{4,0},{8,12},{12,8},{16,20},{20,16},{24,28},{28,24},{1,5},{5... | collective-permute-start | bytes 1966088 | tf_op jit(solution)/shard_map/ppermute | solution.py:482
  29.1 2.1 %collective-permute-start.6 = (f32[8,128]{1,0:T(8,128)S(1)}, f32[8,128]{1,0:T(8,128)S(1)}, u32[]{:S(2)}, u32[]{:S(2)}) collective-permute-start(f32[8,128]{1,0:T(8,128)S(1)} %get-tuple-element.32), channel_id=1, source_target_pairs={{0,4},{4,0},{8,12},{12,8},{16,20},{20,16},{24,28},{28,24},{1,5},{5... | collective-permute-start | bytes 12296 | tf_op jit(solution)/shard_map/ppermute | solution.py:482
  31.2 8.9 %collective-permute-start.14 = (f32[2,8,128]{2,1,0:T(8,128)S(1)}, f32[2,8,128]{2,1,0:T(8,128)S(1)}, u32[]{:S(2)}, u32[]{:S(2)}) collective-permute-start(f32[2,8,128]{2,1,0:T(8,128)S(1)} %pad_maximum_fusion.refs_0_), channel_id=1, source_target_pairs={{0,24},{4,28},{8,16},{12,20},{16,8},{20,12},{24,0},{28,4},{1,25},{... | collective-permute-start | bytes 24584 | tf_op jit(solution)/shard_map/ppermute | solution.py:479
  32.6 8.3 %collective-permute-start.15 = (f32[2,8,128]{2,1,0:T(8,128)S(1)}, f32[2,8,128]{2,1,0:T(8,128)S(1)}, u32[]{:S(2)}, u32[]{:S(2)}) collective-permute-start(f32[2,8,128]{2,1,0:T(8,128)S(1)} %pad_maximum_fusion.refs_0_), channel_id=1, source_target_pairs={{0,8},{4,12},{8,0},{12,4},{16,24},{20,28},{24,16},{28,20},{1,9},{5... | collective-permute-start | bytes 24584 | tf_op jit(solution)/shard_map/ppermute | solution.py:479
  33.2 7.7 %collective-permute-start.16 = (f32[2,8,128]{2,1,0:T(8,128)S(1)}, f32[2,8,128]{2,1,0:T(8,128)S(1)}, u32[]{:S(2)}, u32[]{:S(2)}) collective-permute-start(f32[2,8,128]{2,1,0:T(8,128)S(1)} %pad_maximum_fusion.refs_0_), channel_id=1, source_target_pairs={{0,16},{4,20},{8,24},{12,28},{16,0},{20,4},{24,8},{28,12},{1,17},{... | collective-permute-start | bytes 24584 | tf_op jit(solution)/shard_map/ppermute | solution.py:479
  36.4 7.7 %collective-permute-start.18 = (bf16[225,128]{1,0:T(8,128)(2,1)S(1)}, bf16[225,128]{1,0:T(8,128)(2,1)S(1)}, u32[]{:S(2)}, u32[]{:S(2)}) collective-permute-start(bf16[225,128]{1,0:T(8,128)(2,1)S(1)} %get-tuple-element.56), channel_id=1, source_target_pairs={{0,3},{1,2},{2,1},{3,0},{4,7},{5,6},{6,5},{7,4},{8,11},{9,10},{10,... | collective-permute-start | bytes 172808 | tf_op jit(solution)/shard_map/ppermute | solution.py:572
  40.1 5.1 %collective-permute-start.19 = (bf16[225,128]{1,0:T(8,128)(2,1)S(1)}, bf16[225,128]{1,0:T(8,128)(2,1)S(1)}, u32[]{:S(2)}, u32[]{:S(2)}) collective-permute-start(bf16[225,128]{1,0:T(8,128)(2,1)S(1)} %get-tuple-element.57), channel_id=1, source_target_pairs={{0,2},{1,3},{2,0},{3,1},{4,6},{5,7},{6,4},{7,5},{8,10},{9,11},{10,... | collective-permute-start | bytes 172808 | tf_op jit(solution)/shard_map/ppermute | solution.py:572
  40.1 5.1 %collective-permute-start.20 = (bf16[225,128]{1,0:T(8,128)(2,1)S(1)}, bf16[225,128]{1,0:T(8,128)(2,1)S(1)}, u32[]{:S(2)}, u32[]{:S(2)}) collective-permute-start(bf16[225,128]{1,0:T(8,128)(2,1)S(1)} %get-tuple-element.58), channel_id=1, source_target_pairs={{0,1},{1,0},{2,3},{3,2},{4,5},{5,4},{6,7},{7,6},{8,9},{9,8},{10,11... | collective-permute-start | bytes 172808 | tf_op jit(solution)/shard_map/ppermute | solution.py:572

commit v5 on v4

--- a/solution.py
+++ b/solution.py
@@ -165,11 +165,13 @@
     return lax.dot_general(left, right, (dims, ((), ())), preferred_element_type=F32)
 
 
-def group_total(same, value):
-    column = jnp.sum(value, axis=1, keepdims=True)
-    wide = jnp.broadcast_to(column, value.shape)
+def group_totals(same, values, scale):
+    width = values[0].shape[1]
+    columns = [jnp.sum(value, axis=1, keepdims=True) * scale for value in values]
+    wide = jnp.concatenate([jnp.broadcast_to(c, values[0].shape) for c in columns], axis=1)
     high, mid, low = split3(wide)
-    return dot(same, high) + (dot(same, mid) + dot(same, low))
+    total = dot(same, high) + (dot(same, mid) + dot(same, low))
+    return [total[:, i * width : (i + 1) * width] for i in range(len(values))]
 
 
 def lane_tiles(size):
@@ -298,24 +300,16 @@
         parts = [total[:, i * width : (i + 1) * width] for i in range(wide)]
         for i in range(wide):
             z[row + i] = parts[i]
-        offs = [part - (parts[0] if start else z[0]) for part in parts]
-        sums = functools.reduce(jnp.add, offs)
-        squares = functools.reduce(jnp.add, [off * off for off in offs])
+        sums = functools.reduce(jnp.add, parts)
+        squares = functools.reduce(jnp.add, [part * part for part in parts])
         lane[0] = sums if start else lane[0] + sums
         lane[1] = squares if start else lane[1] + squares
 
     conv(0, True)
     lax.fori_loop(1, image // wide, lambda p, carry: conv(p) or carry, 0)
-
-    same = same_group(half, chans)
-    middle = lane[0] * (1.0 / image)
-    spread = lane[1] - middle * lane[0]
-    middle = z[0] + middle
-    mean = group_total(same, middle) * (float(image) / count)
+    mean, square = group_totals(same_group(half, chans), (lane[0], lane[1]), 1.0 / count)
     norm[0] = mean
-    apart = middle - mean
-    var = group_total(same, spread + apart * apart * float(image)) * (1.0 / count)
-    norm[1] = lax.rsqrt(var + eps)
+    norm[1] = lax.rsqrt(square - mean * mean + eps)
 
 
 def pull_kernel(*refs, blocks, rows, count):
@@ -354,9 +348,7 @@
         return carry
 
     lax.fori_loop(0, half // step, pulled, 0)
-    same = same_group(half, chans)
-    coef[0] = group_total(same, coef[0]) * (1.0 / count)
-    coef[1] = group_total(same, coef[1]) * (1.0 / count)
+    coef[0], coef[1] = group_totals(same_group(half, chans), (coef[0], coef[1]), 1.0 / count)
 
     def rounded(i, carry):
         at = pl.ds(pl.multiple_of(i * step, step), step)
@@ -473,7 +465,6 @@
     shape = jax.ShapeDtypeStruct
 
     chips = sorted(range(2, blocks, 2), key=lambda k: -bin(k).count("1"))
-    last = chips[:1]
 
     def far(own, offsets):
         return {k: lax.ppermute(own, "height", pairs(blocks, k)) for k in offsets}
@@ -549,7 +540,7 @@
     )
     gz_other = near(gz_own)
     stat_pair, gz_own = lax.optimization_barrier((stat_pair, gz_own))
-    stat_far = far(stat_pair, last)
+    stat_far = far(stat_pair, chips)
     results = call(
         filter_kernel,
         (shape((piece, LANES), F32),)
@@ -570,7 +561,6 @@
     total = results[0]
     for s in range(groups_dp - 1, 0, -1):
         total = total + lax.ppermute(results[s], "dp", pairs(groups_dp, s)).astype(F32)
-    stat_far |= far(stat_pair, [k for k in chips if k not in last])
     grad_x = call(
         grad_x_kernel,
         shape((rows, chans, width), BF16),

time: 46.1 us -> 46 us (level)
  Pallas kernels: 13.8 us -> 13.2 us
  waiting for transfers between devices: 10.9 us -> 11.5 us
    pallas_call x8, Pallas kernels: 12.8 us -> 12.1 us  [call(): pl.pallas_call(functools.partial(kernel, **static), out_shape=out_shape,...]
    ppermute x9, waiting for transfers between devices: 8.22 us -> 8.77 us  [far(): return {k: lax.ppermute(own, 'height', pairs(blocks, k)) for k in offsets}]
  transfers between devices with their start and end apart: 21 -> 21, of which waited for: 5 -> 5; matrix products, arithmetic and copies ran while one was open for 0% -> 0% of each run, Pallas kernels for 26% -> 25%
where the time goes in v5:
time: 46 us; the launch traced here: 45.8 us
  starting transfers between devices  19.4 us (42%)
  Pallas kernels  13.2 us (29%)
  waiting for transfers between devices  11.5 us (25%)
  between operations  0.81 us (2%)
  other arithmetic  0.68 us (1%)
    pallas_call x8, Pallas kernels, call(): pl.pallas_call(functools.partial(kernel, **static), out_shape=out_shape,...  12.1 us
    ppermute x9, starting transfers between devices, far(): return {k: lax.ppermute(own, 'height', pairs(blocks, k)) for k in offsets}  12 us
    ppermute x9, waiting for transfers between devices, far(): return {k: lax.ppermute(own, 'height', pairs(blocks, k)) for k in offsets}  8.77 us
    ppermute x3, starting transfers between devices, gathered(): lax.ppermute(results[s], 'dp', pairs(groups_dp, s)).astype(F32)  4.45 us
    ppermute x8, starting transfers between devices, near(): return lax.ppermute(own, 'height', pairs(blocks, 1))  2.16 us
    ppermute x8, waiting for transfers between devices, near(): return lax.ppermute(own, 'height', pairs(blocks, 1))  1.61 us
    ppermute x3, waiting for transfers between devices, gathered(): lax.ppermute(results[s], 'dp', pairs(groups_dp, s)).astype(F32)  1.09 us
    pallas_call x1, Pallas kernels, gathered(): pl.pallas_call(edge_kernel, out_shape=shape((chans, width), BF16), in_spe...  1.05 us
  transfers between devices with their start and end apart: 21, of which 5 were waited for; matrix products, arithmetic and copies ran while one was open for 0% of the time, Pallas kernels for 25%

profile of v5, /device:TPU:0, one launch (start us, length us, event | category | flops | bytes accessed | tf_op | source)
XLA Modules:
  0.0 45.8 jit_solution(9275770251389488436)
XLA Ops:
  0.6 3.0 %collective-permute-start.2 = (bf16[2,320,128]{2,1,0:T(8,128)(2,1)}, bf16[2,320,128]{2,1,0:T(8,128)(2,1)S(1)}, u32[]{:S(2)}, u32[]{:S(2)}) collective-permute-start(bf16[2,320,128]{2,1,0:T(8,128)(2,1)} %bitcast.15), channel_id=1, source_target_pairs={{0,8},{4,12},{8,0},{12,4},{16,24},{20,28},{24,16},{28,20},{1,9},{5... | collective-permute-start | bytes 491528 | tf_op jit(solution)/shard_map/ppermute | solution.py:470
  3.7 1.5 %collective-permute-start.3 = (bf16[2,320,128]{2,1,0:T(8,128)(2,1)}, bf16[2,320,128]{2,1,0:T(8,128)(2,1)S(1)}, u32[]{:S(2)}, u32[]{:S(2)}) collective-permute-start(bf16[2,320,128]{2,1,0:T(8,128)(2,1)} %bitcast.16), channel_id=1, source_target_pairs={{0,16},{4,20},{8,24},{12,28},{16,0},{20,4},{24,8},{28,12},{1,17},{... | collective-permute-start | bytes 491528 | tf_op jit(solution)/shard_map/ppermute | solution.py:470
  5.2 0.0 collective-permute-start.4
  5.2 0.0 collective-permute-start.5
  5.2 0.5 %collective-permute-start.1 = (bf16[2,320,128]{2,1,0:T(8,128)(2,1)}, bf16[2,320,128]{2,1,0:T(8,128)(2,1)S(1)}, u32[]{:S(2)}, u32[]{:S(2)}) collective-permute-start(bf16[2,320,128]{2,1,0:T(8,128)(2,1)} %bitcast.9), channel_id=1, source_target_pairs={{0,4},{4,0},{8,12},{12,8},{16,20},{20,16},{24,28},{28,24},{1,5},{5... | collective-permute-start | bytes 491528 | tf_op jit(solution)/shard_map/ppermute | solution.py:473
  5.7 1.1 %edge.1 = bf16[320,128]{1,0:T(8,128)(2,1)S(1)} custom-call(bf16[2,320,128]{2,1,0:T(8,128)(2,1)} %bitcast.10), custom_call_target="tpu_custom_call" | custom-call | flops 3774873600 | tf_op jit(solution)/shard_map/edge/pallas_call | solution.py:476
  6.8 0.1 copy-done
  6.8 0.0 copy-start.2
  6.8 0.4 shard_map.85.w_ref.refs_8_
  7.2 0.0 copy-start.4
  7.2 0.0 copy-start.5
  7.2 0.0 copy-start.3
  7.3 0.0 copy-start.1
  7.3 0.0 collective-permute-done.5.near_ref
  7.3 0.8 %collective-permute-start = (bf16[320,128]{1,0:T(8,128)(2,1)S(1)}, bf16[320,128]{1,0:T(8,128)(2,1)S(1)}, u32[]{:S(2)}, u32[]{:S(2)}) collective-permute-start(bf16[320,128]{1,0:T(8,128)(2,1)S(1)} %edge.1), channel_id=1, source_target_pairs={{4,8},{12,16},{20,24},{8,4},{16,12},{24,20},{5,9},{13,17},{21,25},... | collective-permute-start | bytes 245768 | tf_op jit(solution)/shard_map/ppermute | solution.py:488
  8.1 0.0 copy-done.2
  8.1 0.8 %collective-permute-done.2.refs_2_ = bf16[2,320,128]{2,1,0:T(8,128)(2,1)S(1)} collective-permute-done((bf16[2,320,128]{2,1,0:T(8,128)(2,1)}, bf16[2,320,128]{2,1,0:T(8,128)(2,1)S(1)}, u32[]{:S(2)}, u32[]{:S(2)}) %collective-permute-start.2) | collective-permute-done | bytes 163872 | tf_op jit(solution)/shard_map/ppermute | solution.py:470
  8.9 4.1 %collective-permute-done.3.refs_4_ = bf16[2,320,128]{2,1,0:T(8,128)(2,1)S(1)} collective-permute-done((bf16[2,320,128]{2,1,0:T(8,128)(2,1)}, bf16[2,320,128]{2,1,0:T(8,128)(2,1)S(1)}, u32[]{:S(2)}, u32[]{:S(2)}) %collective-permute-start.3) | collective-permute-done | bytes 163872 | tf_op jit(solution)/shard_map/ppermute | solution.py:470
  13.0 0.0 collective-permute-done.4.refs_6_
  13.0 0.0 copy-done.4
  13.0 0.1 broadcast_in_dim.8.refs_6_.refs_5_
  13.2 0.0 copy-done.5
  13.2 0.1 broadcast_in_dim.9.refs_7_.refs_6_
  13.3 0.0 copy-done.3
  13.3 0.1 collective-permute-start.10
  13.4 0.5 %collective-permute-start.11 = (bf16[2,320,128]{2,1,0:T(8,128)(2,1)S(1)}, bf16[2,320,128]{2,1,0:T(8,128)(2,1)S(1)}, u32[]{:S(2)}, u32[]{:S(2)}) collective-permute-start(bf16[2,320,128]{2,1,0:T(8,128)(2,1)S(1)} %collective-permute-done.2.refs_2_), channel_id=1, source_target_pairs={{0,4},{4,0},{8,12},{12,8},{16,20},{20,16},{24,28},{28,24},{1,5},{5... | collective-permute-start | bytes 491528 | tf_op jit(solution)/shard_map/ppermute | solution.py:473
  13.9 0.1 collective-permute-start.12
  13.9 0.0 collective-permute-done.edge_ref
  13.9 0.4 collective-permute-start.13
  14.4 0.0 collective-permute-done.1.near_ref
  14.4 2.4 %collective-permute-start.7 = (bf16[2,2,160,128]{3,2,1,0:T(8,128)(2,1)S(1)}, bf16[2,2,160,128]{3,2,1,0:T(8,128)(2,1)S(1)}, u32[]{:S(2)}, u32[]{:S(2)}) collective-permute-start(bf16[2,2,160,128]{3,2,1,0:T(8,128)(2,1)S(1)} %shard_map.86.refs_0_), channel_id=1, source_target_pairs={{0,8},{4,12},{8,0},{12,4},{16,24},{20,28},{24,16},{28,20},{1,9},{5... | collective-permute-start | bytes 491528 | tf_op jit(solution)/shard_map/ppermute | solution.py:470
  16.8 0.0 copy-done.1
  16.8 1.2 %shard_map.87 = (f32[2,320,128]{2,1,0:T(8,128)S(1)}, f32[8,128]{1,0:T(8,128)S(1)}) custom-call(bf16[320,128]{1,0:T(8,128)(2,1)S(1)} %collective-permute-done.edge_ref, bf16[2,320,128]{2,1,0:T(8,128)(2,1)S(1)} %collective-permute-done.1.near_ref, bf16[2,320,128]{2,1,0:T(8,128)(2,1)S(1)} %bitcast.11, bf16[3,320,960]{2,1,0:T(8,128)(2,1)S(1)} %shard_map.85.w_ref.refs_8_), custom_call_target="tpu_custom_call" | custom-call | flops 471859200 | tf_op jit(solution)/shard_map/pallas_call | solution.py:442
  17.9 0.0 collective-permute-done.10.refs_1_
  17.9 0.1 collective-permute-start.8
  18.1 0.0 collective-permute-done.11.refs_3_
  18.1 1.4 %collective-permute-start.9 = (bf16[2,2,160,128]{3,2,1,0:T(8,128)(2,1)S(1)}, bf16[2,2,160,128]{3,2,1,0:T(8,128)(2,1)S(1)}, u32[]{:S(2)}, u32[]{:S(2)}) collective-permute-start(bf16[2,2,160,128]{3,2,1,0:T(8,128)(2,1)S(1)} %shard_map.86.refs_0_), channel_id=1, source_target_pairs={{0,24},{4,28},{8,16},{12,20},{16,8},{20,12},{24,0},{28,4},{1,25},{... | collective-permute-start | bytes 491528 | tf_op jit(solution)/shard_map/ppermute | solution.py:470
  19.5 0.0 collective-permute-done.12.refs_5_
  19.5 0.0 collective-permute-done.13.refs_7_
  19.5 4.0 %shard_map.88 = (bf16[18,960,128]{2,1,0:T(8,128)(2,1)S(1)}, f32[16,160,128]{2,1,0:T(8,128)S(1)}, f32[2,160,128]{2,1,0:T(8,128)S(1)}) custom-call(bf16[2,320,128]{2,1,0:T(8,128)(2,1)S(1)} %bitcast.19, bf16[2,320,128]{2,1,0:T(8,128)(2,1)S(1)} %collective-permute-done.10.refs_1_, bf16[2,320,128]{2,1,0:T(8,128)(2,1)S(1)} %collective-permute-done.2.refs_2_, ...), custom_call_target="tpu_custom_call" | custom-call | flops 1887436800 | tf_op jit(solution)/shard_map/pallas_call | solution.py:442
  23.5 0.0 collective-permute-done.7.refs_1_
  23.5 3.8 %collective-permute-done.8.refs_2_ = bf16[2,2,160,128]{3,2,1,0:T(8,128)(2,1)S(1)} collective-permute-done((bf16[2,2,160,128]{3,2,1,0:T(8,128)(2,1)S(1)}, bf16[2,2,160,128]{3,2,1,0:T(8,128)(2,1)S(1)}, u32[]{:S(2)}, u32[]{:S(2)}) %collective-permute-start.8) | collective-permute-done | bytes 163872 | tf_op jit(solution)/shard_map/ppermute | solution.py:470
  27.3 0.0 collective-permute-done.9.refs_3_
  27.3 1.6 %shard_map.89.own_ref = bf16[16,160,128]{2,1,0:T(8,128)(2,1)S(1)} custom-call(bf16[2,2,160,128]{3,2,1,0:T(8,128)(2,1)S(1)} %shard_map.86.refs_0_, bf16[2,2,160,128]{3,2,1,0:T(8,128)(2,1)S(1)} %collective-permute-done.7.refs_1_, bf16[2,2,160,128]{3,2,1,0:T(8,128)(2,1)S(1)} %collective-permute-done.8.refs_2_, ...), custom_call_target="tpu_custom_call" | custom-call | flops 471859200 | tf_op jit(solution)/shard_map/pallas_call | solution.py:442
  29.0 0.1 collective-permute-start.17
  29.0 0.5 %collective-permute-start.6 = (f32[8,128]{1,0:T(8,128)S(1)}, f32[8,128]{1,0:T(8,128)S(1)}, u32[]{:S(2)}, u32[]{:S(2)}) collective-permute-start(f32[8,128]{1,0:T(8,128)S(1)} %get-tuple-element.32), channel_id=1, source_target_pairs={{0,4},{4,0},{8,12},{12,8},{16,20},{20,16},{24,28},{28,24},{1,5},{5... | collective-permute-start | bytes 12296 | tf_op jit(solution)/shard_map/ppermute | solution.py:473
  29.5 1.6 %collective-permute-done.6 = f32[8,128]{1,0:T(8,128)S(1)} collective-permute-done((f32[8,128]{1,0:T(8,128)S(1)}, f32[8,128]{1,0:T(8,128)S(1)}, u32[]{:S(2)}, u32[]{:S(2)}) %collective-permute-start.6) | collective-permute-done | bytes 4128 | tf_op jit(solution)/shard_map/ppermute | solution.py:473
  31.1 1.4 %collective-permute-start.14 = (f32[2,8,128]{2,1,0:T(8,128)S(1)}, f32[2,8,128]{2,1,0:T(8,128)S(1)}, u32[]{:S(2)}, u32[]{:S(2)}) collective-permute-start(f32[2,8,128]{2,1,0:T(8,128)S(1)} %pad_maximum_fusion.refs_0_), channel_id=1, source_target_pairs={{0,24},{4,28},{8,16},{12,20},{16,8},{20,12},{24,0},{28,4},{1,25},{... | collective-permute-start | bytes 24584 | tf_op jit(solution)/shard_map/ppermute | solution.py:470
  32.6 0.6 %collective-permute-start.15 = (f32[2,8,128]{2,1,0:T(8,128)S(1)}, f32[2,8,128]{2,1,0:T(8,128)S(1)}, u32[]{:S(2)}, u32[]{:S(2)}) collective-permute-start(f32[2,8,128]{2,1,0:T(8,128)S(1)} %pad_maximum_fusion.refs_0_), channel_id=1, source_target_pairs={{0,8},{4,12},{8,0},{12,4},{16,24},{20,28},{24,16},{28,20},{1,9},{5... | collective-permute-start | bytes 24584 | tf_op jit(solution)/shard_map/ppermute | solution.py:470
  33.2 1.4 %collective-permute-start.16 = (f32[2,8,128]{2,1,0:T(8,128)S(1)}, f32[2,8,128]{2,1,0:T(8,128)S(1)}, u32[]{:S(2)}, u32[]{:S(2)}) collective-permute-start(f32[2,8,128]{2,1,0:T(8,128)S(1)} %pad_maximum_fusion.refs_0_), channel_id=1, source_target_pairs={{0,16},{4,20},{8,24},{12,28},{16,0},{20,4},{24,8},{28,12},{1,17},{... | collective-permute-start | bytes 24584 | tf_op jit(solution)/shard_map/ppermute | solution.py:470
  34.6 0.0 collective-permute-done.17.other_ref
  34.6 1.8 %shard_map.91 = (f32[225,128]{1,0:T(8,128)S(1)}, bf16[225,128]{1,0:T(8,128)(2,1)S(1)}, bf16[225,128]{1,0:T(8,128)(2,1)S(1)}, bf16[225,128]{1,0:T(8,128)(2,1)S(1)}, bf16[4,320,128]{2,1,0:T(8,128)(2,1)S(1)}) custom-call(bf16[16,160,128]{2,1,0:T(8,128)(2,1)S(1)} %shard_map.89.own_ref, bf16[16,160,128]{2,1,0:T(8,128)(2,1)S(1)} %collective-permute-done.17.other_ref, ...), custom_call_target="tpu_custom_call" | custom-call | flops 943718400 | tf_op jit(solution)/shard_map/pallas_call | solution.py:442
  36.4 3.7 %collective-permute-start.18 = (bf16[225,128]{1,0:T(8,128)(2,1)S(1)}, bf16[225,128]{1,0:T(8,128)(2,1)S(1)}, u32[]{:S(2)}, u32[]{:S(2)}) collective-permute-start(bf16[225,128]{1,0:T(8,128)(2,1)S(1)} %get-tuple-element.56), channel_id=1, source_target_pairs={{0,3},{1,2},{2,1},{3,0},{4,7},{5,6},{6,5},{7,4},{8,11},{9,10},{10,... | collective-permute-start | bytes 172808 | tf_op jit(solution)/shard_map/ppermute | solution.py:563
  40.1 0.0 collective-permute-start.19
  40.1 0.0 collective-permute-done.14.refs_1_
  40.1 0.8 %collective-permute-start.20 = (bf16[225,128]{1,0:T(8,128)(2,1)S(1)}, bf16[225,128]{1,0:T(8,128)(2,1)S(1)}, u32[]{:S(2)}, u32[]{:S(2)}) collective-permute-start(bf16[225,128]{1,0:T(8,128)(2,1)S(1)} %get-tuple-element.58), channel_id=1, source_target_pairs={{0,1},{1,0},{2,3},{3,2},{4,5},{5,4},{6,7},{7,6},{8,9},{9,8},{10,11... | collective-permute-start | bytes 172808 | tf_op jit(solution)/shard_map/ppermute | solution.py:563
  40.8 0.0 collective-permute-done.15.refs_2_
  40.8 0.0 collective-permute-done.16.refs_3_
  40.8 1.5 %shard_map.90 = bf16[2,320,128]{2,1,0:T(8,128)(2,1)} custom-call(f32[2,8,128]{2,1,0:T(8,128)S(1)} %pad_maximum_fusion.refs_0_, f32[2,8,128]{2,1,0:T(8,128)S(1)} %collective-permute-done.14.refs_1_, f32[2,8,128]{2,1,0:T(8,128)S(1)} %collective-permute-done.15.refs_2_, f32[2,8,128]{2,1,0:T(8,128)S(1)} %collective-permute-done.16.refs_3_, ...), custom_call_target="tpu_custom_call" | custom-call | flops 117964800 | tf_op jit(solution)/shard_map/pallas_call | solution.py:442
  42.3 1.7 %shard_map.92 = bf16[2,320,128]{2,1,0:T(8,128)(2,1)} custom-call(bf16[4,320,128]{2,1,0:T(8,128)(2,1)S(1)} %get-tuple-element.54.gz_ref, bf16[3,320,960]{2,1,0:T(8,128)(2,1)S(1)} %shard_map.85.w_ref.refs_8_), custom_call_target="tpu_custom_call" | custom-call | flops 471859200 | tf_op jit(solution)/shard_map/pallas_call | solution.py:442
  44.1 0.0 collective-permute-done.18
  44.1 1.1 %collective-permute-done.19 = bf16[225,128]{1,0:T(8,128)(2,1)S(1)} collective-permute-done((bf16[225,128]{1,0:T(8,128)(2,1)S(1)}, bf16[225,128]{1,0:T(8,128)(2,1)S(1)}, u32[]{:S(2)}, u32[]{:S(2)}) %collective-permute-start.19) | collective-permute-done | bytes 57632 | tf_op jit(solution)/shard_map/ppermute | solution.py:563
  45.2 0.0 collective-permute-done.20
  45.2 0.7 %add_bitcast_fusion = f32[28800]{0:T(1024)} fusion(bf16[225,128]{1,0:T(8,128)(2,1)S(1)} %collective-permute-done.20, bf16[225,128]{1,0:T(8,128)(2,1)S(1)} %collective-permute-done.19, f32[225,128]{1,0:T(8,128)S(1)} %get-tuple-element.55, bf16[225,128]{1,0:T(8,128)(2,1)S(1)} %collective-permute-done.18), kind=kLoop, calls=%fused_computation | loop fusion | flops 172800 | bytes 403200 | tf_op jit(solution)/shard_map/reshape | solution.py:579
  (3 shorter events, 0.0 us)
Async XLA Ops:
  0.6 8.3 %collective-permute-start.2 = (bf16[2,320,128]{2,1,0:T(8,128)(2,1)}, bf16[2,320,128]{2,1,0:T(8,128)(2,1)S(1)}, u32[]{:S(2)}, u32[]{:S(2)}) collective-permute-start(bf16[2,320,128]{2,1,0:T(8,128)(2,1)} %bitcast.15), channel_id=1, source_target_pairs={{0,8},{4,12},{8,0},{12,4},{16,24},{20,28},{24,16},{28,20},{1,9},{5... | collective-permute-start | bytes 491528 | tf_op jit(solution)/shard_map/ppermute | solution.py:470
  3.7 9.4 %collective-permute-start.3 = (bf16[2,320,128]{2,1,0:T(8,128)(2,1)}, bf16[2,320,128]{2,1,0:T(8,128)(2,1)S(1)}, u32[]{:S(2)}, u32[]{:S(2)}) collective-permute-start(bf16[2,320,128]{2,1,0:T(8,128)(2,1)} %bitcast.16), channel_id=1, source_target_pairs={{0,16},{4,20},{8,24},{12,28},{16,0},{20,4},{24,8},{28,12},{1,17},{... | collective-permute-start | bytes 491528 | tf_op jit(solution)/shard_map/ppermute | solution.py:470
  5.2 7.9 %collective-permute-start.4 = (bf16[2,320,128]{2,1,0:T(8,128)(2,1)}, bf16[2,320,128]{2,1,0:T(8,128)(2,1)S(1)}, u32[]{:S(2)}, u32[]{:S(2)}) collective-permute-start(bf16[2,320,128]{2,1,0:T(8,128)(2,1)} %bitcast.17), channel_id=1, source_target_pairs={{0,24},{4,28},{8,16},{12,20},{16,8},{20,12},{24,0},{28,4},{1,25},{... | collective-permute-start | bytes 491528 | tf_op jit(solution)/shard_map/ppermute | solution.py:470
  5.2 2.1 %collective-permute-start.5 = (bf16[2,320,128]{2,1,0:T(8,128)(2,1)}, bf16[2,320,128]{2,1,0:T(8,128)(2,1)S(1)}, u32[]{:S(2)}, u32[]{:S(2)}) collective-permute-start(bf16[2,320,128]{2,1,0:T(8,128)(2,1)} %bitcast.13), channel_id=1, source_target_pairs={{0,4},{4,0},{8,12},{12,8},{16,20},{20,16},{24,28},{28,24},{1,5},{5... | collective-permute-start | bytes 491528 | tf_op jit(solution)/shard_map/ppermute | solution.py:473
  5.2 1.6 %copy-start = (bf16[3,3,320,320]{3,2,1,0:T(8,128)(2,1)S(1)}, bf16[3,3,320,320]{3,2,1,0:T(8,128)(2,1)}, u32[]{:S(2)}) copy-start(bf16[3,3,320,320]{3,2,1,0:T(8,128)(2,1)} %w_ref.1) | copy-start | bytes 5529604
  5.2 9.2 %collective-permute-start.1 = (bf16[2,320,128]{2,1,0:T(8,128)(2,1)}, bf16[2,320,128]{2,1,0:T(8,128)(2,1)S(1)}, u32[]{:S(2)}, u32[]{:S(2)}) collective-permute-start(bf16[2,320,128]{2,1,0:T(8,128)(2,1)} %bitcast.9), channel_id=1, source_target_pairs={{0,4},{4,0},{8,12},{12,8},{16,20},{20,16},{24,28},{28,24},{1,5},{5... | collective-permute-start | bytes 491528 | tf_op jit(solution)/shard_map/ppermute | solution.py:473
  6.8 1.2 %copy-start.2 = (bf16[1,2,320,128]{3,2,1,0:T(8,128)(2,1)S(1)}, bf16[1,2,320,128]{3,2,1,0:T(8,128)(2,1)}, u32[]{:S(2)}) copy-start(bf16[1,2,320,128]{3,2,1,0:T(8,128)(2,1)} %param.8) | copy-start | bytes 491524
  7.2 5.8 %copy-start.4 = (f32[320]{0:T(512)S(1)}, f32[320]{0:T(512)}, u32[]{:S(2)}) copy-start(f32[320]{0:T(512)} %param.10) | copy-start | bytes 3844
  7.2 5.9 %copy-start.5 = (f32[320]{0:T(512)S(1)}, f32[320]{0:T(512)}, u32[]{:S(2)}) copy-start(f32[320]{0:T(512)} %param.11) | copy-start | bytes 3844
  7.2 6.0 %copy-start.3 = (bf16[1,2,320,128]{3,2,1,0:T(8,128)(2,1)S(1)}, bf16[1,2,320,128]{3,2,1,0:T(8,128)(2,1)}, u32[]{:S(2)}) copy-start(bf16[1,2,320,128]{3,2,1,0:T(8,128)(2,1)} %param.7) | copy-start | bytes 491524
  7.3 9.5 %copy-start.1 = (bf16[1,2,320,128]{3,2,1,0:T(8,128)(2,1)S(1)}, bf16[1,2,320,128]{3,2,1,0:T(8,128)(2,1)}, u32[]{:S(2)}) copy-start(bf16[1,2,320,128]{3,2,1,0:T(8,128)(2,1)} %param.6) | copy-start | bytes 491524
  7.3 6.7 %collective-permute-start = (bf16[320,128]{1,0:T(8,128)(2,1)S(1)}, bf16[320,128]{1,0:T(8,128)(2,1)S(1)}, u32[]{:S(2)}, u32[]{:S(2)}) collective-permute-start(bf16[320,128]{1,0:T(8,128)(2,1)S(1)} %edge.1), channel_id=1, source_target_pairs={{4,8},{12,16},{20,24},{8,4},{16,12},{24,20},{5,9},{13,17},{21,25},... | collective-permute-start | bytes 245768 | tf_op jit(solution)/shard_map/ppermute | solution.py:488
  13.3 4.7 %collective-permute-start.10 = (bf16[2,320,128]{2,1,0:T(8,128)(2,1)S(1)}, bf16[2,320,128]{2,1,0:T(8,128)(2,1)S(1)}, u32[]{:S(2)}, u32[]{:S(2)}) collective-permute-start(bf16[2,320,128]{2,1,0:T(8,128)(2,1)S(1)} %bitcast.18), channel_id=1, source_target_pairs={{0,4},{4,0},{8,12},{12,8},{16,20},{20,16},{24,28},{28,24},{1,5},{5... | collective-permute-start | bytes 491528 | tf_op jit(solution)/shard_map/ppermute | solution.py:473
  13.4 4.7 %collective-permute-start.11 = (bf16[2,320,128]{2,1,0:T(8,128)(2,1)S(1)}, bf16[2,320,128]{2,1,0:T(8,128)(2,1)S(1)}, u32[]{:S(2)}, u32[]{:S(2)}) collective-permute-start(bf16[2,320,128]{2,1,0:T(8,128)(2,1)S(1)} %collective-permute-done.2.refs_2_), channel_id=1, source_target_pairs={{0,4},{4,0},{8,12},{12,8},{16,20},{20,16},{24,28},{28,24},{1,5},{5... | collective-permute-start | bytes 491528 | tf_op jit(solution)/shard_map/ppermute | solution.py:473
  13.9 5.6 %collective-permute-start.12 = (bf16[2,320,128]{2,1,0:T(8,128)(2,1)S(1)}, bf16[2,320,128]{2,1,0:T(8,128)(2,1)S(1)}, u32[]{:S(2)}, u32[]{:S(2)}) collective-permute-start(bf16[2,320,128]{2,1,0:T(8,128)(2,1)S(1)} %collective-permute-done.3.refs_4_), channel_id=1, source_target_pairs={{0,4},{4,0},{8,12},{12,8},{16,20},{20,16},{24,28},{28,24},{1,5},{5... | collective-permute-start | bytes 491528 | tf_op jit(solution)/shard_map/ppermute | solution.py:473
  13.9 5.5 %collective-permute-start.13 = (bf16[2,320,128]{2,1,0:T(8,128)(2,1)S(1)}, bf16[2,320,128]{2,1,0:T(8,128)(2,1)S(1)}, u32[]{:S(2)}, u32[]{:S(2)}) collective-permute-start(bf16[2,320,128]{2,1,0:T(8,128)(2,1)S(1)} %collective-permute-done.4.refs_6_), channel_id=1, source_target_pairs={{0,4},{4,0},{8,12},{12,8},{16,20},{20,16},{24,28},{28,24},{1,5},{5... | collective-permute-start | bytes 491528 | tf_op jit(solution)/shard_map/ppermute | solution.py:473
  14.4 9.1 %collective-permute-start.7 = (bf16[2,2,160,128]{3,2,1,0:T(8,128)(2,1)S(1)}, bf16[2,2,160,128]{3,2,1,0:T(8,128)(2,1)S(1)}, u32[]{:S(2)}, u32[]{:S(2)}) collective-permute-start(bf16[2,2,160,128]{3,2,1,0:T(8,128)(2,1)S(1)} %shard_map.86.refs_0_), channel_id=1, source_target_pairs={{0,8},{4,12},{8,0},{12,4},{16,24},{20,28},{24,16},{28,20},{1,9},{5... | collective-permute-start | bytes 491528 | tf_op jit(solution)/shard_map/ppermute | solution.py:470
  17.9 9.4 %collective-permute-start.8 = (bf16[2,2,160,128]{3,2,1,0:T(8,128)(2,1)S(1)}, bf16[2,2,160,128]{3,2,1,0:T(8,128)(2,1)S(1)}, u32[]{:S(2)}, u32[]{:S(2)}) collective-permute-start(bf16[2,2,160,128]{3,2,1,0:T(8,128)(2,1)S(1)} %shard_map.86.refs_0_), channel_id=1, source_target_pairs={{0,16},{4,20},{8,24},{12,28},{16,0},{20,4},{24,8},{28,12},{1,17},{... | collective-permute-start | bytes 491528 | tf_op jit(solution)/shard_map/ppermute | solution.py:470
  18.1 9.3 %collective-permute-start.9 = (bf16[2,2,160,128]{3,2,1,0:T(8,128)(2,1)S(1)}, bf16[2,2,160,128]{3,2,1,0:T(8,128)(2,1)S(1)}, u32[]{:S(2)}, u32[]{:S(2)}) collective-permute-start(bf16[2,2,160,128]{3,2,1,0:T(8,128)(2,1)S(1)} %shard_map.86.refs_0_), channel_id=1, source_target_pairs={{0,24},{4,28},{8,16},{12,20},{16,8},{20,12},{24,0},{28,4},{1,25},{... | collective-permute-start | bytes 491528 | tf_op jit(solution)/shard_map/ppermute | solution.py:470
  29.0 5.7 %collective-permute-start.17 = (bf16[16,160,128]{2,1,0:T(8,128)(2,1)S(1)}, bf16[16,160,128]{2,1,0:T(8,128)(2,1)S(1)}, u32[]{:S(2)}, u32[]{:S(2)}) collective-permute-start(bf16[16,160,128]{2,1,0:T(8,128)(2,1)S(1)} %shard_map.89.own_ref), channel_id=1, source_target_pairs={{0,4},{4,0},{8,12},{12,8},{16,20},{20,16},{24,28},{28,24},{1,5},{5... | collective-permute-start | bytes 1966088 | tf_op jit(solution)/shard_map/ppermute | solution.py:473
  29.0 2.1 %collective-permute-start.6 = (f32[8,128]{1,0:T(8,128)S(1)}, f32[8,128]{1,0:T(8,128)S(1)}, u32[]{:S(2)}, u32[]{:S(2)}) collective-permute-start(f32[8,128]{1,0:T(8,128)S(1)} %get-tuple-element.32), channel_id=1, source_target_pairs={{0,4},{4,0},{8,12},{12,8},{16,20},{20,16},{24,28},{28,24},{1,5},{5... | collective-permute-start | bytes 12296 | tf_op jit(solution)/shard_map/ppermute | solution.py:473
  31.1 8.9 %collective-permute-start.14 = (f32[2,8,128]{2,1,0:T(8,128)S(1)}, f32[2,8,128]{2,1,0:T(8,128)S(1)}, u32[]{:S(2)}, u32[]{:S(2)}) collective-permute-start(f32[2,8,128]{2,1,0:T(8,128)S(1)} %pad_maximum_fusion.refs_0_), channel_id=1, source_target_pairs={{0,24},{4,28},{8,16},{12,20},{16,8},{20,12},{24,0},{28,4},{1,25},{... | collective-permute-start | bytes 24584 | tf_op jit(solution)/shard_map/ppermute | solution.py:470
  32.6 8.3 %collective-permute-start.15 = (f32[2,8,128]{2,1,0:T(8,128)S(1)}, f32[2,8,128]{2,1,0:T(8,128)S(1)}, u32[]{:S(2)}, u32[]{:S(2)}) collective-permute-start(f32[2,8,128]{2,1,0:T(8,128)S(1)} %pad_maximum_fusion.refs_0_), channel_id=1, source_target_pairs={{0,8},{4,12},{8,0},{12,4},{16,24},{20,28},{24,16},{28,20},{1,9},{5... | collective-permute-start | bytes 24584 | tf_op jit(solution)/shard_map/ppermute | solution.py:470
  33.2 7.7 %collective-permute-start.16 = (f32[2,8,128]{2,1,0:T(8,128)S(1)}, f32[2,8,128]{2,1,0:T(8,128)S(1)}, u32[]{:S(2)}, u32[]{:S(2)}) collective-permute-start(f32[2,8,128]{2,1,0:T(8,128)S(1)} %pad_maximum_fusion.refs_0_), channel_id=1, source_target_pairs={{0,16},{4,20},{8,24},{12,28},{16,0},{20,4},{24,8},{28,12},{1,17},{... | collective-permute-start | bytes 24584 | tf_op jit(solution)/shard_map/ppermute | solution.py:470
  36.4 7.7 %collective-permute-start.18 = (bf16[225,128]{1,0:T(8,128)(2,1)S(1)}, bf16[225,128]{1,0:T(8,128)(2,1)S(1)}, u32[]{:S(2)}, u32[]{:S(2)}) collective-permute-start(bf16[225,128]{1,0:T(8,128)(2,1)S(1)} %get-tuple-element.56), channel_id=1, source_target_pairs={{0,3},{1,2},{2,1},{3,0},{4,7},{5,6},{6,5},{7,4},{8,11},{9,10},{10,... | collective-permute-start | bytes 172808 | tf_op jit(solution)/shard_map/ppermute | solution.py:563
  40.1 5.1 %collective-permute-start.19 = (bf16[225,128]{1,0:T(8,128)(2,1)S(1)}, bf16[225,128]{1,0:T(8,128)(2,1)S(1)}, u32[]{:S(2)}, u32[]{:S(2)}) collective-permute-start(bf16[225,128]{1,0:T(8,128)(2,1)S(1)} %get-tuple-element.57), channel_id=1, source_target_pairs={{0,2},{1,3},{2,0},{3,1},{4,6},{5,7},{6,4},{7,5},{8,10},{9,11},{10,... | collective-permute-start | bytes 172808 | tf_op jit(solution)/shard_map/ppermute | solution.py:563
  40.1 5.1 %collective-permute-start.20 = (bf16[225,128]{1,0:T(8,128)(2,1)S(1)}, bf16[225,128]{1,0:T(8,128)(2,1)S(1)}, u32[]{:S(2)}, u32[]{:S(2)}) collective-permute-start(bf16[225,128]{1,0:T(8,128)(2,1)S(1)} %get-tuple-element.58), channel_id=1, source_target_pairs={{0,1},{1,0},{2,3},{3,2},{4,5},{5,4},{6,7},{7,6},{8,9},{9,8},{10,11... | collective-permute-start | bytes 172808 | tf_op jit(solution)/shard_map/ppermute | solution.py:563

commit v6 on v5

--- a/solution.py
+++ b/solution.py
@@ -382,18 +382,20 @@
         gz_out[r] = gz[home * rows + r]
 
     block = 9 * chans // blocks
-    tap0 = (home * block) // chans
-    left = jnp.concatenate([gz[r + 1] for r in range(image)], axis=1)
+    unit0 = (home * block) // half
     for j in range(span):
-        tap = jnp.minimum(tap0 + j, 8)
+        unit = jnp.minimum(unit0 + j, 17)
+        tap = unit // 2
         a = tap // 3
+        these = pl.ds(pl.multiple_of((unit - tap * 2) * half, step), half)
         side = pl.ds(pl.multiple_of((tap - a * 3) * chans, step), chans)
+        left = jnp.concatenate([gz[r + 1, these] for r in range(image)], axis=1)
         right = jnp.concatenate([xs[r + a, side] for r in range(image)], axis=1)
         rows_of = dot(left, right, ((1,), (1,)))
         for i, (start, size) in enumerate(lane_tiles(chans)):
-            taps[i, j * chans : (j + 1) * chans, :size] = rows_of[:, start : start + size]
-
-    off = pl.multiple_of(home * block - tap0 * chans, 8)
+            taps[i, j * half : (j + 1) * half, :size] = rows_of[:, start : start + size]
+
+    off = pl.multiple_of(home * block - unit0 * half, 8)
     shared = math.gcd(chans, LANES)
     few, many = LANES // shared, chans // shared
     for i in range(taps.shape[0]):
@@ -458,7 +460,7 @@
     half = chans // 2
     count = image * (chans // GROUPS) * width
     block = 9 * chans // blocks
-    span = max((h * block % chans + block - 1) // chans + 1 for h in range(blocks))
+    span = max((h * block % half + block - 1) // half + 1 for h in range(blocks))
     piece = block * chans // (groups_dp * LANES)
     flops = 18 * chans * chans * width
     x_next, grad_out = x_next[0], grad_out[0]
@@ -524,6 +526,8 @@
         wide=4 if image % 4 == 0 else 2,
     )
     stat_pair = jnp.stack((stat, stat_near))
+    stat_pair, norm = lax.optimization_barrier((stat_pair, norm))
+    stat_far = far(stat_pair, chips[:1])
     gz_own = call(
         pull_kernel,
         shape((image, half, width), BF16),
@@ -539,8 +543,8 @@
         count=count,
     )
     gz_other = near(gz_own)
-    stat_pair, gz_own = lax.optimization_barrier((stat_pair, gz_own))
-    stat_far = far(stat_pair, chips)
+    stat_rest, gz_own = lax.optimization_barrier((stat_pair, gz_own))
+    stat_far |= far(stat_rest, chips[1:])
     results = call(
         filter_kernel,
         (shape((piece, LANES), F32),)
@@ -549,7 +553,7 @@
         (gz_own, gz_other, xs),
         scratch=(
             pltpu.VMEM((image + 2, chans, width), BF16),
-            pltpu.VMEM((len(lane_tiles(chans)), span * chans, LANES), F32),
+            pltpu.VMEM((len(lane_tiles(chans)), span * half, LANES), F32),
             pltpu.VMEM((groups_dp * piece, LANES), F32),
         ),
         flops=image * flops // 4,

time: 46 us -> 45.4 us (0.987)
    ppermute x8, waiting for transfers between devices: 1.61 us -> 1.1 us  [near(): return lax.ppermute(own, 'height', pairs(blocks, 1))]
  transfers between devices with their start and end apart: 21 -> 21, of which waited for: 5 -> 5; matrix products, arithmetic and copies ran while one was open for 0% -> 0% of each run, Pallas kernels for 25% -> 26%
where the time goes in v6:
time: 45.4 us; the launch traced here: 45.2 us
  starting transfers between devices  19.1 us (42%)
  Pallas kernels  13.3 us (29%)
  waiting for transfers between devices  11.1 us (24%)
  between operations  0.81 us (2%)
  other arithmetic  0.68 us (1%)
    pallas_call x8, Pallas kernels, call(): pl.pallas_call(functools.partial(kernel, **static), out_shape=out_shape,...  12.2 us
    ppermute x9, starting transfers between devices, far(): return {k: lax.ppermute(own, 'height', pairs(blocks, k)) for k in offsets}  12.1 us
    ppermute x9, waiting for transfers between devices, far(): return {k: lax.ppermute(own, 'height', pairs(blocks, k)) for k in offsets}  8.87 us
    ppermute x3, starting transfers between devices, gathered(): lax.ppermute(results[s], 'dp', pairs(groups_dp, s)).astype(F32)  4.45 us
    ppermute x8, starting transfers between devices, near(): return lax.ppermute(own, 'height', pairs(blocks, 1))  1.77 us
    ppermute x8, waiting for transfers between devices, near(): return lax.ppermute(own, 'height', pairs(blocks, 1))  1.1 us
    ppermute x3, waiting for transfers between devices, gathered(): lax.ppermute(results[s], 'dp', pairs(groups_dp, s)).astype(F32)  1.09 us
    pallas_call x1, Pallas kernels, gathered(): pl.pallas_call(edge_kernel, out_shape=shape((chans, width), BF16), in_spe...  1.05 us
  transfers between devices with their start and end apart: 21, of which 5 were waited for; matrix products, arithmetic and copies ran while one was open for 0% of the time, Pallas kernels for 26%

profile of v6, /device:TPU:0, one launch (start us, length us, event | category | flops | bytes accessed | tf_op | source)
XLA Modules:
  0.0 45.2 jit_solution(5513274879066715334)
XLA Ops:
  0.6 3.0 %collective-permute-start.2 = (bf16[2,320,128]{2,1,0:T(8,128)(2,1)}, bf16[2,320,128]{2,1,0:T(8,128)(2,1)S(1)}, u32[]{:S(2)}, u32[]{:S(2)}) collective-permute-start(bf16[2,320,128]{2,1,0:T(8,128)(2,1)} %bitcast.15), channel_id=1, source_target_pairs={{0,8},{4,12},{8,0},{12,4},{16,24},{20,28},{24,16},{28,20},{1,9},{5... | collective-permute-start | bytes 491528 | tf_op jit(solution)/shard_map/ppermute | solution.py:472
  3.7 1.5 %collective-permute-start.3 = (bf16[2,320,128]{2,1,0:T(8,128)(2,1)}, bf16[2,320,128]{2,1,0:T(8,128)(2,1)S(1)}, u32[]{:S(2)}, u32[]{:S(2)}) collective-permute-start(bf16[2,320,128]{2,1,0:T(8,128)(2,1)} %bitcast.16), channel_id=1, source_target_pairs={{0,16},{4,20},{8,24},{12,28},{16,0},{20,4},{24,8},{28,12},{1,17},{... | collective-permute-start | bytes 491528 | tf_op jit(solution)/shard_map/ppermute | solution.py:472
  5.2 0.0 collective-permute-start.4
  5.2 0.0 collective-permute-start.5
  5.2 0.5 %collective-permute-start.1 = (bf16[2,320,128]{2,1,0:T(8,128)(2,1)}, bf16[2,320,128]{2,1,0:T(8,128)(2,1)S(1)}, u32[]{:S(2)}, u32[]{:S(2)}) collective-permute-start(bf16[2,320,128]{2,1,0:T(8,128)(2,1)} %bitcast.9), channel_id=1, source_target_pairs={{0,4},{4,0},{8,12},{12,8},{16,20},{20,16},{24,28},{28,24},{1,5},{5... | collective-permute-start | bytes 491528 | tf_op jit(solution)/shard_map/ppermute | solution.py:475
  5.7 1.1 %edge.1 = bf16[320,128]{1,0:T(8,128)(2,1)S(1)} custom-call(bf16[2,320,128]{2,1,0:T(8,128)(2,1)} %bitcast.10), custom_call_target="tpu_custom_call" | custom-call | flops 3774873600 | tf_op jit(solution)/shard_map/edge/pallas_call | solution.py:478
  6.8 0.1 copy-done
  6.8 0.0 copy-start.2
  6.8 0.4 shard_map.85.w_ref.refs_8_
  7.2 0.0 copy-start.4
  7.2 0.0 copy-start.5
  7.2 0.0 copy-start.3
  7.3 0.0 copy-start.1
  7.3 0.0 collective-permute-done.5.near_ref
  7.3 0.8 %collective-permute-start = (bf16[320,128]{1,0:T(8,128)(2,1)S(1)}, bf16[320,128]{1,0:T(8,128)(2,1)S(1)}, u32[]{:S(2)}, u32[]{:S(2)}) collective-permute-start(bf16[320,128]{1,0:T(8,128)(2,1)S(1)} %edge.1), channel_id=1, source_target_pairs={{4,8},{12,16},{20,24},{8,4},{16,12},{24,20},{5,9},{13,17},{21,25},... | collective-permute-start | bytes 245768 | tf_op jit(solution)/shard_map/ppermute | solution.py:490
  8.1 0.0 copy-done.2
  8.1 0.8 %collective-permute-done.2.refs_2_ = bf16[2,320,128]{2,1,0:T(8,128)(2,1)S(1)} collective-permute-done((bf16[2,320,128]{2,1,0:T(8,128)(2,1)}, bf16[2,320,128]{2,1,0:T(8,128)(2,1)S(1)}, u32[]{:S(2)}, u32[]{:S(2)}) %collective-permute-start.2) | collective-permute-done | bytes 163872 | tf_op jit(solution)/shard_map/ppermute | solution.py:472
  8.9 4.1 %collective-permute-done.3.refs_4_ = bf16[2,320,128]{2,1,0:T(8,128)(2,1)S(1)} collective-permute-done((bf16[2,320,128]{2,1,0:T(8,128)(2,1)}, bf16[2,320,128]{2,1,0:T(8,128)(2,1)S(1)}, u32[]{:S(2)}, u32[]{:S(2)}) %collective-permute-start.3) | collective-permute-done | bytes 163872 | tf_op jit(solution)/shard_map/ppermute | solution.py:472
  13.0 0.0 collective-permute-done.4.refs_6_
  13.0 0.0 copy-done.4
  13.0 0.1 broadcast_in_dim.8.refs_6_.refs_5_
  13.2 0.0 copy-done.5
  13.2 0.1 broadcast_in_dim.9.refs_7_.refs_6_
  13.3 0.1 collective-permute-start.10
  13.3 0.0 copy-done.3
  13.4 0.5 %collective-permute-start.7 = (bf16[2,320,128]{2,1,0:T(8,128)(2,1)S(1)}, bf16[2,320,128]{2,1,0:T(8,128)(2,1)S(1)}, u32[]{:S(2)}, u32[]{:S(2)}) collective-permute-start(bf16[2,320,128]{2,1,0:T(8,128)(2,1)S(1)} %bitcast.18), channel_id=1, source_target_pairs={{0,4},{4,0},{8,12},{12,8},{16,20},{20,16},{24,28},{28,24},{1,5},{5... | collective-permute-start | bytes 491528 | tf_op jit(solution)/shard_map/ppermute | solution.py:475
  13.8 0.1 collective-permute-start.8
  13.9 0.0 collective-permute-done.edge_ref
  13.9 0.4 collective-permute-start.9
  14.4 0.0 collective-permute-done.1.near_ref
  14.4 0.0 copy-done.1
  14.4 1.2 %shard_map.87 = (f32[2,320,128]{2,1,0:T(8,128)S(1)}, f32[8,128]{1,0:T(8,128)S(1)}) custom-call(bf16[320,128]{1,0:T(8,128)(2,1)S(1)} %collective-permute-done.edge_ref, bf16[2,320,128]{2,1,0:T(8,128)(2,1)S(1)} %collective-permute-done.1.near_ref, bf16[2,320,128]{2,1,0:T(8,128)(2,1)S(1)} %bitcast.11, bf16[3,320,960]{2,1,0:T(8,128)(2,1)S(1)} %shard_map.85.w_ref.refs_8_), custom_call_target="tpu_custom_call" | custom-call | flops 471859200 | tf_op jit(solution)/shard_map/pallas_call | solution.py:444
  15.5 0.1 collective-permute-start.6
  15.7 1.1 %collective-permute-done.6 = f32[8,128]{1,0:T(8,128)S(1)} collective-permute-done((f32[8,128]{1,0:T(8,128)S(1)}, f32[8,128]{1,0:T(8,128)S(1)}, u32[]{:S(2)}, u32[]{:S(2)}) %collective-permute-start.6) | collective-permute-done | bytes 4128 | tf_op jit(solution)/shard_map/ppermute | solution.py:475
  16.7 2.4 %collective-permute-start.12 = (bf16[2,2,160,128]{3,2,1,0:T(8,128)(2,1)S(1)}, bf16[2,2,160,128]{3,2,1,0:T(8,128)(2,1)S(1)}, u32[]{:S(2)}, u32[]{:S(2)}) collective-permute-start(bf16[2,2,160,128]{3,2,1,0:T(8,128)(2,1)S(1)} %shard_map.86.refs_0_), channel_id=1, source_target_pairs={{0,8},{4,12},{8,0},{12,4},{16,24},{20,28},{24,16},{28,20},{1,9},{5... | collective-permute-start | bytes 491528 | tf_op jit(solution)/shard_map/ppermute | solution.py:472
  19.1 0.0 collective-permute-done.10.refs_7_
  19.1 0.2 collective-permute-start.13
  19.4 0.0 collective-permute-done.7.refs_1_
  19.4 1.3 %collective-permute-start.14 = (bf16[2,2,160,128]{3,2,1,0:T(8,128)(2,1)S(1)}, bf16[2,2,160,128]{3,2,1,0:T(8,128)(2,1)S(1)}, u32[]{:S(2)}, u32[]{:S(2)}) collective-permute-start(bf16[2,2,160,128]{3,2,1,0:T(8,128)(2,1)S(1)} %shard_map.86.refs_0_), channel_id=1, source_target_pairs={{0,24},{4,28},{8,16},{12,20},{16,8},{20,12},{24,0},{28,4},{1,25},{... | collective-permute-start | bytes 491528 | tf_op jit(solution)/shard_map/ppermute | solution.py:472
  20.7 0.0 collective-permute-done.8.refs_3_
  20.7 0.0 collective-permute-done.9.refs_5_
  20.7 4.0 %shard_map.88 = (bf16[18,960,128]{2,1,0:T(8,128)(2,1)S(1)}, f32[16,160,128]{2,1,0:T(8,128)S(1)}, f32[2,160,128]{2,1,0:T(8,128)S(1)}) custom-call(bf16[2,320,128]{2,1,0:T(8,128)(2,1)S(1)} %bitcast.19, bf16[2,320,128]{2,1,0:T(8,128)(2,1)S(1)} %collective-permute-done.7.refs_1_, bf16[2,320,128]{2,1,0:T(8,128)(2,1)S(1)} %collective-permute-done.2.refs_2_, ...), custom_call_target="tpu_custom_call" | custom-call | flops 1887436800 | tf_op jit(solution)/shard_map/pallas_call | solution.py:444
  24.7 0.0 collective-permute-done.12.refs_1_
  24.7 3.9 %collective-permute-done.13.refs_2_ = bf16[2,2,160,128]{3,2,1,0:T(8,128)(2,1)S(1)} collective-permute-done((bf16[2,2,160,128]{3,2,1,0:T(8,128)(2,1)S(1)}, bf16[2,2,160,128]{3,2,1,0:T(8,128)(2,1)S(1)}, u32[]{:S(2)}, u32[]{:S(2)}) %collective-permute-start.13) | collective-permute-done | bytes 163872 | tf_op jit(solution)/shard_map/ppermute | solution.py:472
  28.6 0.0 collective-permute-done.14.refs_3_
  28.7 1.6 %shard_map.89.own_ref = bf16[16,160,128]{2,1,0:T(8,128)(2,1)S(1)} custom-call(bf16[2,2,160,128]{3,2,1,0:T(8,128)(2,1)S(1)} %shard_map.86.refs_0_, bf16[2,2,160,128]{3,2,1,0:T(8,128)(2,1)S(1)} %collective-permute-done.12.refs_1_, bf16[2,2,160,128]{3,2,1,0:T(8,128)(2,1)S(1)} %collective-permute-done.13.refs_2_, ...), custom_call_target="tpu_custom_call" | custom-call | flops 471859200 | tf_op jit(solution)/shard_map/pallas_call | solution.py:444
  30.3 0.1 collective-permute-start.17
  30.3 0.4 collective-permute-start.15
  30.8 1.5 %collective-permute-start.16 = (f32[2,8,128]{2,1,0:T(8,128)S(1)}, f32[2,8,128]{2,1,0:T(8,128)S(1)}, u32[]{:S(2)}, u32[]{:S(2)}) collective-permute-start(f32[2,8,128]{2,1,0:T(8,128)S(1)} %pad_maximum_fusion.refs_0_), channel_id=1, source_target_pairs={{0,16},{4,20},{8,24},{12,28},{16,0},{20,4},{24,8},{28,12},{1,17},{... | collective-permute-start | bytes 24584 | tf_op jit(solution)/shard_map/ppermute | solution.py:472
  32.2 1.7 %collective-permute-start.11 = (f32[2,8,128]{2,1,0:T(8,128)S(1)}, f32[2,8,128]{2,1,0:T(8,128)S(1)}, u32[]{:S(2)}, u32[]{:S(2)}) collective-permute-start(f32[2,8,128]{2,1,0:T(8,128)S(1)} %pad_maximum_fusion.refs_0_), channel_id=1, source_target_pairs={{0,24},{4,28},{8,16},{12,20},{16,8},{20,12},{24,0},{28,4},{1,25},{... | collective-permute-start | bytes 24584 | tf_op jit(solution)/shard_map/ppermute | solution.py:472
  33.9 0.0 collective-permute-done.17.other_ref
  33.9 1.9 %shard_map.91 = (f32[225,128]{1,0:T(8,128)S(1)}, bf16[225,128]{1,0:T(8,128)(2,1)S(1)}, bf16[225,128]{1,0:T(8,128)(2,1)S(1)}, bf16[225,128]{1,0:T(8,128)(2,1)S(1)}, bf16[4,320,128]{2,1,0:T(8,128)(2,1)S(1)}) custom-call(bf16[16,160,128]{2,1,0:T(8,128)(2,1)S(1)} %shard_map.89.own_ref, bf16[16,160,128]{2,1,0:T(8,128)(2,1)S(1)} %collective-permute-done.17.other_ref, ...), custom_call_target="tpu_custom_call" | custom-call | flops 943718400 | tf_op jit(solution)/shard_map/pallas_call | solution.py:444
  35.8 3.7 %collective-permute-start.18 = (bf16[225,128]{1,0:T(8,128)(2,1)S(1)}, bf16[225,128]{1,0:T(8,128)(2,1)S(1)}, u32[]{:S(2)}, u32[]{:S(2)}) collective-permute-start(bf16[225,128]{1,0:T(8,128)(2,1)S(1)} %get-tuple-element.60), channel_id=1, source_target_pairs={{0,3},{1,2},{2,1},{3,0},{4,7},{5,6},{6,5},{7,4},{8,11},{9,10},{10,... | collective-permute-start | bytes 172808 | tf_op jit(solution)/shard_map/ppermute | solution.py:567
  39.4 0.0 collective-permute-start.19
  39.4 0.0 collective-permute-done.15.refs_2_
  39.4 0.8 %collective-permute-start.20 = (bf16[225,128]{1,0:T(8,128)(2,1)S(1)}, bf16[225,128]{1,0:T(8,128)(2,1)S(1)}, u32[]{:S(2)}, u32[]{:S(2)}) collective-permute-start(bf16[225,128]{1,0:T(8,128)(2,1)S(1)} %get-tuple-element.62), channel_id=1, source_target_pairs={{0,1},{1,0},{2,3},{3,2},{4,5},{5,4},{6,7},{7,6},{8,9},{9,8},{10,11... | collective-permute-start | bytes 172808 | tf_op jit(solution)/shard_map/ppermute | solution.py:567
  40.2 0.0 collective-permute-done.16.refs_3_
  40.2 0.0 collective-permute-done.11.refs_1_
  40.2 1.5 %shard_map.90 = bf16[2,320,128]{2,1,0:T(8,128)(2,1)} custom-call(f32[2,8,128]{2,1,0:T(8,128)S(1)} %pad_maximum_fusion.refs_0_, f32[2,8,128]{2,1,0:T(8,128)S(1)} %collective-permute-done.11.refs_1_, f32[2,8,128]{2,1,0:T(8,128)S(1)} %collective-permute-done.15.refs_2_, f32[2,8,128]{2,1,0:T(8,128)S(1)} %collective-permute-done.16.refs_3_, ...), custom_call_target="tpu_custom_call" | custom-call | flops 117964800 | tf_op jit(solution)/shard_map/pallas_call | solution.py:444
  41.7 1.7 %shard_map.92 = bf16[2,320,128]{2,1,0:T(8,128)(2,1)} custom-call(bf16[4,320,128]{2,1,0:T(8,128)(2,1)S(1)} %get-tuple-element.58.gz_ref, bf16[3,320,960]{2,1,0:T(8,128)(2,1)S(1)} %shard_map.85.w_ref.refs_8_), custom_call_target="tpu_custom_call" | custom-call | flops 471859200 | tf_op jit(solution)/shard_map/pallas_call | solution.py:444
  43.4 0.0 collective-permute-done.18
  43.4 1.1 %collective-permute-done.19 = bf16[225,128]{1,0:T(8,128)(2,1)S(1)} collective-permute-done((bf16[225,128]{1,0:T(8,128)(2,1)S(1)}, bf16[225,128]{1,0:T(8,128)(2,1)S(1)}, u32[]{:S(2)}, u32[]{:S(2)}) %collective-permute-start.19) | collective-permute-done | bytes 57632 | tf_op jit(solution)/shard_map/ppermute | solution.py:567
  44.5 0.0 collective-permute-done.20
  44.5 0.7 %add_bitcast_fusion = f32[28800]{0:T(1024)} fusion(bf16[225,128]{1,0:T(8,128)(2,1)S(1)} %collective-permute-done.20, bf16[225,128]{1,0:T(8,128)(2,1)S(1)} %collective-permute-done.19, f32[225,128]{1,0:T(8,128)S(1)} %get-tuple-element.59, bf16[225,128]{1,0:T(8,128)(2,1)S(1)} %collective-permute-done.18), kind=kLoop, calls=%fused_computation | loop fusion | flops 172800 | bytes 403200 | tf_op jit(solution)/shard_map/reshape | solution.py:583
  (3 shorter events, 0.0 us)
Async XLA Ops:
  0.6 8.3 %collective-permute-start.2 = (bf16[2,320,128]{2,1,0:T(8,128)(2,1)}, bf16[2,320,128]{2,1,0:T(8,128)(2,1)S(1)}, u32[]{:S(2)}, u32[]{:S(2)}) collective-permute-start(bf16[2,320,128]{2,1,0:T(8,128)(2,1)} %bitcast.15), channel_id=1, source_target_pairs={{0,8},{4,12},{8,0},{12,4},{16,24},{20,28},{24,16},{28,20},{1,9},{5... | collective-permute-start | bytes 491528 | tf_op jit(solution)/shard_map/ppermute | solution.py:472
  3.7 9.4 %collective-permute-start.3 = (bf16[2,320,128]{2,1,0:T(8,128)(2,1)}, bf16[2,320,128]{2,1,0:T(8,128)(2,1)S(1)}, u32[]{:S(2)}, u32[]{:S(2)}) collective-permute-start(bf16[2,320,128]{2,1,0:T(8,128)(2,1)} %bitcast.16), channel_id=1, source_target_pairs={{0,16},{4,20},{8,24},{12,28},{16,0},{20,4},{24,8},{28,12},{1,17},{... | collective-permute-start | bytes 491528 | tf_op jit(solution)/shard_map/ppermute | solution.py:472
  5.2 7.9 %collective-permute-start.4 = (bf16[2,320,128]{2,1,0:T(8,128)(2,1)}, bf16[2,320,128]{2,1,0:T(8,128)(2,1)S(1)}, u32[]{:S(2)}, u32[]{:S(2)}) collective-permute-start(bf16[2,320,128]{2,1,0:T(8,128)(2,1)} %bitcast.17), channel_id=1, source_target_pairs={{0,24},{4,28},{8,16},{12,20},{16,8},{20,12},{24,0},{28,4},{1,25},{... | collective-permute-start | bytes 491528 | tf_op jit(solution)/shard_map/ppermute | solution.py:472
  5.2 2.1 %collective-permute-start.5 = (bf16[2,320,128]{2,1,0:T(8,128)(2,1)}, bf16[2,320,128]{2,1,0:T(8,128)(2,1)S(1)}, u32[]{:S(2)}, u32[]{:S(2)}) collective-permute-start(bf16[2,320,128]{2,1,0:T(8,128)(2,1)} %bitcast.13), channel_id=1, source_target_pairs={{0,4},{4,0},{8,12},{12,8},{16,20},{20,16},{24,28},{28,24},{1,5},{5... | collective-permute-start | bytes 491528 | tf_op jit(solution)/shard_map/ppermute | solution.py:475
  5.2 1.6 %copy-start = (bf16[3,3,320,320]{3,2,1,0:T(8,128)(2,1)S(1)}, bf16[3,3,320,320]{3,2,1,0:T(8,128)(2,1)}, u32[]{:S(2)}) copy-start(bf16[3,3,320,320]{3,2,1,0:T(8,128)(2,1)} %w_ref.1) | copy-start | bytes 5529604
  5.2 9.2 %collective-permute-start.1 = (bf16[2,320,128]{2,1,0:T(8,128)(2,1)}, bf16[2,320,128]{2,1,0:T(8,128)(2,1)S(1)}, u32[]{:S(2)}, u32[]{:S(2)}) collective-permute-start(bf16[2,320,128]{2,1,0:T(8,128)(2,1)} %bitcast.9), channel_id=1, source_target_pairs={{0,4},{4,0},{8,12},{12,8},{16,20},{20,16},{24,28},{28,24},{1,5},{5... | collective-permute-start | bytes 491528 | tf_op jit(solution)/shard_map/ppermute | solution.py:475
  6.8 1.2 %copy-start.2 = (bf16[1,2,320,128]{3,2,1,0:T(8,128)(2,1)S(1)}, bf16[1,2,320,128]{3,2,1,0:T(8,128)(2,1)}, u32[]{:S(2)}) copy-start(bf16[1,2,320,128]{3,2,1,0:T(8,128)(2,1)} %param.8) | copy-start | bytes 491524
  7.2 5.8 %copy-start.4 = (f32[320]{0:T(512)S(1)}, f32[320]{0:T(512)}, u32[]{:S(2)}) copy-start(f32[320]{0:T(512)} %param.10) | copy-start | bytes 3844
  7.2 5.9 %copy-start.5 = (f32[320]{0:T(512)S(1)}, f32[320]{0:T(512)}, u32[]{:S(2)}) copy-start(f32[320]{0:T(512)} %param.11) | copy-start | bytes 3844
  7.2 6.1 %copy-start.3 = (bf16[1,2,320,128]{3,2,1,0:T(8,128)(2,1)S(1)}, bf16[1,2,320,128]{3,2,1,0:T(8,128)(2,1)}, u32[]{:S(2)}) copy-start(bf16[1,2,320,128]{3,2,1,0:T(8,128)(2,1)} %param.7) | copy-start | bytes 491524
  7.3 7.1 %copy-start.1 = (bf16[1,2,320,128]{3,2,1,0:T(8,128)(2,1)S(1)}, bf16[1,2,320,128]{3,2,1,0:T(8,128)(2,1)}, u32[]{:S(2)}) copy-start(bf16[1,2,320,128]{3,2,1,0:T(8,128)(2,1)} %param.6) | copy-start | bytes 491524
  7.3 6.7 %collective-permute-start = (bf16[320,128]{1,0:T(8,128)(2,1)S(1)}, bf16[320,128]{1,0:T(8,128)(2,1)S(1)}, u32[]{:S(2)}, u32[]{:S(2)}) collective-permute-start(bf16[320,128]{1,0:T(8,128)(2,1)S(1)} %edge.1), channel_id=1, source_target_pairs={{4,8},{12,16},{20,24},{8,4},{16,12},{24,20},{5,9},{13,17},{21,25},... | collective-permute-start | bytes 245768 | tf_op jit(solution)/shard_map/ppermute | solution.py:490
  13.3 5.9 %collective-permute-start.10 = (bf16[2,320,128]{2,1,0:T(8,128)(2,1)S(1)}, bf16[2,320,128]{2,1,0:T(8,128)(2,1)S(1)}, u32[]{:S(2)}, u32[]{:S(2)}) collective-permute-start(bf16[2,320,128]{2,1,0:T(8,128)(2,1)S(1)} %collective-permute-done.4.refs_6_), channel_id=1, source_target_pairs={{0,4},{4,0},{8,12},{12,8},{16,20},{20,16},{24,28},{28,24},{1,5},{5... | collective-permute-start | bytes 491528 | tf_op jit(solution)/shard_map/ppermute | solution.py:475
  13.4 6.0 %collective-permute-start.7 = (bf16[2,320,128]{2,1,0:T(8,128)(2,1)S(1)}, bf16[2,320,128]{2,1,0:T(8,128)(2,1)S(1)}, u32[]{:S(2)}, u32[]{:S(2)}) collective-permute-start(bf16[2,320,128]{2,1,0:T(8,128)(2,1)S(1)} %bitcast.18), channel_id=1, source_target_pairs={{0,4},{4,0},{8,12},{12,8},{16,20},{20,16},{24,28},{28,24},{1,5},{5... | collective-permute-start | bytes 491528 | tf_op jit(solution)/shard_map/ppermute | solution.py:475
  13.8 6.8 %collective-permute-start.8 = (bf16[2,320,128]{2,1,0:T(8,128)(2,1)S(1)}, bf16[2,320,128]{2,1,0:T(8,128)(2,1)S(1)}, u32[]{:S(2)}, u32[]{:S(2)}) collective-permute-start(bf16[2,320,128]{2,1,0:T(8,128)(2,1)S(1)} %collective-permute-done.2.refs_2_), channel_id=1, source_target_pairs={{0,4},{4,0},{8,12},{12,8},{16,20},{20,16},{24,28},{28,24},{1,5},{5... | collective-permute-start | bytes 491528 | tf_op jit(solution)/shard_map/ppermute | solution.py:475
  13.9 6.8 %collective-permute-start.9 = (bf16[2,320,128]{2,1,0:T(8,128)(2,1)S(1)}, bf16[2,320,128]{2,1,0:T(8,128)(2,1)S(1)}, u32[]{:S(2)}, u32[]{:S(2)}) collective-permute-start(bf16[2,320,128]{2,1,0:T(8,128)(2,1)S(1)} %collective-permute-done.3.refs_4_), channel_id=1, source_target_pairs={{0,4},{4,0},{8,12},{12,8},{16,20},{20,16},{24,28},{28,24},{1,5},{5... | collective-permute-start | bytes 491528 | tf_op jit(solution)/shard_map/ppermute | solution.py:475
  15.5 1.2 %collective-permute-start.6 = (f32[8,128]{1,0:T(8,128)S(1)}, f32[8,128]{1,0:T(8,128)S(1)}, u32[]{:S(2)}, u32[]{:S(2)}) collective-permute-start(f32[8,128]{1,0:T(8,128)S(1)} %get-tuple-element.34), channel_id=1, source_target_pairs={{0,4},{4,0},{8,12},{12,8},{16,20},{20,16},{24,28},{28,24},{1,5},{5... | collective-permute-start | bytes 12296 | tf_op jit(solution)/shard_map/ppermute | solution.py:475
  16.7 8.0 %collective-permute-start.12 = (bf16[2,2,160,128]{3,2,1,0:T(8,128)(2,1)S(1)}, bf16[2,2,160,128]{3,2,1,0:T(8,128)(2,1)S(1)}, u32[]{:S(2)}, u32[]{:S(2)}) collective-permute-start(bf16[2,2,160,128]{3,2,1,0:T(8,128)(2,1)S(1)} %shard_map.86.refs_0_), channel_id=1, source_target_pairs={{0,8},{4,12},{8,0},{12,4},{16,24},{20,28},{24,16},{28,20},{1,9},{5... | collective-permute-start | bytes 491528 | tf_op jit(solution)/shard_map/ppermute | solution.py:472
  19.1 9.5 %collective-permute-start.13 = (bf16[2,2,160,128]{3,2,1,0:T(8,128)(2,1)S(1)}, bf16[2,2,160,128]{3,2,1,0:T(8,128)(2,1)S(1)}, u32[]{:S(2)}, u32[]{:S(2)}) collective-permute-start(bf16[2,2,160,128]{3,2,1,0:T(8,128)(2,1)S(1)} %shard_map.86.refs_0_), channel_id=1, source_target_pairs={{0,16},{4,20},{8,24},{12,28},{16,0},{20,4},{24,8},{28,12},{1,17},{... | collective-permute-start | bytes 491528 | tf_op jit(solution)/shard_map/ppermute | solution.py:472
  19.4 9.3 %collective-permute-start.14 = (bf16[2,2,160,128]{3,2,1,0:T(8,128)(2,1)S(1)}, bf16[2,2,160,128]{3,2,1,0:T(8,128)(2,1)S(1)}, u32[]{:S(2)}, u32[]{:S(2)}) collective-permute-start(bf16[2,2,160,128]{3,2,1,0:T(8,128)(2,1)S(1)} %shard_map.86.refs_0_), channel_id=1, source_target_pairs={{0,24},{4,28},{8,16},{12,20},{16,8},{20,12},{24,0},{28,4},{1,25},{... | collective-permute-start | bytes 491528 | tf_op jit(solution)/shard_map/ppermute | solution.py:472
  30.3 3.6 %collective-permute-start.17 = (bf16[16,160,128]{2,1,0:T(8,128)(2,1)S(1)}, bf16[16,160,128]{2,1,0:T(8,128)(2,1)S(1)}, u32[]{:S(2)}, u32[]{:S(2)}) collective-permute-start(bf16[16,160,128]{2,1,0:T(8,128)(2,1)S(1)} %shard_map.89.own_ref), channel_id=1, source_target_pairs={{0,4},{4,0},{8,12},{12,8},{16,20},{20,16},{24,28},{28,24},{1,5},{5... | collective-permute-start | bytes 1966088 | tf_op jit(solution)/shard_map/ppermute | solution.py:475
  30.3 9.1 %collective-permute-start.15 = (f32[2,8,128]{2,1,0:T(8,128)S(1)}, f32[2,8,128]{2,1,0:T(8,128)S(1)}, u32[]{:S(2)}, u32[]{:S(2)}) collective-permute-start(f32[2,8,128]{2,1,0:T(8,128)S(1)} %pad_maximum_fusion.refs_0_), channel_id=1, source_target_pairs={{0,8},{4,12},{8,0},{12,4},{16,24},{20,28},{24,16},{28,20},{1,9},{5... | collective-permute-start | bytes 24584 | tf_op jit(solution)/shard_map/ppermute | solution.py:472
  30.8 9.5 %collective-permute-start.16 = (f32[2,8,128]{2,1,0:T(8,128)S(1)}, f32[2,8,128]{2,1,0:T(8,128)S(1)}, u32[]{:S(2)}, u32[]{:S(2)}) collective-permute-start(f32[2,8,128]{2,1,0:T(8,128)S(1)} %pad_maximum_fusion.refs_0_), channel_id=1, source_target_pairs={{0,16},{4,20},{8,24},{12,28},{16,0},{20,4},{24,8},{28,12},{1,17},{... | collective-permute-start | bytes 24584 | tf_op jit(solution)/shard_map/ppermute | solution.py:472
  32.2 8.0 %collective-permute-start.11 = (f32[2,8,128]{2,1,0:T(8,128)S(1)}, f32[2,8,128]{2,1,0:T(8,128)S(1)}, u32[]{:S(2)}, u32[]{:S(2)}) collective-permute-start(f32[2,8,128]{2,1,0:T(8,128)S(1)} %pad_maximum_fusion.refs_0_), channel_id=1, source_target_pairs={{0,24},{4,28},{8,16},{12,20},{16,8},{20,12},{24,0},{28,4},{1,25},{... | collective-permute-start | bytes 24584 | tf_op jit(solution)/shard_map/ppermute | solution.py:472
  35.8 7.7 %collective-permute-start.18 = (bf16[225,128]{1,0:T(8,128)(2,1)S(1)}, bf16[225,128]{1,0:T(8,128)(2,1)S(1)}, u32[]{:S(2)}, u32[]{:S(2)}) collective-permute-start(bf16[225,128]{1,0:T(8,128)(2,1)S(1)} %get-tuple-element.60), channel_id=1, source_target_pairs={{0,3},{1,2},{2,1},{3,0},{4,7},{5,6},{6,5},{7,4},{8,11},{9,10},{10,... | collective-permute-start | bytes 172808 | tf_op jit(solution)/shard_map/ppermute | solution.py:567
  39.4 5.1 %collective-permute-start.19 = (bf16[225,128]{1,0:T(8,128)(2,1)S(1)}, bf16[225,128]{1,0:T(8,128)(2,1)S(1)}, u32[]{:S(2)}, u32[]{:S(2)}) collective-permute-start(bf16[225,128]{1,0:T(8,128)(2,1)S(1)} %get-tuple-element.61), channel_id=1, source_target_pairs={{0,2},{1,3},{2,0},{3,1},{4,6},{5,7},{6,4},{7,5},{8,10},{9,11},{10,... | collective-permute-start | bytes 172808 | tf_op jit(solution)/shard_map/ppermute | solution.py:567
  39.4 5.1 %collective-permute-start.20 = (bf16[225,128]{1,0:T(8,128)(2,1)S(1)}, bf16[225,128]{1,0:T(8,128)(2,1)S(1)}, u32[]{:S(2)}, u32[]{:S(2)}) collective-permute-start(bf16[225,128]{1,0:T(8,128)(2,1)S(1)} %get-tuple-element.62), channel_id=1, source_target_pairs={{0,1},{1,0},{2,3},{3,2},{4,5},{5,4},{6,7},{7,6},{8,9},{9,8},{10,11... | collective-permute-start | bytes 172808 | tf_op jit(solution)/shard_map/ppermute | solution.py:567

commit v7 on v5

--- a/solution.py
+++ b/solution.py
@@ -178,10 +178,6 @@
     return [(at, min(LANES, size - at)) for at in range(0, size, LANES)]
 
 
-def sigmoid(value):
-    return 1.0 / (1.0 + jnp.exp(-value))
-
-
 def weights_kernel(w_ref, flat_ref):
     chans = flat_ref.shape[1]
     for a in range(3):
@@ -267,8 +263,8 @@
     var = sum(dot(same, part, ((1,), (1,))) for part in split3(spread)) * (1.0 / count)
     rstd = lax.rsqrt(var + eps)
     for r in range(rows):
-        affine = (z_ref[r] - mean) * rstd * gain_ref[...] + shift_ref[...]
-        y_ref[r] = (affine * sigmoid(affine)).astype(BF16)
+        middle = ((z_ref[r] - mean) * rstd * gain_ref[...] + shift_ref[...]) * 0.5
+        y_ref[r] = (middle + middle * jnp.tanh(middle)).astype(BF16)
 
 
 def conv_kernel(*refs, blocks, rows, count, wide):
@@ -327,18 +323,18 @@
         all_at = pl.ds(pl.multiple_of(core * half + start, step), step)
         mean = norm[0, at]
         rstd = norm[1, at]
-        gain = gain_ref[all_at]
-        shift = shift_ref[all_at]
+        gain = gain_ref[all_at] * 0.5
+        shift = shift_ref[all_at] * 0.5
         first = None
         second = None
         for k in range(blocks):
             base = (home ^ k) * rows
             for r in range(rows):
                 n = (z[base + r, at] - mean) * rstd
-                affine = n * gain + shift
-                sig = sigmoid(affine)
-                slope = sig * (1.0 + affine * (1.0 - sig))
-                value = g_refs[k // 2][k % 2, r, at].astype(F32) * slope * gain
+                middle = n * gain + shift
+                bent = jnp.tanh(middle)
+                slope = (1.0 + bent) * (1.0 + middle * (1.0 - bent))
+                value = (g_refs[k // 2][k % 2, r, at].astype(F32) * gain) * slope
                 gn[base + r, at] = value
                 ns[base + r, at] = n
                 first = value if first is None else first + value
@@ -464,7 +460,7 @@
     x_next, grad_out = x_next[0], grad_out[0]
     shape = jax.ShapeDtypeStruct
 
-    chips = sorted(range(2, blocks, 2), key=lambda k: -bin(k).count("1"))
+    chips = sorted(range(2, blocks, 2), key=lambda k: bin(k).count("1"))
 
     def far(own, offsets):
         return {k: lax.ppermute(own, "height", pairs(blocks, k)) for k in offsets}

time: 46 us -> 45.9 us (level)
  no operation moved by 1% of the time
where the time goes in v7:
time: 45.9 us; the launch traced here: 45.7 us
  starting transfers between devices  19.4 us (42%)
  Pallas kernels  13.1 us (29%)
  waiting for transfers between devices  11.5 us (25%)
  between operations  0.81 us (2%)
  other arithmetic  0.68 us (1%)
    pallas_call x8, Pallas kernels, call(): pl.pallas_call(functools.partial(kernel, **static), out_shape=out_shape,...  12 us
    ppermute x9, starting transfers between devices, far(): return {k: lax.ppermute(own, 'height', pairs(blocks, k)) for k in offsets}  12 us
    ppermute x9, waiting for transfers between devices, far(): return {k: lax.ppermute(own, 'height', pairs(blocks, k)) for k in offsets}  8.77 us
    ppermute x3, starting transfers between devices, gathered(): lax.ppermute(results[s], 'dp', pairs(groups_dp, s)).astype(F32)  4.45 us
    ppermute x8, starting transfers between devices, near(): return lax.ppermute(own, 'height', pairs(blocks, 1))  2.16 us
    ppermute x8, waiting for transfers between devices, near(): return lax.ppermute(own, 'height', pairs(blocks, 1))  1.61 us
    ppermute x3, waiting for transfers between devices, gathered(): lax.ppermute(results[s], 'dp', pairs(groups_dp, s)).astype(F32)  1.11 us
    pallas_call x1, Pallas kernels, gathered(): pl.pallas_call(edge_kernel, out_shape=shape((chans, width), BF16), in_spe...  1.05 us
  transfers between devices with their start and end apart: 21, of which 5 were waited for; matrix products, arithmetic and copies ran while one was open for 0% of the time, Pallas kernels for 25%

profile of v7, /device:TPU:0, one launch (start us, length us, event | category | flops | bytes accessed | tf_op | source)
XLA Modules:
  0.0 45.7 jit_solution(4721712842344655606)
XLA Ops:
  0.6 3.0 %collective-permute-start.2 = (bf16[2,320,128]{2,1,0:T(8,128)(2,1)}, bf16[2,320,128]{2,1,0:T(8,128)(2,1)S(1)}, u32[]{:S(2)}, u32[]{:S(2)}) collective-permute-start(bf16[2,320,128]{2,1,0:T(8,128)(2,1)} %bitcast.15), channel_id=1, source_target_pairs={{0,8},{4,12},{8,0},{12,4},{16,24},{20,28},{24,16},{28,20},{1,9},{5... | collective-permute-start | bytes 491528 | tf_op jit(solution)/shard_map/ppermute | solution.py:466
  3.7 1.5 %collective-permute-start.3 = (bf16[2,320,128]{2,1,0:T(8,128)(2,1)}, bf16[2,320,128]{2,1,0:T(8,128)(2,1)S(1)}, u32[]{:S(2)}, u32[]{:S(2)}) collective-permute-start(bf16[2,320,128]{2,1,0:T(8,128)(2,1)} %bitcast.16), channel_id=1, source_target_pairs={{0,16},{4,20},{8,24},{12,28},{16,0},{20,4},{24,8},{28,12},{1,17},{... | collective-permute-start | bytes 491528 | tf_op jit(solution)/shard_map/ppermute | solution.py:466
  5.2 0.0 collective-permute-start.4
  5.2 0.0 collective-permute-start.5
  5.2 0.5 %collective-permute-start.1 = (bf16[2,320,128]{2,1,0:T(8,128)(2,1)}, bf16[2,320,128]{2,1,0:T(8,128)(2,1)S(1)}, u32[]{:S(2)}, u32[]{:S(2)}) collective-permute-start(bf16[2,320,128]{2,1,0:T(8,128)(2,1)} %bitcast.9), channel_id=1, source_target_pairs={{0,4},{4,0},{8,12},{12,8},{16,20},{20,16},{24,28},{28,24},{1,5},{5... | collective-permute-start | bytes 491528 | tf_op jit(solution)/shard_map/ppermute | solution.py:469
  5.7 1.1 %edge.1 = bf16[320,128]{1,0:T(8,128)(2,1)S(1)} custom-call(bf16[2,320,128]{2,1,0:T(8,128)(2,1)} %bitcast.10), custom_call_target="tpu_custom_call" | custom-call | flops 3774873600 | tf_op jit(solution)/shard_map/edge/pallas_call | solution.py:472
  6.8 0.1 copy-done
  6.8 0.0 copy-start.2
  6.8 0.4 shard_map.85.w_ref.refs_8_
  7.2 0.0 copy-start.4
  7.2 0.0 copy-start.5
  7.2 0.0 copy-start.3
  7.3 0.0 copy-start.1
  7.3 0.0 collective-permute-done.5.near_ref
  7.3 0.8 %collective-permute-start = (bf16[320,128]{1,0:T(8,128)(2,1)S(1)}, bf16[320,128]{1,0:T(8,128)(2,1)S(1)}, u32[]{:S(2)}, u32[]{:S(2)}) collective-permute-start(bf16[320,128]{1,0:T(8,128)(2,1)S(1)} %edge.1), channel_id=1, source_target_pairs={{4,8},{12,16},{20,24},{8,4},{16,12},{24,20},{5,9},{13,17},{21,25},... | collective-permute-start | bytes 245768 | tf_op jit(solution)/shard_map/ppermute | solution.py:484
  8.1 0.0 copy-done.2
  8.1 0.8 %collective-permute-done.2.refs_2_ = bf16[2,320,128]{2,1,0:T(8,128)(2,1)S(1)} collective-permute-done((bf16[2,320,128]{2,1,0:T(8,128)(2,1)}, bf16[2,320,128]{2,1,0:T(8,128)(2,1)S(1)}, u32[]{:S(2)}, u32[]{:S(2)}) %collective-permute-start.2) | collective-permute-done | bytes 163872 | tf_op jit(solution)/shard_map/ppermute | solution.py:466
  8.9 4.1 %collective-permute-done.3.refs_4_ = bf16[2,320,128]{2,1,0:T(8,128)(2,1)S(1)} collective-permute-done((bf16[2,320,128]{2,1,0:T(8,128)(2,1)}, bf16[2,320,128]{2,1,0:T(8,128)(2,1)S(1)}, u32[]{:S(2)}, u32[]{:S(2)}) %collective-permute-start.3) | collective-permute-done | bytes 163872 | tf_op jit(solution)/shard_map/ppermute | solution.py:466
  13.0 0.0 collective-permute-done.4.refs_6_
  13.0 0.0 copy-done.4
  13.0 0.1 broadcast_in_dim.8.refs_6_.refs_5_
  13.2 0.0 copy-done.5
  13.2 0.1 broadcast_in_dim.9.refs_7_.refs_6_
  13.3 0.0 copy-done.3
  13.3 0.1 collective-permute-start.10
  13.4 0.5 %collective-permute-start.11 = (bf16[2,320,128]{2,1,0:T(8,128)(2,1)S(1)}, bf16[2,320,128]{2,1,0:T(8,128)(2,1)S(1)}, u32[]{:S(2)}, u32[]{:S(2)}) collective-permute-start(bf16[2,320,128]{2,1,0:T(8,128)(2,1)S(1)} %collective-permute-done.2.refs_2_), channel_id=1, source_target_pairs={{0,4},{4,0},{8,12},{12,8},{16,20},{20,16},{24,28},{28,24},{1,5},{5... | collective-permute-start | bytes 491528 | tf_op jit(solution)/shard_map/ppermute | solution.py:469
  13.9 0.1 collective-permute-start.12
  13.9 0.0 collective-permute-done.edge_ref
  13.9 0.4 collective-permute-start.13
  14.4 0.0 collective-permute-done.1.near_ref
  14.4 2.4 %collective-permute-start.7 = (bf16[2,2,160,128]{3,2,1,0:T(8,128)(2,1)S(1)}, bf16[2,2,160,128]{3,2,1,0:T(8,128)(2,1)S(1)}, u32[]{:S(2)}, u32[]{:S(2)}) collective-permute-start(bf16[2,2,160,128]{3,2,1,0:T(8,128)(2,1)S(1)} %shard_map.86.refs_0_), channel_id=1, source_target_pairs={{0,8},{4,12},{8,0},{12,4},{16,24},{20,28},{24,16},{28,20},{1,9},{5... | collective-permute-start | bytes 491528 | tf_op jit(solution)/shard_map/ppermute | solution.py:466
  16.8 0.0 copy-done.1
  16.8 1.2 %shard_map.87 = (f32[2,320,128]{2,1,0:T(8,128)S(1)}, f32[8,128]{1,0:T(8,128)S(1)}) custom-call(bf16[320,128]{1,0:T(8,128)(2,1)S(1)} %collective-permute-done.edge_ref, bf16[2,320,128]{2,1,0:T(8,128)(2,1)S(1)} %collective-permute-done.1.near_ref, bf16[2,320,128]{2,1,0:T(8,128)(2,1)S(1)} %bitcast.11, bf16[3,320,960]{2,1,0:T(8,128)(2,1)S(1)} %shard_map.85.w_ref.refs_8_), custom_call_target="tpu_custom_call" | custom-call | flops 471859200 | tf_op jit(solution)/shard_map/pallas_call | solution.py:438
  17.9 0.0 collective-permute-done.10.refs_1_
  17.9 0.1 collective-permute-start.8
  18.1 0.0 collective-permute-done.11.refs_3_
  18.1 1.4 %collective-permute-start.9 = (bf16[2,2,160,128]{3,2,1,0:T(8,128)(2,1)S(1)}, bf16[2,2,160,128]{3,2,1,0:T(8,128)(2,1)S(1)}, u32[]{:S(2)}, u32[]{:S(2)}) collective-permute-start(bf16[2,2,160,128]{3,2,1,0:T(8,128)(2,1)S(1)} %shard_map.86.refs_0_), channel_id=1, source_target_pairs={{0,24},{4,28},{8,16},{12,20},{16,8},{20,12},{24,0},{28,4},{1,25},{... | collective-permute-start | bytes 491528 | tf_op jit(solution)/shard_map/ppermute | solution.py:466
  19.5 0.0 collective-permute-done.12.refs_5_
  19.5 0.0 collective-permute-done.13.refs_7_
  19.5 4.0 %shard_map.88 = (bf16[18,960,128]{2,1,0:T(8,128)(2,1)S(1)}, f32[16,160,128]{2,1,0:T(8,128)S(1)}, f32[2,160,128]{2,1,0:T(8,128)S(1)}) custom-call(bf16[2,320,128]{2,1,0:T(8,128)(2,1)S(1)} %bitcast.19, bf16[2,320,128]{2,1,0:T(8,128)(2,1)S(1)} %collective-permute-done.10.refs_1_, bf16[2,320,128]{2,1,0:T(8,128)(2,1)S(1)} %collective-permute-done.2.refs_2_, ...), custom_call_target="tpu_custom_call" | custom-call | flops 1887436800 | tf_op jit(solution)/shard_map/pallas_call | solution.py:438
  23.5 0.0 collective-permute-done.7.refs_1_
  23.5 3.8 %collective-permute-done.8.refs_2_ = bf16[2,2,160,128]{3,2,1,0:T(8,128)(2,1)S(1)} collective-permute-done((bf16[2,2,160,128]{3,2,1,0:T(8,128)(2,1)S(1)}, bf16[2,2,160,128]{3,2,1,0:T(8,128)(2,1)S(1)}, u32[]{:S(2)}, u32[]{:S(2)}) %collective-permute-start.8) | collective-permute-done | bytes 163872 | tf_op jit(solution)/shard_map/ppermute | solution.py:466
  27.3 0.0 collective-permute-done.9.refs_3_
  27.3 1.5 %shard_map.89.own_ref = bf16[16,160,128]{2,1,0:T(8,128)(2,1)S(1)} custom-call(bf16[2,2,160,128]{3,2,1,0:T(8,128)(2,1)S(1)} %shard_map.86.refs_0_, bf16[2,2,160,128]{3,2,1,0:T(8,128)(2,1)S(1)} %collective-permute-done.7.refs_1_, bf16[2,2,160,128]{3,2,1,0:T(8,128)(2,1)S(1)} %collective-permute-done.8.refs_2_, ...), custom_call_target="tpu_custom_call" | custom-call | flops 471859200 | tf_op jit(solution)/shard_map/pallas_call | solution.py:438
  28.9 0.1 collective-permute-start.17
  28.9 0.5 %collective-permute-start.6 = (f32[8,128]{1,0:T(8,128)S(1)}, f32[8,128]{1,0:T(8,128)S(1)}, u32[]{:S(2)}, u32[]{:S(2)}) collective-permute-start(f32[8,128]{1,0:T(8,128)S(1)} %get-tuple-element.32), channel_id=1, source_target_pairs={{0,4},{4,0},{8,12},{12,8},{16,20},{20,16},{24,28},{28,24},{1,5},{5... | collective-permute-start | bytes 12296 | tf_op jit(solution)/shard_map/ppermute | solution.py:469
  29.4 1.6 %collective-permute-done.6 = f32[8,128]{1,0:T(8,128)S(1)} collective-permute-done((f32[8,128]{1,0:T(8,128)S(1)}, f32[8,128]{1,0:T(8,128)S(1)}, u32[]{:S(2)}, u32[]{:S(2)}) %collective-permute-start.6) | collective-permute-done | bytes 4128 | tf_op jit(solution)/shard_map/ppermute | solution.py:469
  31.0 0.3 collective-permute-start.14
  31.3 1.7 %collective-permute-start.15 = (f32[2,8,128]{2,1,0:T(8,128)S(1)}, f32[2,8,128]{2,1,0:T(8,128)S(1)}, u32[]{:S(2)}, u32[]{:S(2)}) collective-permute-start(f32[2,8,128]{2,1,0:T(8,128)S(1)} %pad_maximum_fusion.refs_0_), channel_id=1, source_target_pairs={{0,16},{4,20},{8,24},{12,28},{16,0},{20,4},{24,8},{28,12},{1,17},{... | collective-permute-start | bytes 24584 | tf_op jit(solution)/shard_map/ppermute | solution.py:466
  33.0 1.5 %collective-permute-start.16 = (f32[2,8,128]{2,1,0:T(8,128)S(1)}, f32[2,8,128]{2,1,0:T(8,128)S(1)}, u32[]{:S(2)}, u32[]{:S(2)}) collective-permute-start(f32[2,8,128]{2,1,0:T(8,128)S(1)} %pad_maximum_fusion.refs_0_), channel_id=1, source_target_pairs={{0,24},{4,28},{8,16},{12,20},{16,8},{20,12},{24,0},{28,4},{1,25},{... | collective-permute-start | bytes 24584 | tf_op jit(solution)/shard_map/ppermute | solution.py:466
  34.5 0.0 collective-permute-done.17.other_ref
  34.5 1.8 %shard_map.91 = (f32[225,128]{1,0:T(8,128)S(1)}, bf16[225,128]{1,0:T(8,128)(2,1)S(1)}, bf16[225,128]{1,0:T(8,128)(2,1)S(1)}, bf16[225,128]{1,0:T(8,128)(2,1)S(1)}, bf16[4,320,128]{2,1,0:T(8,128)(2,1)S(1)}) custom-call(bf16[16,160,128]{2,1,0:T(8,128)(2,1)S(1)} %shard_map.89.own_ref, bf16[16,160,128]{2,1,0:T(8,128)(2,1)S(1)} %collective-permute-done.17.other_ref, ...), custom_call_target="tpu_custom_call" | custom-call | flops 943718400 | tf_op jit(solution)/shard_map/pallas_call | solution.py:438
  36.3 3.7 %collective-permute-start.18 = (bf16[225,128]{1,0:T(8,128)(2,1)S(1)}, bf16[225,128]{1,0:T(8,128)(2,1)S(1)}, u32[]{:S(2)}, u32[]{:S(2)}) collective-permute-start(bf16[225,128]{1,0:T(8,128)(2,1)S(1)} %get-tuple-element.56), channel_id=1, source_target_pairs={{0,3},{1,2},{2,1},{3,0},{4,7},{5,6},{6,5},{7,4},{8,11},{9,10},{10,... | collective-permute-start | bytes 172808 | tf_op jit(solution)/shard_map/ppermute | solution.py:559
  39.9 0.0 collective-permute-start.19
  40.0 0.0 collective-permute-done.14.refs_1_
  40.0 0.8 %collective-permute-start.20 = (bf16[225,128]{1,0:T(8,128)(2,1)S(1)}, bf16[225,128]{1,0:T(8,128)(2,1)S(1)}, u32[]{:S(2)}, u32[]{:S(2)}) collective-permute-start(bf16[225,128]{1,0:T(8,128)(2,1)S(1)} %get-tuple-element.58), channel_id=1, source_target_pairs={{0,1},{1,0},{2,3},{3,2},{4,5},{5,4},{6,7},{7,6},{8,9},{9,8},{10,11... | collective-permute-start | bytes 172808 | tf_op jit(solution)/shard_map/ppermute | solution.py:559
  40.7 0.0 collective-permute-done.15.refs_2_
  40.7 0.0 collective-permute-done.16.refs_3_
  40.7 1.5 %shard_map.90 = bf16[2,320,128]{2,1,0:T(8,128)(2,1)} custom-call(f32[2,8,128]{2,1,0:T(8,128)S(1)} %pad_maximum_fusion.refs_0_, f32[2,8,128]{2,1,0:T(8,128)S(1)} %collective-permute-done.14.refs_1_, f32[2,8,128]{2,1,0:T(8,128)S(1)} %collective-permute-done.15.refs_2_, f32[2,8,128]{2,1,0:T(8,128)S(1)} %collective-permute-done.16.refs_3_, ...), custom_call_target="tpu_custom_call" | custom-call | flops 117964800 | tf_op jit(solution)/shard_map/pallas_call | solution.py:438
  42.2 1.7 %shard_map.92 = bf16[2,320,128]{2,1,0:T(8,128)(2,1)} custom-call(bf16[4,320,128]{2,1,0:T(8,128)(2,1)S(1)} %get-tuple-element.54.gz_ref, bf16[3,320,960]{2,1,0:T(8,128)(2,1)S(1)} %shard_map.85.w_ref.refs_8_), custom_call_target="tpu_custom_call" | custom-call | flops 471859200 | tf_op jit(solution)/shard_map/pallas_call | solution.py:438
  43.9 0.0 collective-permute-done.18
  44.0 1.1 %collective-permute-done.19 = bf16[225,128]{1,0:T(8,128)(2,1)S(1)} collective-permute-done((bf16[225,128]{1,0:T(8,128)(2,1)S(1)}, bf16[225,128]{1,0:T(8,128)(2,1)S(1)}, u32[]{:S(2)}, u32[]{:S(2)}) %collective-permute-start.19) | collective-permute-done | bytes 57632 | tf_op jit(solution)/shard_map/ppermute | solution.py:559
  45.1 0.0 collective-permute-done.20
  45.1 0.7 %add_bitcast_fusion = f32[28800]{0:T(1024)} fusion(bf16[225,128]{1,0:T(8,128)(2,1)S(1)} %collective-permute-done.20, bf16[225,128]{1,0:T(8,128)(2,1)S(1)} %collective-permute-done.19, f32[225,128]{1,0:T(8,128)S(1)} %get-tuple-element.55, bf16[225,128]{1,0:T(8,128)(2,1)S(1)} %collective-permute-done.18), kind=kLoop, calls=%fused_computation | loop fusion | flops 172800 | bytes 403200 | tf_op jit(solution)/shard_map/reshape | solution.py:575
  (3 shorter events, 0.0 us)
Async XLA Ops:
  0.6 8.3 %collective-permute-start.2 = (bf16[2,320,128]{2,1,0:T(8,128)(2,1)}, bf16[2,320,128]{2,1,0:T(8,128)(2,1)S(1)}, u32[]{:S(2)}, u32[]{:S(2)}) collective-permute-start(bf16[2,320,128]{2,1,0:T(8,128)(2,1)} %bitcast.15), channel_id=1, source_target_pairs={{0,8},{4,12},{8,0},{12,4},{16,24},{20,28},{24,16},{28,20},{1,9},{5... | collective-permute-start | bytes 491528 | tf_op jit(solution)/shard_map/ppermute | solution.py:466
  3.7 9.4 %collective-permute-start.3 = (bf16[2,320,128]{2,1,0:T(8,128)(2,1)}, bf16[2,320,128]{2,1,0:T(8,128)(2,1)S(1)}, u32[]{:S(2)}, u32[]{:S(2)}) collective-permute-start(bf16[2,320,128]{2,1,0:T(8,128)(2,1)} %bitcast.16), channel_id=1, source_target_pairs={{0,16},{4,20},{8,24},{12,28},{16,0},{20,4},{24,8},{28,12},{1,17},{... | collective-permute-start | bytes 491528 | tf_op jit(solution)/shard_map/ppermute | solution.py:466
  5.2 7.9 %collective-permute-start.4 = (bf16[2,320,128]{2,1,0:T(8,128)(2,1)}, bf16[2,320,128]{2,1,0:T(8,128)(2,1)S(1)}, u32[]{:S(2)}, u32[]{:S(2)}) collective-permute-start(bf16[2,320,128]{2,1,0:T(8,128)(2,1)} %bitcast.17), channel_id=1, source_target_pairs={{0,24},{4,28},{8,16},{12,20},{16,8},{20,12},{24,0},{28,4},{1,25},{... | collective-permute-start | bytes 491528 | tf_op jit(solution)/shard_map/ppermute | solution.py:466
  5.2 2.1 %collective-permute-start.5 = (bf16[2,320,128]{2,1,0:T(8,128)(2,1)}, bf16[2,320,128]{2,1,0:T(8,128)(2,1)S(1)}, u32[]{:S(2)}, u32[]{:S(2)}) collective-permute-start(bf16[2,320,128]{2,1,0:T(8,128)(2,1)} %bitcast.13), channel_id=1, source_target_pairs={{0,4},{4,0},{8,12},{12,8},{16,20},{20,16},{24,28},{28,24},{1,5},{5... | collective-permute-start | bytes 491528 | tf_op jit(solution)/shard_map/ppermute | solution.py:469
  5.2 1.6 %copy-start = (bf16[3,3,320,320]{3,2,1,0:T(8,128)(2,1)S(1)}, bf16[3,3,320,320]{3,2,1,0:T(8,128)(2,1)}, u32[]{:S(2)}) copy-start(bf16[3,3,320,320]{3,2,1,0:T(8,128)(2,1)} %w_ref.1) | copy-start | bytes 5529604
  5.2 9.2 %collective-permute-start.1 = (bf16[2,320,128]{2,1,0:T(8,128)(2,1)}, bf16[2,320,128]{2,1,0:T(8,128)(2,1)S(1)}, u32[]{:S(2)}, u32[]{:S(2)}) collective-permute-start(bf16[2,320,128]{2,1,0:T(8,128)(2,1)} %bitcast.9), channel_id=1, source_target_pairs={{0,4},{4,0},{8,12},{12,8},{16,20},{20,16},{24,28},{28,24},{1,5},{5... | collective-permute-start | bytes 491528 | tf_op jit(solution)/shard_map/ppermute | solution.py:469
  6.8 1.2 %copy-start.2 = (bf16[1,2,320,128]{3,2,1,0:T(8,128)(2,1)S(1)}, bf16[1,2,320,128]{3,2,1,0:T(8,128)(2,1)}, u32[]{:S(2)}) copy-start(bf16[1,2,320,128]{3,2,1,0:T(8,128)(2,1)} %param.8) | copy-start | bytes 491524
  7.2 5.8 %copy-start.4 = (f32[320]{0:T(512)S(1)}, f32[320]{0:T(512)}, u32[]{:S(2)}) copy-start(f32[320]{0:T(512)} %param.10) | copy-start | bytes 3844
  7.2 5.9 %copy-start.5 = (f32[320]{0:T(512)S(1)}, f32[320]{0:T(512)}, u32[]{:S(2)}) copy-start(f32[320]{0:T(512)} %param.11) | copy-start | bytes 3844
  7.2 6.0 %copy-start.3 = (bf16[1,2,320,128]{3,2,1,0:T(8,128)(2,1)S(1)}, bf16[1,2,320,128]{3,2,1,0:T(8,128)(2,1)}, u32[]{:S(2)}) copy-start(bf16[1,2,320,128]{3,2,1,0:T(8,128)(2,1)} %param.7) | copy-start | bytes 491524
  7.3 9.5 %copy-start.1 = (bf16[1,2,320,128]{3,2,1,0:T(8,128)(2,1)S(1)}, bf16[1,2,320,128]{3,2,1,0:T(8,128)(2,1)}, u32[]{:S(2)}) copy-start(bf16[1,2,320,128]{3,2,1,0:T(8,128)(2,1)} %param.6) | copy-start | bytes 491524
  7.3 6.7 %collective-permute-start = (bf16[320,128]{1,0:T(8,128)(2,1)S(1)}, bf16[320,128]{1,0:T(8,128)(2,1)S(1)}, u32[]{:S(2)}, u32[]{:S(2)}) collective-permute-start(bf16[320,128]{1,0:T(8,128)(2,1)S(1)} %edge.1), channel_id=1, source_target_pairs={{4,8},{12,16},{20,24},{8,4},{16,12},{24,20},{5,9},{13,17},{21,25},... | collective-permute-start | bytes 245768 | tf_op jit(solution)/shard_map/ppermute | solution.py:484
  13.3 4.7 %collective-permute-start.10 = (bf16[2,320,128]{2,1,0:T(8,128)(2,1)S(1)}, bf16[2,320,128]{2,1,0:T(8,128)(2,1)S(1)}, u32[]{:S(2)}, u32[]{:S(2)}) collective-permute-start(bf16[2,320,128]{2,1,0:T(8,128)(2,1)S(1)} %bitcast.18), channel_id=1, source_target_pairs={{0,4},{4,0},{8,12},{12,8},{16,20},{20,16},{24,28},{28,24},{1,5},{5... | collective-permute-start | bytes 491528 | tf_op jit(solution)/shard_map/ppermute | solution.py:469
  13.4 4.7 %collective-permute-start.11 = (bf16[2,320,128]{2,1,0:T(8,128)(2,1)S(1)}, bf16[2,320,128]{2,1,0:T(8,128)(2,1)S(1)}, u32[]{:S(2)}, u32[]{:S(2)}) collective-permute-start(bf16[2,320,128]{2,1,0:T(8,128)(2,1)S(1)} %collective-permute-done.2.refs_2_), channel_id=1, source_target_pairs={{0,4},{4,0},{8,12},{12,8},{16,20},{20,16},{24,28},{28,24},{1,5},{5... | collective-permute-start | bytes 491528 | tf_op jit(solution)/shard_map/ppermute | solution.py:469
  13.9 5.6 %collective-permute-start.12 = (bf16[2,320,128]{2,1,0:T(8,128)(2,1)S(1)}, bf16[2,320,128]{2,1,0:T(8,128)(2,1)S(1)}, u32[]{:S(2)}, u32[]{:S(2)}) collective-permute-start(bf16[2,320,128]{2,1,0:T(8,128)(2,1)S(1)} %collective-permute-done.3.refs_4_), channel_id=1, source_target_pairs={{0,4},{4,0},{8,12},{12,8},{16,20},{20,16},{24,28},{28,24},{1,5},{5... | collective-permute-start | bytes 491528 | tf_op jit(solution)/shard_map/ppermute | solution.py:469
  13.9 5.5 %collective-permute-start.13 = (bf16[2,320,128]{2,1,0:T(8,128)(2,1)S(1)}, bf16[2,320,128]{2,1,0:T(8,128)(2,1)S(1)}, u32[]{:S(2)}, u32[]{:S(2)}) collective-permute-start(bf16[2,320,128]{2,1,0:T(8,128)(2,1)S(1)} %collective-permute-done.4.refs_6_), channel_id=1, source_target_pairs={{0,4},{4,0},{8,12},{12,8},{16,20},{20,16},{24,28},{28,24},{1,5},{5... | collective-permute-start | bytes 491528 | tf_op jit(solution)/shard_map/ppermute | solution.py:469
  14.4 9.1 %collective-permute-start.7 = (bf16[2,2,160,128]{3,2,1,0:T(8,128)(2,1)S(1)}, bf16[2,2,160,128]{3,2,1,0:T(8,128)(2,1)S(1)}, u32[]{:S(2)}, u32[]{:S(2)}) collective-permute-start(bf16[2,2,160,128]{3,2,1,0:T(8,128)(2,1)S(1)} %shard_map.86.refs_0_), channel_id=1, source_target_pairs={{0,8},{4,12},{8,0},{12,4},{16,24},{20,28},{24,16},{28,20},{1,9},{5... | collective-permute-start | bytes 491528 | tf_op jit(solution)/shard_map/ppermute | solution.py:466
  17.9 9.4 %collective-permute-start.8 = (bf16[2,2,160,128]{3,2,1,0:T(8,128)(2,1)S(1)}, bf16[2,2,160,128]{3,2,1,0:T(8,128)(2,1)S(1)}, u32[]{:S(2)}, u32[]{:S(2)}) collective-permute-start(bf16[2,2,160,128]{3,2,1,0:T(8,128)(2,1)S(1)} %shard_map.86.refs_0_), channel_id=1, source_target_pairs={{0,16},{4,20},{8,24},{12,28},{16,0},{20,4},{24,8},{28,12},{1,17},{... | collective-permute-start | bytes 491528 | tf_op jit(solution)/shard_map/ppermute | solution.py:466
  18.1 9.3 %collective-permute-start.9 = (bf16[2,2,160,128]{3,2,1,0:T(8,128)(2,1)S(1)}, bf16[2,2,160,128]{3,2,1,0:T(8,128)(2,1)S(1)}, u32[]{:S(2)}, u32[]{:S(2)}) collective-permute-start(bf16[2,2,160,128]{3,2,1,0:T(8,128)(2,1)S(1)} %shard_map.86.refs_0_), channel_id=1, source_target_pairs={{0,24},{4,28},{8,16},{12,20},{16,8},{20,12},{24,0},{28,4},{1,25},{... | collective-permute-start | bytes 491528 | tf_op jit(solution)/shard_map/ppermute | solution.py:466
  28.9 5.7 %collective-permute-start.17 = (bf16[16,160,128]{2,1,0:T(8,128)(2,1)S(1)}, bf16[16,160,128]{2,1,0:T(8,128)(2,1)S(1)}, u32[]{:S(2)}, u32[]{:S(2)}) collective-permute-start(bf16[16,160,128]{2,1,0:T(8,128)(2,1)S(1)} %shard_map.89.own_ref), channel_id=1, source_target_pairs={{0,4},{4,0},{8,12},{12,8},{16,20},{20,16},{24,28},{28,24},{1,5},{5... | collective-permute-start | bytes 1966088 | tf_op jit(solution)/shard_map/ppermute | solution.py:469
  28.9 2.1 %collective-permute-start.6 = (f32[8,128]{1,0:T(8,128)S(1)}, f32[8,128]{1,0:T(8,128)S(1)}, u32[]{:S(2)}, u32[]{:S(2)}) collective-permute-start(f32[8,128]{1,0:T(8,128)S(1)} %get-tuple-element.32), channel_id=1, source_target_pairs={{0,4},{4,0},{8,12},{12,8},{16,20},{20,16},{24,28},{28,24},{1,5},{5... | collective-permute-start | bytes 12296 | tf_op jit(solution)/shard_map/ppermute | solution.py:469
  31.0 8.9 %collective-permute-start.14 = (f32[2,8,128]{2,1,0:T(8,128)S(1)}, f32[2,8,128]{2,1,0:T(8,128)S(1)}, u32[]{:S(2)}, u32[]{:S(2)}) collective-permute-start(f32[2,8,128]{2,1,0:T(8,128)S(1)} %pad_maximum_fusion.refs_0_), channel_id=1, source_target_pairs={{0,8},{4,12},{8,0},{12,4},{16,24},{20,28},{24,16},{28,20},{1,9},{5... | collective-permute-start | bytes 24584 | tf_op jit(solution)/shard_map/ppermute | solution.py:466
  31.3 9.4 %collective-permute-start.15 = (f32[2,8,128]{2,1,0:T(8,128)S(1)}, f32[2,8,128]{2,1,0:T(8,128)S(1)}, u32[]{:S(2)}, u32[]{:S(2)}) collective-permute-start(f32[2,8,128]{2,1,0:T(8,128)S(1)} %pad_maximum_fusion.refs_0_), channel_id=1, source_target_pairs={{0,16},{4,20},{8,24},{12,28},{16,0},{20,4},{24,8},{28,12},{1,17},{... | collective-permute-start | bytes 24584 | tf_op jit(solution)/shard_map/ppermute | solution.py:466
  33.0 7.7 %collective-permute-start.16 = (f32[2,8,128]{2,1,0:T(8,128)S(1)}, f32[2,8,128]{2,1,0:T(8,128)S(1)}, u32[]{:S(2)}, u32[]{:S(2)}) collective-permute-start(f32[2,8,128]{2,1,0:T(8,128)S(1)} %pad_maximum_fusion.refs_0_), channel_id=1, source_target_pairs={{0,24},{4,28},{8,16},{12,20},{16,8},{20,12},{24,0},{28,4},{1,25},{... | collective-permute-start | bytes 24584 | tf_op jit(solution)/shard_map/ppermute | solution.py:466
  36.3 7.7 %collective-permute-start.18 = (bf16[225,128]{1,0:T(8,128)(2,1)S(1)}, bf16[225,128]{1,0:T(8,128)(2,1)S(1)}, u32[]{:S(2)}, u32[]{:S(2)}) collective-permute-start(bf16[225,128]{1,0:T(8,128)(2,1)S(1)} %get-tuple-element.56), channel_id=1, source_target_pairs={{0,3},{1,2},{2,1},{3,0},{4,7},{5,6},{6,5},{7,4},{8,11},{9,10},{10,... | collective-permute-start | bytes 172808 | tf_op jit(solution)/shard_map/ppermute | solution.py:559
  39.9 5.1 %collective-permute-start.19 = (bf16[225,128]{1,0:T(8,128)(2,1)S(1)}, bf16[225,128]{1,0:T(8,128)(2,1)S(1)}, u32[]{:S(2)}, u32[]{:S(2)}) collective-permute-start(bf16[225,128]{1,0:T(8,128)(2,1)S(1)} %get-tuple-element.57), channel_id=1, source_target_pairs={{0,2},{1,3},{2,0},{3,1},{4,6},{5,7},{6,4},{7,5},{8,10},{9,11},{10,... | collective-permute-start | bytes 172808 | tf_op jit(solution)/shard_map/ppermute | solution.py:559
  40.0 5.1 %collective-permute-start.20 = (bf16[225,128]{1,0:T(8,128)(2,1)S(1)}, bf16[225,128]{1,0:T(8,128)(2,1)S(1)}, u32[]{:S(2)}, u32[]{:S(2)}) collective-permute-start(bf16[225,128]{1,0:T(8,128)(2,1)S(1)} %get-tuple-element.58), channel_id=1, source_target_pairs={{0,1},{1,0},{2,3},{3,2},{4,5},{5,4},{6,7},{7,6},{8,9},{9,8},{10,11... | collective-permute-start | bytes 172808 | tf_op jit(solution)/shard_map/ppermute | solution.py:559
